TPU v7x, 256 devices: a whole 4x4x8 slice. The times are simulated.
256 devices in a mesh: dom: 32 (over x, y, core), group: 8 (over z).
Axes of the slice: x: 4, y: 4, z: 8, core: 2. Of those that a mesh axis runs over, the one named last changes fastest.
Arguments:
- nodes: bfloat16 [256, 256, 128], P(('dom', 'group')), may hold values from -6 to 6
- edges: bfloat16 [256, 1536, 128], P(('dom', 'group')), may hold values from -6 to 6
- node_cot: bfloat16 [256, 256, 128], P(('dom', 'group')), may hold values from -6 to 6
- send_index: int32 [256, 4, 128], P(('dom', 'group')), may hold values from 0 to 255
- halo_count: int32 [256, 4], P(('dom', 'group')), may hold values from 0 to 128, as said below
- senders: int32 [256, 1536], P(('dom', 'group')), may hold values from 0 to 767, as said below
- receivers: int32 [256, 1536], P(('dom', 'group')), may hold values from 0 to 255, as said below
- edge_in_w: bfloat16 [2, 384, 128], replicated, may hold values from -0.3125 to 0.3125
- edge_out_w: bfloat16 [2, 128, 128], replicated, may hold values from -0.5 to 0.5
- node_in_w: bfloat16 [2, 256, 128], replicated, may hold values from -0.375 to 0.375
- node_out_w: bfloat16 [2, 128, 128], replicated, may hold values from -0.5 to 0.5
- biases: float32 [2, 4, 128], replicated, may hold values from -3 to 3
- gains: float32 [2, 2, 128], replicated, may hold values from 0.1 to 1.9
Outputs:
- nodes_out: bfloat16 [256, 256, 128], P(('dom', 'group'))
- node_grad: bfloat16 [256, 256, 128], P(('dom', 'group'))
- edge_grad: bfloat16 [256, 1536, 128], P(('dom', 'group'))
- edge_in_grad: float32 [2, 384, 128], replicated
- edge_out_grad: float32 [2, 128, 128], replicated
- node_in_grad: float32 [2, 256, 128], replicated
- node_out_grad: float32 [2, 128, 128], replicated
- bias_grad: float32 [2, 4, 128], replicated
- gain_grad: float32 [2, 2, 128], replicated
Inputs may be any that keep to these rules, and one draw needn't show every extreme that they name: `halo_count`: slot order: from the lower then the upper partition along dom, then along group; 0 exactly where that neighbour does not exist; every slot reaches 128 on some partition. `senders`: below 256: a node of the partition; 256 + s: the s-th live halo row of the table, s below the partition's total halo_count. `receivers`: never fall along a partition's edges; within each aligned block of 512 edges they span fewer than 128 nodes.
All inputs are finite; a program needn't handle non-finite values.
Results may differ from a plain program's by a relative error of at most 0.02.
Values may be sent and summed in bfloat16 or wider, within the bound.
No kernel may reach another device: no remote copies, remote signals or barrier semaphores. Data moves between devices by JAX's collectives and lax.ppermute only.
A program may use at most 64 MiB of HBM per device.

v0:
```python
import jax
import jax.numpy as jnp
from jax import lax
from jax.experimental import pallas as pl
from jax.experimental.pallas import tpu as pltpu
from jax.sharding import PartitionSpec as P

H = 128
BLOCK = 512
GRAD_ROWS = 1024
VMEM_LIMIT = 28 << 20
F32 = jnp.float32
BF16 = jnp.bfloat16


def mm(a, b):
    return lax.dot_general(a, b, (((1,), (0,)), ((), ())), preferred_element_type=F32)


def mm_nt(a, b):
    return lax.dot_general(a, b, (((1,), (1,)), ((), ())), preferred_element_type=F32)


def mm_tn(a, b):
    return lax.dot_general(a, b, (((0,), (0,)), ((), ())), preferred_element_type=F32)


def column(row):
    return jnp.transpose(jnp.broadcast_to(row, (8, row.shape[1])))[:, :1]


def hot(mask):
    return jnp.where(mask, 1.0, 0.0).astype(BF16)


def pick_rows(row, width):
    col = column(row)
    return hot(lax.broadcasted_iota(jnp.int32, (row.shape[1], width), 1) == col)


def spread_rows(row, width):
    return hot(lax.broadcasted_iota(jnp.int32, (width, row.shape[1]), 0) == row)


def slot_ids(ids, counts):
    out = ids
    end = 256
    for k in range(3):
        end = end + counts[k]
        out = out + jnp.where(ids >= end, 128 - counts[k], 0)
    return out


def silu_parts(pre):
    sig = 0.5 * jnp.tanh(0.5 * pre) + 0.5
    return pre * sig, sig * (1.0 + pre * (1.0 - sig))


def norm_parts(mapped):
    centre = mapped - jnp.mean(mapped, axis=-1, keepdims=True)
    spread = jnp.mean(centre * centre, axis=-1, keepdims=True)
    scale = lax.rsqrt(spread + 1e-05)
    return centre * scale, scale


def norm_back(cot, xhat, scale, gain):
    grad = cot * gain
    first = jnp.mean(grad, axis=-1, keepdims=True)
    second = jnp.mean(grad * xhat, axis=-1, keepdims=True)
    return scale * (grad - first - xhat * second)


def total(x):
    return jnp.sum(x, axis=0, keepdims=True)


def write_sends(send_ref, rows, outs):
    for k in range(4):
        picked = mm(pick_rows(send_ref[k : k + 1, :], 256), rows)
        outs[k][...] = picked.astype(BF16)


def add_returns(send_ref, rets):
    out = jnp.zeros((256, H), F32)
    for k in range(4):
        out = out + mm(spread_rows(send_ref[k : k + 1, :], 256), rets[k][...])
    return out


def sends_kernel(send_ref, x_ref, o0, o1, o2, o3):
    write_sends(send_ref, x_ref[...], (o0, o1, o2, o3))


def edge_forward(counts, snd_ref, rcv_ref, table, e_ref, w1, w2, b_ref, g_ref, joined, hidden, slope, xhat, scale, e_new, agg):
    agg[...] = jnp.zeros((256, H), F32)

    def step(i, carry):
        rows = pl.ds(pl.multiple_of(i * BLOCK, BLOCK), BLOCK)
        ids = slot_ids(snd_ref[i], counts)
        sent = mm(pick_rows(ids, 768), table[...]).astype(BF16)
        recv = mm(pick_rows(rcv_ref[i], 256), table[0:256, :]).astype(BF16)
        joined[rows, 0:128] = e_ref[rows, :]
        joined[rows, 128:256] = sent
        joined[rows, 256:384] = recv
        pre = mm(joined[rows, :], w1[...]) + b_ref[0:1, :]
        act, slo = silu_parts(pre)
        act = act.astype(BF16)
        hidden[rows, :] = act
        slope[rows, :] = slo
        xh, sc = norm_parts(mm(act, w2[...]) + b_ref[1:2, :])
        xhat[rows, :] = xh
        scale[rows, :] = sc
        new = (e_ref[rows, :].astype(F32) + xh * g_ref[0:1, :]).astype(BF16)
        if e_new is not None:
            e_new[rows, :] = new
        agg[...] += mm(spread_rows(rcv_ref[i], 256), new)
        return carry

    lax.fori_loop(0, e_ref.shape[0] // BLOCK, step, 0)


def node_forward(x, agg, wn1, wn2, b_ref, g_ref):
    joined = jnp.concatenate([x, agg.astype(BF16)], axis=1)
    act, slo = silu_parts(mm(joined, wn1[...]) + b_ref[2:3, :])
    act = act.astype(BF16)
    xh, sc = norm_parts(mm(act, wn2[...]) + b_ref[3:4, :])
    new = (x.astype(F32) + xh * g_ref[1:2, :]).astype(BF16)
    return new, (joined, act, slo, xh, sc)


def node_backward(cot, saved, wn1, wn2, g_ref, grads):
    joined, act, slo, xh, sc = saved
    cot = cot.astype(F32)
    back = norm_back(cot, xh, sc, g_ref[1:2, :])
    back_b = back.astype(BF16)
    dpre = mm_nt(back_b, wn2[...]).astype(BF16).astype(F32) * slo
    dpre_b = dpre.astype(BF16)
    djoined = mm_nt(dpre_b, wn1[...]).astype(BF16)
    grads[512:768, :] = mm_tn(joined, dpre_b).astype(BF16)
    grads[768:896, :] = mm_tn(act, back_b).astype(BF16)
    small = (total(dpre), total(back), total(cot * xh))
    return cot + djoined[:, 0:128].astype(F32), djoined[:, 128:256], small


def edge_backward(counts, snd_ref, rcv_ref, w1, w2, g_ref, joined, hidden, slope, xhat, scale, dagg, e_cot, e_grad, acc, acc1, acc2, sums, grads):
    acc[...] = jnp.zeros(acc.shape, F32)
    acc1[...] = jnp.zeros(acc1.shape, F32)
    acc2[...] = jnp.zeros(acc2.shape, F32)
    sums[...] = jnp.zeros(sums.shape, F32)

    def step(i, carry):
        rows = pl.ds(pl.multiple_of(i * BLOCK, BLOCK), BLOCK)
        cot = mm(pick_rows(rcv_ref[i], 256), dagg)
        if e_cot is not None:
            cot = (cot + e_cot[rows, :].astype(F32)).astype(BF16).astype(F32)
        xh = xhat[rows, :]
        back = norm_back(cot, xh, scale[rows, :], g_ref[0:1, :])
        back_b = back.astype(BF16)
        dpre = mm_nt(back_b, w2[...]).astype(BF16).astype(F32) * slope[rows, :]
        dpre_b = dpre.astype(BF16)
        djoined = mm_nt(dpre_b, w1[...]).astype(BF16)
        e_grad[rows, :] = (cot + djoined[:, 0:128].astype(F32)).astype(BF16)
        ids = slot_ids(snd_ref[i], counts)
        acc[...] += mm(spread_rows(ids, 768), djoined[:, 128:256])
        acc[0:256, :] += mm(spread_rows(rcv_ref[i], 256), djoined[:, 256:384])
        acc1[...] += mm_tn(dpre_b, joined[rows, :])
        acc2[...] += mm_tn(back_b, hidden[rows, :])
        sums[0:1, :] += total(dpre)
        sums[1:2, :] += total(back)
        sums[2:3, :] += total(cot * xh)
        return carry

    lax.fori_loop(0, joined.shape[0] // BLOCK, step, 0)
    for k in range(3):
        grads[128 * k : 128 * k + 128, :] = jnp.transpose(acc1[:, 128 * k : 128 * k + 128]).astype(BF16)
    grads[384:512, :] = jnp.transpose(acc2[...]).astype(BF16)


def write_small(grads, sums, small):
    tail = jnp.concatenate(
        [sums[0:2, :], small[0], small[1], sums[2:3, :], small[2], jnp.zeros((122, H), F32)], axis=0
    )
    grads[896:1024, :] = tail.astype(BF16)


def first_kernel(
    cnt, snd_ref, rcv_ref, send_ref, x_ref, r0, r1, r2, r3, e_ref, w1, w2, wn1, wn2, b_ref, g_ref,
    joined, hidden, slope, xhat, scale, e_new, agg_b, x_new, o0, o1, o2, o3, table, agg,
):
    counts = (cnt[0], cnt[1], cnt[2])
    table[0:256, :] = x_ref[...]
    for k, r in enumerate((r0, r1, r2, r3)):
        table[256 + 128 * k : 384 + 128 * k, :] = r[...]
    edge_forward(counts, snd_ref, rcv_ref, table, e_ref, w1, w2, b_ref, g_ref, joined, hidden, slope, xhat, scale, e_new, agg)
    new, saved = node_forward(x_ref[...], agg[...], wn1, wn2, b_ref, g_ref)
    agg_b[...] = agg[...].astype(BF16)
    x_new[...] = new
    write_sends(send_ref, new, (o0, o1, o2, o3))


def last_kernel(
    cnt, snd_ref, rcv_ref, x_ref, r0, r1, r2, r3, e_ref, w1, w2, wn1, wn2, b_ref, g_ref, cot_ref,
    x_new, e_grad, x_grad, c0, c1, c2, c3, grads,
    table, agg, joined, hidden, slope, xhat, scale, acc, acc1, acc2, sums,
):
    counts = (cnt[0], cnt[1], cnt[2])
    table[0:256, :] = x_ref[...]
    for k, r in enumerate((r0, r1, r2, r3)):
        table[256 + 128 * k : 384 + 128 * k, :] = r[...]
    edge_forward(counts, snd_ref, rcv_ref, table, e_ref, w1, w2, b_ref, g_ref, joined, hidden, slope, xhat, scale, None, agg)
    new, saved = node_forward(x_ref[...], agg[...], wn1, wn2, b_ref, g_ref)
    x_new[...] = new
    dx, dagg, small = node_backward(cot_ref[...], saved, wn1, wn2, g_ref, grads)
    edge_backward(counts, snd_ref, rcv_ref, w1, w2, g_ref, joined, hidden, slope, xhat, scale, dagg, None, e_grad, acc, acc1, acc2, sums, grads)
    write_small(grads, sums, small)
    x_grad[...] = dx + acc[0:256, :]
    for k, c in enumerate((c0, c1, c2, c3)):
        c[...] = acc[256 + 128 * k : 384 + 128 * k, :].astype(BF16)


def back_kernel(
    cnt, snd_ref, rcv_ref, send_ref, x_ref, agg_b, own_ref, t0, t1, t2, t3, joined, hidden, slope, xhat, scale, e_cot,
    w1, w2, wn1, wn2, b_ref, g_ref,
    e_grad, x_grad, c0, c1, c2, c3, grads, acc, acc1, acc2, sums,
):
    counts = (cnt[0], cnt[1], cnt[2])
    cot = (own_ref[...] + add_returns(send_ref, (t0, t1, t2, t3))).astype(BF16)
    new, saved = node_forward(x_ref[...], agg_b[...], wn1, wn2, b_ref, g_ref)
    dx, dagg, small = node_backward(cot, saved, wn1, wn2, g_ref, grads)
    edge_backward(counts, snd_ref, rcv_ref, w1, w2, g_ref, joined, hidden, slope, xhat, scale, dagg, e_cot, e_grad, acc, acc1, acc2, sums, grads)
    write_small(grads, sums, small)
    x_grad[...] = dx + acc[0:256, :]
    for k, c in enumerate((c0, c1, c2, c3)):
        c[...] = acc[256 + 128 * k : 384 + 128 * k, :].astype(BF16)


def finish_kernel(send_ref, own_ref, t0, t1, t2, t3, o_ref):
    o_ref[...] = (own_ref[...] + add_returns(send_ref, (t0, t1, t2, t3))).astype(BF16)


def shape(*dims, dtype=F32):
    return jax.ShapeDtypeStruct(dims, dtype)


def call(kernel, outs, scratch, args, name):
    smem = pl.BlockSpec(memory_space=pltpu.SMEM)
    vmem = pl.BlockSpec(memory_space=pltpu.VMEM)
    specs = [smem if a.ndim == 1 else vmem for a in args]
    return pl.pallas_call(
        kernel,
        out_shape=outs,
        in_specs=specs,
        out_specs=[vmem] * len(outs),
        scratch_shapes=[pltpu.VMEM(s.shape, s.dtype) for s in scratch],
        compiler_params=pltpu.CompilerParams(vmem_limit_bytes=VMEM_LIMIT),
        name=name,
    )(*args)


def steps_of(axis):
    size = lax.axis_size(axis)
    up = [(i, i + 1) for i in range(size - 1)]
    down = [(i + 1, i) for i in range(size - 1)]
    return up, down


def exchange(blocks, back):
    up_d, down_d = steps_of("dom")
    up_g, down_g = steps_of("group")
    plan = (("dom", up_d), ("dom", down_d), ("group", up_g), ("group", down_g))
    if back:
        plan = (plan[1], plan[0], plan[3], plan[2])
    return [lax.ppermute(b, axis, pairs) for b, (axis, pairs) in zip(blocks, plan)]


def copies(x, axis):
    many = jnp.broadcast_to(x[None], (lax.axis_size(axis), *x.shape))
    return lax.all_to_all(many, axis, split_axis=0, concat_axis=0, tiled=True)


def reduce_grads(packed):
    tiles = packed.reshape(lax.axis_size("dom"), -1, H)
    tiles = lax.all_to_all(tiles, "dom", split_axis=0, concat_axis=0, tiled=True)
    share = jnp.sum(tiles.astype(F32), axis=0).astype(BF16)
    share = jnp.sum(copies(share, "group").astype(F32), axis=0).astype(BF16)
    return copies(share, "dom").reshape(-1, H)


def shards(nodes, edges, node_cot, send_index, halo_count, senders, receivers, edge_in_w, edge_out_w, node_in_w, node_out_w, biases, gains):
    x0 = nodes[0]
    e0 = edges[0]
    send = send_index[0]
    counts = halo_count[0]
    n_edge = e0.shape[0]
    snd = senders[0].reshape(n_edge // BLOCK, 1, BLOCK)
    rcv = receivers[0].reshape(n_edge // BLOCK, 1, BLOCK)
    weights = [(edge_in_w[l], edge_out_w[l], node_in_w[l], node_out_w[l], biases[l], gains[l]) for l in range(2)]
    rows4 = [shape(H, H, dtype=BF16)] * 4
    residuals = [
        shape(n_edge, 3 * H, dtype=BF16),
        shape(n_edge, H, dtype=BF16),
        shape(n_edge, H),
        shape(n_edge, H),
        shape(n_edge, 1),
    ]
    accs = [shape(768, H), shape(H, 3 * H), shape(H, H), shape(8, H)]
    table = shape(768, H, dtype=BF16)

    sent = call(sends_kernel, rows4, [], (send, x0), "sends")
    got = exchange(sent, False)
    out = call(
        first_kernel,
        residuals + [shape(n_edge, H, dtype=BF16), shape(256, H, dtype=BF16), shape(256, H, dtype=BF16)] + rows4,
        [table, shape(256, H)],
        (counts, snd, rcv, send, x0, *got, e0, *weights[0]),
        "layer0",
    )
    saved, (e1, agg0, x1), sent = out[:5], out[5:8], out[8:]
    got = exchange(sent, False)
    out = call(
        last_kernel,
        [shape(256, H, dtype=BF16), shape(n_edge, H, dtype=BF16), shape(256, H)] + rows4 + [shape(GRAD_ROWS, H, dtype=BF16)],
        [table, shape(256, H)] + residuals + accs,
        (counts, snd, rcv, x1, *got, e1, *weights[1], node_cot[0]),
        "layer1",
    )
    nodes_out, e_cot, own = out[:3]
    grads1 = out[7]
    back = exchange(out[3:7], True)
    out = call(
        back_kernel,
        [shape(n_edge, H, dtype=BF16), shape(256, H)] + rows4 + [shape(GRAD_ROWS, H, dtype=BF16)],
        accs,
        (counts, snd, rcv, send, x0, agg0, own, *back, *saved, e_cot, *weights[0]),
        "back0",
    )
    edge_grad, own = out[:2]
    grads0 = out[6]
    back = exchange(out[2:6], True)
    (node_grad,) = call(finish_kernel, [shape(256, H, dtype=BF16)], [], (send, own, *back), "finish")

    scale = (lax.axis_size("dom") * lax.axis_size("group") * x0.shape[0]) ** (-0.5)
    whole = [reduce_grads(g).astype(F32) * scale for g in (grads0, grads1)]
    cuts = ((0, 384), (384, 512), (512, 768), (768, 896), (896, 900), (900, 902))
    grads = [jnp.stack([w[a:b] for w in whole]) for a, b in cuts]
    return (nodes_out[None], node_grad[None], edge_grad[None], *grads)


def solution(mesh):
    part = ("dom", "group")
    in_specs = (P(part),) * 7 + (P(),) * 6
    out_specs = (P(part),) * 3 + (P(),) * 6
    return jax.shard_map(shards, mesh=mesh, in_specs=in_specs, out_specs=out_specs, check_vma=False)
```

profile of v0, /device:TPU:1, one launch (start us, length us, event | category | flops | bytes accessed | tf_op | source)
XLA Modules:
  0.0 187.1 jit_solution(10381089363145427202)
XLA Ops:
  2.6 4.6 %collective-permute-start = (bf16[128,128]{1,0:T(8,128)(2,1)S(1)}, bf16[128,128]{1,0:T(8,128)(2,1)S(1)}, u32[]{:S(2)}, u32[]{:S(2)}) collective-permute-start(bf16[128,128]{1,0:T(8,128)(2,1)S(1)} %get-tuple-element.40), channel_id=1, source_target_pairs={{0,8},{8,16},{16,24},{24,32},{32,40},{40,48},{48,56},{56,64},{64,7... | collective-permute-start | bytes 98312 | tf_op jit(solution)/shard_map/ppermute | solution.py:273
  9.1 3.5 %collective-permute-start.2 = (bf16[128,128]{1,0:T(8,128)(2,1)S(1)}, bf16[128,128]{1,0:T(8,128)(2,1)S(1)}, u32[]{:S(2)}, u32[]{:S(2)}) collective-permute-start(bf16[128,128]{1,0:T(8,128)(2,1)S(1)} %get-tuple-element.42), channel_id=1, source_target_pairs={{0,1},{1,2},{2,3},{3,4},{4,5},{5,6},{6,7},{8,9},{9,10},{10,11},{11... | collective-permute-start | bytes 98312 | tf_op jit(solution)/shard_map/ppermute | solution.py:273
  20.9 6.2 %layer0.1 = (bf16[1536,384]{1,0:T(8,128)(2,1)S(1)}, bf16[1536,128]{1,0:T(8,128)(2,1)S(1)}, f32[1536,128]{1,0:T(8,128)S(1)}, f32[1536,128]{1,0:T(8,128)S(1)}, f32...) custom-call(s32[4]{0:T(128)S(1)} %bitcast.71, ...), custom_call_target="tpu_custom_call" | custom-call | tf_op jit(solution)/shard_map/layer0/pallas_call | solution.py:249
  28.0 4.2 %collective-permute-start.4 = (bf16[128,128]{1,0:T(8,128)(2,1)S(1)}, bf16[128,128]{1,0:T(8,128)(2,1)S(1)}, u32[]{:S(2)}, u32[]{:S(2)}) collective-permute-start(bf16[128,128]{1,0:T(8,128)(2,1)S(1)} %get-tuple-element.45), channel_id=1, source_target_pairs={{0,8},{8,16},{16,24},{24,32},{32,40},{40,48},{48,56},{56,64},{64,7... | collective-permute-start | bytes 98312 | tf_op jit(solution)/shard_map/ppermute | solution.py:273
  34.1 4.0 %collective-permute-start.6 = (bf16[128,128]{1,0:T(8,128)(2,1)S(1)}, bf16[128,128]{1,0:T(8,128)(2,1)S(1)}, u32[]{:S(2)}, u32[]{:S(2)}) collective-permute-start(bf16[128,128]{1,0:T(8,128)(2,1)S(1)} %get-tuple-element.47), channel_id=1, source_target_pairs={{0,1},{1,2},{2,3},{3,4},{4,5},{5,6},{6,7},{8,9},{9,10},{10,11},{11... | collective-permute-start | bytes 98312 | tf_op jit(solution)/shard_map/ppermute | solution.py:273
  39.4 4.2 %collective-permute-done.7.r3 = bf16[128,128]{1,0:T(8,128)(2,1)S(1)} collective-permute-done((bf16[128,128]{1,0:T(8,128)(2,1)S(1)}, bf16[128,128]{1,0:T(8,128)(2,1)S(1)}, u32[]{:S(2)}, u32[]{:S(2)}) %collective-permute-start.7) | collective-permute-done | bytes 32800 | tf_op jit(solution)/shard_map/ppermute | solution.py:273
  43.6 11.0 %layer1.1 = (bf16[256,128]{1,0:T(8,128)(2,1)}, bf16[1536,128]{1,0:T(8,128)(2,1)S(1)}, f32[256,128]{1,0:T(8,128)S(1)}, bf16[128,128]{1,0:T(8,128)(2,1)S(1)}, bf16...) custom-call(s32[4]{0:T(128)S(1)} %bitcast.72, ...), custom_call_target="tpu_custom_call" | custom-call | tf_op jit(solution)/shard_map/layer1/pallas_call | solution.py:249
  59.2 10.4 %all-to-all-start.3 = ((bf16[32,32,128]{2,1,0:T(8,128)(2,1)}), bf16[32,32,128]{2,1,0:T(8,128)(2,1)}, u32[]{:S(2)}, u32[]{:S(2)}) async-start(bf16[32,32,128]{2,1,0:T(8,128)(2,1)} %bitcast.58), calls=%async_computation.3 | async-start | bytes 524288 | tf_op jit(solution)/shard_map/all_to_all | solution.py:283
  69.6 2.2 %collective-permute-start.8 = (bf16[128,128]{1,0:T(8,128)(2,1)}, bf16[128,128]{1,0:T(8,128)(2,1)S(1)}, u32[]{:S(2)}, u32[]{:S(2)}) collective-permute-start(bf16[128,128]{1,0:T(8,128)(2,1)} %copy-done.34), channel_id=1, source_target_pairs={{8,0},{16,8},{24,16},{32,24},{40,32},{48,40},{56,48},{64,56},{72,6... | collective-permute-start | bytes 98312 | tf_op jit(solution)/shard_map/ppermute | solution.py:273
  71.8 3.3 %collective-permute-start.9 = (bf16[128,128]{1,0:T(8,128)(2,1)}, bf16[128,128]{1,0:T(8,128)(2,1)S(1)}, u32[]{:S(2)}, u32[]{:S(2)}) collective-permute-start(bf16[128,128]{1,0:T(8,128)(2,1)} %copy-done.33), channel_id=1, source_target_pairs={{0,8},{8,16},{16,24},{24,32},{32,40},{40,48},{48,56},{56,64},{64,7... | collective-permute-start | bytes 98312 | tf_op jit(solution)/shard_map/ppermute | solution.py:273
  76.5 5.5 %collective-permute-start.11 = (bf16[128,128]{1,0:T(8,128)(2,1)}, bf16[128,128]{1,0:T(8,128)(2,1)S(1)}, u32[]{:S(2)}, u32[]{:S(2)}) collective-permute-start(bf16[128,128]{1,0:T(8,128)(2,1)} %copy-done.31), channel_id=1, source_target_pairs={{0,1},{1,2},{2,3},{3,4},{4,5},{5,6},{6,7},{8,9},{9,10},{10,11},{11... | collective-permute-start | bytes 98312 | tf_op jit(solution)/shard_map/ppermute | solution.py:273
  86.3 6.2 %back0.1 = (bf16[1536,128]{1,0:T(8,128)(2,1)}, f32[256,128]{1,0:T(8,128)S(1)}, bf16[128,128]{1,0:T(8,128)(2,1)S(1)}, bf16[128,128]{1,0:T(8,128)(2,1)S(1)}, bf16[...) custom-call(s32[4]{0:T(128)S(1)} %bitcast.73, s32[3,1,512]{2,1,0:T(1,128)S(1)} %bitcast.63, ...), custom_call_target="tpu_custom_call" | custom-call | tf_op jit(solution)/shard_map/back0/pallas_call | solution.py:249
  96.3 9.1 %all-to-all-start = ((bf16[32,32,128]{2,1,0:T(8,128)(2,1)}), bf16[32,32,128]{2,1,0:T(8,128)(2,1)S(1)}, u32[]{:S(2)}, u32[]{:S(2)}) async-start(bf16[32,32,128]{2,1,0:T(8,128)(2,1)} %bitcast.59), calls=%async_computation | async-start | bytes 524288 | tf_op jit(solution)/shard_map/all_to_all | solution.py:283
  106.4 8.0 %all-to-all-done = bf16[32,32,128]{2,1,0:T(8,128)(2,1)S(1)} async-done(((bf16[32,32,128]{2,1,0:T(8,128)(2,1)}), bf16[32,32,128]{2,1,0:T(8,128)(2,1)S(1)}, u32[]{:S(2)}, u32[]{:S(2)}) %all-to-all-start) | async-done | bytes 262176 | tf_op jit(solution)/shard_map/all_to_all | solution.py:283
  115.0 11.0 %all-to-all-start.4 = ((bf16[8,32,128]{2,1,0:T(8,128)(2,1)}), bf16[8,32,128]{2,1,0:T(8,128)(2,1)S(1)}, u32[]{:S(2)}, u32[]{:S(2)}) async-start(bf16[8,32,128]{2,1,0:T(8,128)(2,1)} %broadcast_in_dim.38), calls=%async_computation.4 | async-start | bytes 131072 | tf_op jit(solution)/shard_map/all_to_all | solution.py:278
  126.0 7.1 %all-to-all-done.4 = bf16[8,32,128]{2,1,0:T(8,128)(2,1)S(1)} async-done(((bf16[8,32,128]{2,1,0:T(8,128)(2,1)}), bf16[8,32,128]{2,1,0:T(8,128)(2,1)S(1)}, u32[]{:S(2)}, u32[]{:S(2)}) %all-to-all-start.4) | async-done | bytes 65568 | tf_op jit(solution)/shard_map/all_to_all | solution.py:278
  133.8 3.4 %all-to-all-start.1 = ((bf16[8,32,128]{2,1,0:T(8,128)(2,1)}), bf16[8,32,128]{2,1,0:T(8,128)(2,1)S(1)}, u32[]{:S(2)}, u32[]{:S(2)}) async-start(bf16[8,32,128]{2,1,0:T(8,128)(2,1)} %broadcast_in_dim.17), calls=%async_computation.1 | async-start | bytes 131072 | tf_op jit(solution)/shard_map/all_to_all | solution.py:278
  137.2 7.2 %all-to-all-done.1 = bf16[8,32,128]{2,1,0:T(8,128)(2,1)S(1)} async-done(((bf16[8,32,128]{2,1,0:T(8,128)(2,1)}), bf16[8,32,128]{2,1,0:T(8,128)(2,1)S(1)}, u32[]{:S(2)}, u32[]{:S(2)}) %all-to-all-start.1) | async-done | bytes 65568 | tf_op jit(solution)/shard_map/all_to_all | solution.py:278
  145.1 6.3 %all-to-all-start.5 = ((bf16[32,32,128]{2,1,0:T(8,128)(2,1)}), bf16[32,32,128]{2,1,0:T(8,128)(2,1)S(1)}, u32[]{:S(2)}, u32[]{:S(2)}) async-start(bf16[32,32,128]{2,1,0:T(8,128)(2,1)} %broadcast_in_dim.39), calls=%async_computation.5 | async-start | bytes 524288 | tf_op jit(solution)/shard_map/all_to_all | solution.py:278
  151.4 2.3 %collective-permute-start.12 = (bf16[128,128]{1,0:T(8,128)(2,1)S(1)}, bf16[128,128]{1,0:T(8,128)(2,1)S(1)}, u32[]{:S(2)}, u32[]{:S(2)}) collective-permute-start(bf16[128,128]{1,0:T(8,128)(2,1)S(1)} %copy-done.30), channel_id=1, source_target_pairs={{8,0},{16,8},{24,16},{32,24},{40,32},{48,40},{56,48},{64,56},{72,6... | collective-permute-start | bytes 98312 | tf_op jit(solution)/shard_map/ppermute | solution.py:273
  153.7 3.3 %collective-permute-start.13 = (bf16[128,128]{1,0:T(8,128)(2,1)S(1)}, bf16[128,128]{1,0:T(8,128)(2,1)S(1)}, u32[]{:S(2)}, u32[]{:S(2)}) collective-permute-start(bf16[128,128]{1,0:T(8,128)(2,1)S(1)} %copy-done.28), channel_id=1, source_target_pairs={{0,8},{8,16},{16,24},{24,32},{32,40},{40,48},{48,56},{56,64},{64,7... | collective-permute-start | bytes 98312 | tf_op jit(solution)/shard_map/ppermute | solution.py:273
  158.3 4.0 %collective-permute-start.15 = (bf16[128,128]{1,0:T(8,128)(2,1)S(1)}, bf16[128,128]{1,0:T(8,128)(2,1)S(1)}, u32[]{:S(2)}, u32[]{:S(2)}) collective-permute-start(bf16[128,128]{1,0:T(8,128)(2,1)S(1)} %copy-done.24), channel_id=1, source_target_pairs={{0,1},{1,2},{2,3},{3,4},{4,5},{5,6},{6,7},{8,9},{9,10},{10,11},{11... | collective-permute-start | bytes 98312 | tf_op jit(solution)/shard_map/ppermute | solution.py:273
  165.0 9.0 %all-to-all-start.2 = ((bf16[32,32,128]{2,1,0:T(8,128)(2,1)}), bf16[32,32,128]{2,1,0:T(8,128)(2,1)S(1)}, u32[]{:S(2)}, u32[]{:S(2)}) async-start(bf16[32,32,128]{2,1,0:T(8,128)(2,1)} %broadcast_in_dim.18), calls=%async_computation.2 | async-start | bytes 524288 | tf_op jit(solution)/shard_map/all_to_all | solution.py:278
  174.1 8.8 %all-to-all-done.2 = bf16[32,32,128]{2,1,0:T(8,128)(2,1)S(1)} async-done(((bf16[32,32,128]{2,1,0:T(8,128)(2,1)}), bf16[32,32,128]{2,1,0:T(8,128)(2,1)S(1)}, u32[]{:S(2)}, u32[]{:S(2)}) %all-to-all-start.2) | async-done | bytes 262176 | tf_op jit(solution)/shard_map/all_to_all | solution.py:278
  (126 shorter events, 41.3 us)
Async XLA Ops:
  2.6 15.6 %collective-permute-start = (bf16[128,128]{1,0:T(8,128)(2,1)S(1)}, bf16[128,128]{1,0:T(8,128)(2,1)S(1)}, u32[]{:S(2)}, u32[]{:S(2)}) collective-permute-start(bf16[128,128]{1,0:T(8,128)(2,1)S(1)} %get-tuple-element.40), channel_id=1, source_target_pairs={{0,8},{8,16},{16,24},{24,32},{32,40},{40,48},{48,56},{56,64},{64,7... | collective-permute-start | bytes 98312 | tf_op jit(solution)/shard_map/ppermute | solution.py:273
  7.1 11.0 %collective-permute-start.1 = (bf16[128,128]{1,0:T(8,128)(2,1)S(1)}, bf16[128,128]{1,0:T(8,128)(2,1)S(1)}, u32[]{:S(2)}, u32[]{:S(2)}) collective-permute-start(bf16[128,128]{1,0:T(8,128)(2,1)S(1)} %get-tuple-element.41), channel_id=1, source_target_pairs={{8,0},{16,8},{24,16},{32,24},{40,32},{48,40},{56,48},{64,56},{72,6... | collective-permute-start | bytes 98312 | tf_op jit(solution)/shard_map/ppermute | solution.py:273
  9.1 9.0 %collective-permute-start.2 = (bf16[128,128]{1,0:T(8,128)(2,1)S(1)}, bf16[128,128]{1,0:T(8,128)(2,1)S(1)}, u32[]{:S(2)}, u32[]{:S(2)}) collective-permute-start(bf16[128,128]{1,0:T(8,128)(2,1)S(1)} %get-tuple-element.42), channel_id=1, source_target_pairs={{0,1},{1,2},{2,3},{3,4},{4,5},{5,6},{6,7},{8,9},{9,10},{10,11},{11... | collective-permute-start | bytes 98312 | tf_op jit(solution)/shard_map/ppermute | solution.py:273
  12.6 5.5 %collective-permute-start.3 = (bf16[128,128]{1,0:T(8,128)(2,1)S(1)}, bf16[128,128]{1,0:T(8,128)(2,1)S(1)}, u32[]{:S(2)}, u32[]{:S(2)}) collective-permute-start(bf16[128,128]{1,0:T(8,128)(2,1)S(1)} %get-tuple-element.43), channel_id=1, source_target_pairs={{1,0},{2,1},{3,2},{4,3},{5,4},{6,5},{7,6},{9,8},{10,9},{11,10},{12... | collective-permute-start | bytes 98312 | tf_op jit(solution)/shard_map/ppermute | solution.py:273
  16.5 66.8 %copy-start.15 = (s32[1,1536]{1,0:T(1,128)S(1)}, s32[1,1536]{1,0:T(1,128)}, u32[]{:S(2)}) copy-start(s32[1,1536]{1,0:T(1,128)} %param.18) | copy-start | bytes 18436
  28.0 11.4 %collective-permute-start.4 = (bf16[128,128]{1,0:T(8,128)(2,1)S(1)}, bf16[128,128]{1,0:T(8,128)(2,1)S(1)}, u32[]{:S(2)}, u32[]{:S(2)}) collective-permute-start(bf16[128,128]{1,0:T(8,128)(2,1)S(1)} %get-tuple-element.45), channel_id=1, source_target_pairs={{0,8},{8,16},{16,24},{24,32},{32,40},{40,48},{48,56},{56,64},{64,7... | collective-permute-start | bytes 98312 | tf_op jit(solution)/shard_map/ppermute | solution.py:273
  32.2 7.2 %collective-permute-start.5 = (bf16[128,128]{1,0:T(8,128)(2,1)S(1)}, bf16[128,128]{1,0:T(8,128)(2,1)S(1)}, u32[]{:S(2)}, u32[]{:S(2)}) collective-permute-start(bf16[128,128]{1,0:T(8,128)(2,1)S(1)} %get-tuple-element.46), channel_id=1, source_target_pairs={{8,0},{16,8},{24,16},{32,24},{40,32},{48,40},{56,48},{64,56},{72,6... | collective-permute-start | bytes 98312 | tf_op jit(solution)/shard_map/ppermute | solution.py:273
  34.1 5.3 %collective-permute-start.6 = (bf16[128,128]{1,0:T(8,128)(2,1)S(1)}, bf16[128,128]{1,0:T(8,128)(2,1)S(1)}, u32[]{:S(2)}, u32[]{:S(2)}) collective-permute-start(bf16[128,128]{1,0:T(8,128)(2,1)S(1)} %get-tuple-element.47), channel_id=1, source_target_pairs={{0,1},{1,2},{2,3},{3,4},{4,5},{5,6},{6,7},{8,9},{9,10},{10,11},{11... | collective-permute-start | bytes 98312 | tf_op jit(solution)/shard_map/ppermute | solution.py:273
  38.1 5.5 %collective-permute-start.7 = (bf16[128,128]{1,0:T(8,128)(2,1)S(1)}, bf16[128,128]{1,0:T(8,128)(2,1)S(1)}, u32[]{:S(2)}, u32[]{:S(2)}) collective-permute-start(bf16[128,128]{1,0:T(8,128)(2,1)S(1)} %get-tuple-element.48), channel_id=1, source_target_pairs={{1,0},{2,1},{3,2},{4,3},{5,4},{6,5},{7,6},{9,8},{10,9},{11,10},{12... | collective-permute-start | bytes 98312 | tf_op jit(solution)/shard_map/ppermute | solution.py:273
  59.2 37.1 %all-to-all-start.3 = ((bf16[32,32,128]{2,1,0:T(8,128)(2,1)}), bf16[32,32,128]{2,1,0:T(8,128)(2,1)}, u32[]{:S(2)}, u32[]{:S(2)}) async-start(bf16[32,32,128]{2,1,0:T(8,128)(2,1)} %bitcast.58), calls=%async_computation.3 | async-start | bytes 524288 | tf_op jit(solution)/shard_map/all_to_all | solution.py:283
  69.6 12.4 %collective-permute-start.8 = (bf16[128,128]{1,0:T(8,128)(2,1)}, bf16[128,128]{1,0:T(8,128)(2,1)S(1)}, u32[]{:S(2)}, u32[]{:S(2)}) collective-permute-start(bf16[128,128]{1,0:T(8,128)(2,1)} %copy-done.34), channel_id=1, source_target_pairs={{8,0},{16,8},{24,16},{32,24},{40,32},{48,40},{56,48},{64,56},{72,6... | collective-permute-start | bytes 98312 | tf_op jit(solution)/shard_map/ppermute | solution.py:273
  71.8 10.1 %collective-permute-start.9 = (bf16[128,128]{1,0:T(8,128)(2,1)}, bf16[128,128]{1,0:T(8,128)(2,1)S(1)}, u32[]{:S(2)}, u32[]{:S(2)}) collective-permute-start(bf16[128,128]{1,0:T(8,128)(2,1)} %copy-done.33), channel_id=1, source_target_pairs={{0,8},{8,16},{16,24},{24,32},{32,40},{40,48},{48,56},{56,64},{64,7... | collective-permute-start | bytes 98312 | tf_op jit(solution)/shard_map/ppermute | solution.py:273
  75.2 6.8 %collective-permute-start.10 = (bf16[128,128]{1,0:T(8,128)(2,1)}, bf16[128,128]{1,0:T(8,128)(2,1)S(1)}, u32[]{:S(2)}, u32[]{:S(2)}) collective-permute-start(bf16[128,128]{1,0:T(8,128)(2,1)} %copy-done.32), channel_id=1, source_target_pairs={{1,0},{2,1},{3,2},{4,3},{5,4},{6,5},{7,6},{9,8},{10,9},{11,10},{12... | collective-permute-start | bytes 98312 | tf_op jit(solution)/shard_map/ppermute | solution.py:273
  76.5 6.8 %collective-permute-start.11 = (bf16[128,128]{1,0:T(8,128)(2,1)}, bf16[128,128]{1,0:T(8,128)(2,1)S(1)}, u32[]{:S(2)}, u32[]{:S(2)}) collective-permute-start(bf16[128,128]{1,0:T(8,128)(2,1)} %copy-done.31), channel_id=1, source_target_pairs={{0,1},{1,2},{2,3},{3,4},{4,5},{5,6},{6,7},{8,9},{9,10},{10,11},{11... | collective-permute-start | bytes 98312 | tf_op jit(solution)/shard_map/ppermute | solution.py:273
  96.3 67.1 %copy-start.12 = (f32[256,128]{1,0:T(8,128)S(1)}, f32[256,128]{1,0:T(8,128)}, u32[]{:S(2)}) copy-start(f32[256,128]{1,0:T(8,128)} %copy-done.11) | copy-start | bytes 393220
  96.3 18.0 %all-to-all-start = ((bf16[32,32,128]{2,1,0:T(8,128)(2,1)}), bf16[32,32,128]{2,1,0:T(8,128)(2,1)S(1)}, u32[]{:S(2)}, u32[]{:S(2)}) async-start(bf16[32,32,128]{2,1,0:T(8,128)(2,1)} %bitcast.59), calls=%async_computation | async-start | bytes 524288 | tf_op jit(solution)/shard_map/all_to_all | solution.py:283
  115.0 18.1 %all-to-all-start.4 = ((bf16[8,32,128]{2,1,0:T(8,128)(2,1)}), bf16[8,32,128]{2,1,0:T(8,128)(2,1)S(1)}, u32[]{:S(2)}, u32[]{:S(2)}) async-start(bf16[8,32,128]{2,1,0:T(8,128)(2,1)} %broadcast_in_dim.38), calls=%async_computation.4 | async-start | bytes 131072 | tf_op jit(solution)/shard_map/all_to_all | solution.py:278
  133.8 10.6 %all-to-all-start.1 = ((bf16[8,32,128]{2,1,0:T(8,128)(2,1)}), bf16[8,32,128]{2,1,0:T(8,128)(2,1)S(1)}, u32[]{:S(2)}, u32[]{:S(2)}) async-start(bf16[8,32,128]{2,1,0:T(8,128)(2,1)} %broadcast_in_dim.17), calls=%async_computation.1 | async-start | bytes 131072 | tf_op jit(solution)/shard_map/all_to_all | solution.py:278
  145.1 19.1 %all-to-all-start.5 = ((bf16[32,32,128]{2,1,0:T(8,128)(2,1)}), bf16[32,32,128]{2,1,0:T(8,128)(2,1)S(1)}, u32[]{:S(2)}, u32[]{:S(2)}) async-start(bf16[32,32,128]{2,1,0:T(8,128)(2,1)} %broadcast_in_dim.39), calls=%async_computation.5 | async-start | bytes 524288 | tf_op jit(solution)/shard_map/all_to_all | solution.py:278
  151.4 10.9 %collective-permute-start.12 = (bf16[128,128]{1,0:T(8,128)(2,1)S(1)}, bf16[128,128]{1,0:T(8,128)(2,1)S(1)}, u32[]{:S(2)}, u32[]{:S(2)}) collective-permute-start(bf16[128,128]{1,0:T(8,128)(2,1)S(1)} %copy-done.30), channel_id=1, source_target_pairs={{8,0},{16,8},{24,16},{32,24},{40,32},{48,40},{56,48},{64,56},{72,6... | collective-permute-start | bytes 98312 | tf_op jit(solution)/shard_map/ppermute | solution.py:273
  153.7 8.6 %collective-permute-start.13 = (bf16[128,128]{1,0:T(8,128)(2,1)S(1)}, bf16[128,128]{1,0:T(8,128)(2,1)S(1)}, u32[]{:S(2)}, u32[]{:S(2)}) collective-permute-start(bf16[128,128]{1,0:T(8,128)(2,1)S(1)} %copy-done.28), channel_id=1, source_target_pairs={{0,8},{8,16},{16,24},{24,32},{32,40},{40,48},{48,56},{56,64},{64,7... | collective-permute-start | bytes 98312 | tf_op jit(solution)/shard_map/ppermute | solution.py:273
  157.0 5.3 %collective-permute-start.14 = (bf16[128,128]{1,0:T(8,128)(2,1)S(1)}, bf16[128,128]{1,0:T(8,128)(2,1)S(1)}, u32[]{:S(2)}, u32[]{:S(2)}) collective-permute-start(bf16[128,128]{1,0:T(8,128)(2,1)S(1)} %copy-done.26), channel_id=1, source_target_pairs={{1,0},{2,1},{3,2},{4,3},{5,4},{6,5},{7,6},{9,8},{10,9},{11,10},{12... | collective-permute-start | bytes 98312 | tf_op jit(solution)/shard_map/ppermute | solution.py:273
  158.3 5.1 %collective-permute-start.15 = (bf16[128,128]{1,0:T(8,128)(2,1)S(1)}, bf16[128,128]{1,0:T(8,128)(2,1)S(1)}, u32[]{:S(2)}, u32[]{:S(2)}) collective-permute-start(bf16[128,128]{1,0:T(8,128)(2,1)S(1)} %copy-done.24), channel_id=1, source_target_pairs={{0,1},{1,2},{2,3},{3,4},{4,5},{5,6},{6,7},{8,9},{9,10},{10,11},{11... | collective-permute-start | bytes 98312 | tf_op jit(solution)/shard_map/ppermute | solution.py:273
  165.0 17.9 %all-to-all-start.2 = ((bf16[32,32,128]{2,1,0:T(8,128)(2,1)}), bf16[32,32,128]{2,1,0:T(8,128)(2,1)S(1)}, u32[]{:S(2)}, u32[]{:S(2)}) async-start(bf16[32,32,128]{2,1,0:T(8,128)(2,1)} %broadcast_in_dim.18), calls=%async_computation.2 | async-start | bytes 524288 | tf_op jit(solution)/shard_map/all_to_all | solution.py:278
  (33 other events, 575.4 us)
where the time goes:
time: 189 us; the launch traced here: 187 us
  starting transfers between devices  95 us (50%)
  waiting for transfers between devices  37.7 us (20%)
  Pallas kernels  24.5 us (13%)
  local copies, waits for them, and re-layouts  23.5 us (12%)
  other arithmetic  5.19 us (3%)
    ppermute x16, starting transfers between devices, exchange(): lax.ppermute(b, axis, pairs)  45.9 us
    all_to_all x4, starting transfers between devices, copies(): return lax.all_to_all(many, axis, split_axis=0, concat_axis=0, tiled=True)  29.5 us
    pallas_call x5, Pallas kernels, call(): pl.pallas_call(kernel, out_shape=outs, in_specs=specs, out_specs=[vmem] *...  24.5 us
    all_to_all x4, waiting for transfers between devices, copies(): return lax.all_to_all(many, axis, split_axis=0, concat_axis=0, tiled=True)  23.1 us
    all_to_all x2, starting transfers between devices, reduce_grads(): lax.all_to_all(tiles, 'dom', split_axis=0, concat_axis=0, tiled=True)  19.5 us
    unnamed x70, local copies, waits for them, and re-layouts  16.6 us
    all_to_all x2, waiting for transfers between devices, reduce_grads(): lax.all_to_all(tiles, 'dom', split_axis=0, concat_axis=0, tiled=True)  7.96 us
    ppermute x16, waiting for transfers between devices, exchange(): lax.ppermute(b, axis, pairs)  6.57 us
  transfers between devices with their start and end apart: 22, of which 7 were waited for; matrix products, arithmetic and copies ran while one was open for 3% of the time, Pallas kernels for 4%

commit v1 on v0

v1 whole, which is shorter than its diff:
```python
from functools import partial

import jax
import jax.numpy as jnp
from jax import lax
from jax.experimental import pallas as pl
from jax.experimental.pallas import tpu as pltpu
from jax.sharding import PartitionSpec as P

H = 128
BLOCK = 512
GRAD_ROWS = 1024
VMEM_LIMIT = 28 << 20
CUTS = ((0, 384), (384, 512), (512, 768), (768, 896), (896, 900), (900, 902))
F32 = jnp.float32
BF16 = jnp.bfloat16


def mm(a, b):
    return lax.dot_general(a, b, (((1,), (0,)), ((), ())), preferred_element_type=F32)


def mm_nt(a, b):
    return lax.dot_general(a, b, (((1,), (1,)), ((), ())), preferred_element_type=F32)


def mm_tn(a, b):
    return lax.dot_general(a, b, (((0,), (0,)), ((), ())), preferred_element_type=F32)


def column(row):
    return jnp.transpose(jnp.broadcast_to(row, (8, row.shape[1])))[:, :1]


def hot(mask):
    return jnp.where(mask, 1.0, 0.0).astype(BF16)


def pick_rows(row, width):
    col = column(row)
    return hot(lax.broadcasted_iota(jnp.int32, (row.shape[1], width), 1) == col)


def spread_rows(row, width):
    return hot(lax.broadcasted_iota(jnp.int32, (width, row.shape[1]), 0) == row)


def slot_ids(ids, counts):
    out = ids
    end = 256
    for k in range(3):
        end = end + counts[k]
        out = out + jnp.where(ids >= end, 128 - counts[k], 0)
    return out


def silu_parts(pre):
    sig = 0.5 * jnp.tanh(0.5 * pre) + 0.5
    return pre * sig, sig * (1.0 + pre * (1.0 - sig))


def norm_parts(mapped):
    centre = mapped - jnp.mean(mapped, axis=-1, keepdims=True)
    spread = jnp.mean(centre * centre, axis=-1, keepdims=True)
    scale = lax.rsqrt(spread + 1e-05)
    return centre * scale, scale


def norm_back(cot, xhat, scale, gain):
    grad = cot * gain
    first = jnp.mean(grad, axis=-1, keepdims=True)
    second = jnp.mean(grad * xhat, axis=-1, keepdims=True)
    return scale * (grad - first - xhat * second)


def total(x):
    return jnp.sum(x, axis=0, keepdims=True)


def sides():
    p = lax.axis_index("dom") % 2
    g = lax.axis_index("group") % 2
    return (p, 1 - p), (1 - p, p), (2 + g, 3 - g), (3 - g, 2 + g)


def write_sends(send_ref, rows, outs):
    for (src, _), out in zip(sides(), outs):
        picked = mm(pick_rows(send_ref[pl.ds(src, 1), :], 256), rows)
        out[...] = picked.astype(BF16)


def add_returns(send_ref, rets):
    out = jnp.zeros((256, H), F32)
    for (src, _), ret in zip(sides(), rets):
        out = out + mm(spread_rows(send_ref[pl.ds(src, 1), :], 256), ret[...])
    return out


def slot_rows(slot):
    return pl.ds(pl.multiple_of(256 + 128 * slot, 128), 128)


def fill_table(table, x_ref, got):
    table[0:256, :] = x_ref[...]
    for (_, dst), r in zip(sides(), got):
        table[slot_rows(dst), :] = r[...]


def write_backs(acc, outs):
    for (_, dst), out in zip(sides(), outs):
        out[...] = acc[slot_rows(dst), :].astype(BF16)


def fetch(pairs, sems):
    copies = [pltpu.make_async_copy(src, dst, sems.at[i]) for i, (src, dst) in enumerate(pairs)]
    for c in copies:
        c.start()
    return copies


def sends_kernel(send_hbm, x_hbm, o0, o1, o2, o3, send_ref, x_ref, sems):
    for c in fetch(((send_hbm, send_ref), (x_hbm, x_ref)), sems):
        c.wait()
    write_sends(send_ref, x_ref[...], (o0, o1, o2, o3))


def load_kernel(cnt, token, *refs):
    sems = refs[-1]
    n = (len(refs) - 1) // 2
    copies = fetch(tuple(zip(refs[:n], refs[n:-1])), sems)
    for c in copies:
        c.wait()
    snd_ref = refs[n]
    snd_ref[...] = slot_ids(snd_ref[...], (cnt[0], cnt[1], cnt[2]))


def edge_forward(snd_ref, rcv_ref, table, e_ref, w1, w2, b_ref, g_ref, joined, hidden, slope, xhat, scale, e_new, agg):
    agg[...] = jnp.zeros((256, H), F32)

    def step(i, carry):
        rows = pl.ds(pl.multiple_of(i * BLOCK, BLOCK), BLOCK)
        ids = snd_ref[i]
        sent = mm(pick_rows(ids, 768), table[...]).astype(BF16)
        recv = mm(pick_rows(rcv_ref[i], 256), table[0:256, :]).astype(BF16)
        joined[rows, 0:128] = e_ref[rows, :]
        joined[rows, 128:256] = sent
        joined[rows, 256:384] = recv
        pre = mm(joined[rows, :], w1[...]) + b_ref[0:1, :]
        act, slo = silu_parts(pre)
        act = act.astype(BF16)
        hidden[rows, :] = act
        slope[rows, :] = slo
        xh, sc = norm_parts(mm(act, w2[...]) + b_ref[1:2, :])
        xhat[rows, :] = xh
        scale[rows, :] = sc
        new = (e_ref[rows, :].astype(F32) + xh * g_ref[0:1, :]).astype(BF16)
        if e_new is not None:
            e_new[rows, :] = new
        agg[...] += mm(spread_rows(rcv_ref[i], 256), new)
        return carry

    lax.fori_loop(0, e_ref.shape[0] // BLOCK, step, 0)


def node_forward(x, agg, wn1, wn2, b_ref, g_ref):
    joined = jnp.concatenate([x, agg.astype(BF16)], axis=1)
    act, slo = silu_parts(mm(joined, wn1[...]) + b_ref[2:3, :])
    act = act.astype(BF16)
    xh, sc = norm_parts(mm(act, wn2[...]) + b_ref[3:4, :])
    new = (x.astype(F32) + xh * g_ref[1:2, :]).astype(BF16)
    return new, (joined, act, slo, xh, sc)


def node_backward(cot, saved, wn1, wn2, g_ref, grads):
    joined, act, slo, xh, sc = saved
    cot = cot.astype(F32)
    back = norm_back(cot, xh, sc, g_ref[1:2, :])
    back_b = back.astype(BF16)
    dpre = mm_nt(back_b, wn2[...]).astype(BF16).astype(F32) * slo
    dpre_b = dpre.astype(BF16)
    djoined = mm_nt(dpre_b, wn1[...]).astype(BF16)
    grads[512:768, :] = mm_tn(joined, dpre_b).astype(BF16)
    grads[768:896, :] = mm_tn(act, back_b).astype(BF16)
    small = (total(dpre), total(back), total(cot * xh))
    return cot + djoined[:, 0:128].astype(F32), djoined[:, 128:256], small


def edge_backward(snd_ref, rcv_ref, w1, w2, g_ref, joined, hidden, slope, xhat, scale, dagg, e_cot, e_grad, acc, acc1, acc2, sums, grads):
    acc[...] = jnp.zeros(acc.shape, F32)
    acc1[...] = jnp.zeros(acc1.shape, F32)
    acc2[...] = jnp.zeros(acc2.shape, F32)
    sums[...] = jnp.zeros(sums.shape, F32)

    def step(i, carry):
        rows = pl.ds(pl.multiple_of(i * BLOCK, BLOCK), BLOCK)
        cot = mm(pick_rows(rcv_ref[i], 256), dagg)
        if e_cot is not None:
            cot = (cot + e_cot[rows, :].astype(F32)).astype(BF16).astype(F32)
        xh = xhat[rows, :]
        back = norm_back(cot, xh, scale[rows, :], g_ref[0:1, :])
        back_b = back.astype(BF16)
        dpre = mm_nt(back_b, w2[...]).astype(BF16).astype(F32) * slope[rows, :]
        dpre_b = dpre.astype(BF16)
        djoined = mm_nt(dpre_b, w1[...]).astype(BF16)
        e_grad[rows, :] = (cot + djoined[:, 0:128].astype(F32)).astype(BF16)
        ids = snd_ref[i]
        acc[...] += mm(spread_rows(ids, 768), djoined[:, 128:256])
        acc[0:256, :] += mm(spread_rows(rcv_ref[i], 256), djoined[:, 256:384])
        acc1[...] += mm_tn(dpre_b, joined[rows, :])
        acc2[...] += mm_tn(back_b, hidden[rows, :])
        sums[0:1, :] += total(dpre)
        sums[1:2, :] += total(back)
        sums[2:3, :] += total(cot * xh)
        return carry

    lax.fori_loop(0, joined.shape[0] // BLOCK, step, 0)
    for k in range(3):
        grads[128 * k : 128 * k + 128, :] = jnp.transpose(acc1[:, 128 * k : 128 * k + 128]).astype(BF16)
    grads[384:512, :] = jnp.transpose(acc2[...]).astype(BF16)


def write_small(grads, sums, small):
    tail = jnp.concatenate(
        [sums[0:2, :], small[0], small[1], sums[2:3, :], small[2], jnp.zeros((GRAD_ROWS - 902, H), F32)], axis=0
    )
    grads[896:GRAD_ROWS, :] = tail.astype(BF16)


def first_kernel(
    snd_ref, rcv_ref, send_ref, x_ref, r0, r1, r2, r3, e_ref, w1, w2, wn1, wn2, b_ref, g_ref,
    joined, hidden, slope, xhat, scale, e_new, agg_b, x_new, o0, o1, o2, o3, table, agg,
):
    w1, w2, wn1, wn2, b_ref, g_ref = (r.at[0] for r in (w1, w2, wn1, wn2, b_ref, g_ref))
    fill_table(table, x_ref, (r0, r1, r2, r3))
    edge_forward(snd_ref, rcv_ref, table, e_ref, w1, w2, b_ref, g_ref, joined, hidden, slope, xhat, scale, e_new, agg)
    new, saved = node_forward(x_ref[...], agg[...], wn1, wn2, b_ref, g_ref)
    agg_b[...] = agg[...].astype(BF16)
    x_new[...] = new
    write_sends(send_ref, new, (o0, o1, o2, o3))


def last_kernel(
    snd_ref, rcv_ref, x_ref, r0, r1, r2, r3, e_ref, w1, w2, wn1, wn2, b_ref, g_ref, cot_ref,
    x_new, e_grad, x_grad, c0, c1, c2, c3, grads,
    table, agg, joined, hidden, slope, xhat, scale, acc, acc1, acc2, sums,
):
    w1, w2, wn1, wn2, b_ref, g_ref = (r.at[1] for r in (w1, w2, wn1, wn2, b_ref, g_ref))
    fill_table(table, x_ref, (r0, r1, r2, r3))
    edge_forward(snd_ref, rcv_ref, table, e_ref, w1, w2, b_ref, g_ref, joined, hidden, slope, xhat, scale, None, agg)
    new, saved = node_forward(x_ref[...], agg[...], wn1, wn2, b_ref, g_ref)
    x_new[...] = new
    dx, dagg, small = node_backward(cot_ref[...], saved, wn1, wn2, g_ref, grads)
    edge_backward(snd_ref, rcv_ref, w1, w2, g_ref, joined, hidden, slope, xhat, scale, dagg, None, e_grad, acc, acc1, acc2, sums, grads)
    write_small(grads, sums, small)
    x_grad[...] = dx + acc[0:256, :]
    write_backs(acc, (c0, c1, c2, c3))


def back_kernel(
    snd_ref, rcv_ref, send_ref, x_ref, agg_b, own_ref, t0, t1, t2, t3, joined, hidden, slope, xhat, scale, e_cot, late,
    w1, w2, wn1, wn2, b_ref, g_ref,
    e_grad, x_grad, c0, c1, c2, c3, grads, acc, acc1, acc2, sums,
):
    w1, w2, wn1, wn2, b_ref, g_ref = (r.at[0] for r in (w1, w2, wn1, wn2, b_ref, g_ref))
    grads[GRAD_ROWS:, :] = late[...]
    cot = (own_ref[...] + add_returns(send_ref, (t0, t1, t2, t3))).astype(BF16)
    new, saved = node_forward(x_ref[...], agg_b[...], wn1, wn2, b_ref, g_ref)
    dx, dagg, small = node_backward(cot, saved, wn1, wn2, g_ref, grads)
    edge_backward(snd_ref, rcv_ref, w1, w2, g_ref, joined, hidden, slope, xhat, scale, dagg, e_cot, e_grad, acc, acc1, acc2, sums, grads)
    write_small(grads, sums, small)
    x_grad[...] = dx + acc[0:256, :]
    write_backs(acc, (c0, c1, c2, c3))


def finish_kernel(send_ref, own_ref, t0, t1, t2, t3, o_ref):
    o_ref[...] = (own_ref[...] + add_returns(send_ref, (t0, t1, t2, t3))).astype(BF16)


def shape(*dims, dtype=F32):
    return jax.ShapeDtypeStruct(dims, dtype)


SMEM = pltpu.SMEM
VMEM = pltpu.VMEM
HBM = pltpu.HBM


def call(kernel, outs, scratch, args, name, spaces=None, sems=0):
    spaces = spaces or [VMEM] * len(args)
    args = [pltpu.with_memory_space_constraint(a, m) if m is HBM else a for a, m in zip(args, spaces)]
    extra = [pltpu.SemaphoreType.DMA((sems,))] if sems else []
    return pl.pallas_call(
        kernel,
        out_shape=outs,
        in_specs=[pl.BlockSpec(memory_space=m) for m in spaces],
        out_specs=[pl.BlockSpec(memory_space=VMEM)] * len(outs),
        scratch_shapes=[VMEM(s.shape, s.dtype) for s in scratch] + extra,
        compiler_params=pltpu.CompilerParams(vmem_limit_bytes=VMEM_LIMIT),
        name=name,
    )(*args)


def swaps(axis, first):
    size = lax.axis_size(axis)
    return [p for i in range(first, size - 1, 2) for p in ((i, i + 1), (i + 1, i))]


def exchange(blocks):
    plan = (("dom", 0), ("dom", 1), ("group", 0), ("group", 1))
    return [lax.ppermute(b, axis, swaps(axis, first)) for b, (axis, first) in zip(blocks, plan)]


def fold_kernel(x_ref, o_ref):
    out = jnp.sum(x_ref[...].astype(F32), axis=0).astype(BF16)
    for k in range(o_ref.shape[0]):
        o_ref[k] = out


def unpack_kernel(scale, x_ref, *outs):
    for out, (a, b) in zip(outs, CUTS):
        for l in range(2):
            out[l] = x_ref[GRAD_ROWS * l + a : GRAD_ROWS * l + b, :].astype(F32) * scale


def swap_tiles(x, axis):
    return lax.all_to_all(x, axis, split_axis=0, concat_axis=0, tiled=True)


def reduce_grads(packed, scale):
    dom, group = lax.axis_size("dom"), lax.axis_size("group")
    rows = packed.shape[0] // dom
    tiles = swap_tiles(packed.reshape(dom, rows, H), "dom")
    (tiles,) = call(fold_kernel, [shape(group, rows, H, dtype=BF16)], [], (tiles,), "fold_dom")
    tiles = swap_tiles(tiles, "group")
    (tiles,) = call(fold_kernel, [shape(dom, rows, H, dtype=BF16)], [], (tiles,), "fold_group")
    whole = swap_tiles(tiles, "dom").reshape(dom * rows, H)
    return call(partial(unpack_kernel, scale), [shape(2, b - a, H) for a, b in CUTS], [], (whole,), "unpack")


def shards(nodes, edges, node_cot, send_index, halo_count, senders, receivers, edge_in_w, edge_out_w, node_in_w, node_out_w, biases, gains):
    x0 = nodes[0]
    e0 = edges[0]
    send = send_index[0]
    counts = halo_count[0]
    n_edge = e0.shape[0]
    snd = senders[0].reshape(n_edge // BLOCK, 1, BLOCK)
    rcv = receivers[0].reshape(n_edge // BLOCK, 1, BLOCK)
    weights = (edge_in_w, edge_out_w, node_in_w, node_out_w, biases, gains)
    rows4 = [shape(H, H, dtype=BF16)] * 4
    residuals = [
        shape(n_edge, 3 * H, dtype=BF16),
        shape(n_edge, H, dtype=BF16),
        shape(n_edge, H),
        shape(n_edge, H),
        shape(n_edge, 1),
    ]
    accs = [shape(768, H), shape(H, 3 * H), shape(H, H), shape(8, H)]
    table = shape(768, H, dtype=BF16)

    *sent, send, x0 = call(
        sends_kernel,
        rows4 + [shape(4, H, dtype=jnp.int32), shape(256, H, dtype=BF16)],
        [],
        (send, x0),
        "sends",
        [HBM, HBM],
        2,
    )
    raw = (snd, rcv, e0, node_cot[0], *weights)
    loaded = call(
        load_kernel,
        [shape(*a.shape, dtype=a.dtype) for a in raw],
        [],
        (counts, sent[0], *raw),
        "load",
        [SMEM, VMEM] + [HBM] * len(raw),
        len(raw),
    )
    snd, rcv, e0, cot, *weights = loaded
    got = exchange(sent)
    out = call(
        first_kernel,
        residuals + [shape(n_edge, H, dtype=BF16), shape(256, H, dtype=BF16), shape(256, H, dtype=BF16)] + rows4,
        [table, shape(256, H)],
        (snd, rcv, send, x0, *got, e0, *weights),
        "layer0",
    )
    saved, (e1, agg0, x1), sent = out[:5], out[5:8], out[8:]
    got = exchange(sent)
    out = call(
        last_kernel,
        [shape(256, H, dtype=BF16), shape(n_edge, H, dtype=BF16), shape(256, H)] + rows4 + [shape(GRAD_ROWS, H, dtype=BF16)],
        [table, shape(256, H)] + residuals + accs,
        (snd, rcv, x1, *got, e1, *weights, cot),
        "layer1",
    )
    nodes_out, e_cot, own = out[:3]
    grads1 = out[7]
    back = exchange(out[3:7])
    out = call(
        back_kernel,
        [shape(n_edge, H, dtype=BF16), shape(256, H)] + rows4 + [shape(2 * GRAD_ROWS, H, dtype=BF16)],
        accs,
        (snd, rcv, send, x0, agg0, own, *back, *saved, e_cot, grads1, *weights),
        "back0",
    )
    edge_grad, own = out[:2]
    packed = out[6]
    back = exchange(out[2:6])
    (node_grad,) = call(finish_kernel, [shape(256, H, dtype=BF16)], [], (send, own, *back), "finish")

    scale = (lax.axis_size("dom") * lax.axis_size("group") * x0.shape[0]) ** (-0.5)
    grads = reduce_grads(packed, scale)
    return (nodes_out[None], node_grad[None], edge_grad[None], *grads)


def solution(mesh):
    part = ("dom", "group")
    in_specs = (P(part),) * 7 + (P(),) * 6
    out_specs = (P(part),) * 3 + (P(),) * 6
    return jax.shard_map(shards, mesh=mesh, in_specs=in_specs, out_specs=out_specs, check_vma=False)
```

time: 189 us -> 112 us (0.59)
  starting transfers between devices: 95 us -> 35 us
  blocking collectives: 0 us -> 40 us
  waiting for transfers between devices: 37.7 us -> 7.32 us
  local copies, waits for them, and re-layouts: 23.5 us -> 0.65 us
  other arithmetic: 5.19 us -> 0 us
  Pallas kernels: 24.5 us -> 27.9 us
    all_to_all x6 -> x1, starting transfers between devices: 49.1 us -> 4.1 us  [swap_tiles(): return lax.all_to_all(x, axis, split_axis=0, concat_axis=0, tiled=True)]
    all_to_all x0 -> x2, blocking collectives: none -> 40 us  [swap_tiles(): return lax.all_to_all(x, axis, split_axis=0, concat_axis=0, tiled=True)]
    all_to_all x6 -> x1, waiting for transfers between devices: 31.1 us -> 3.85 us  [swap_tiles(): return lax.all_to_all(x, axis, split_axis=0, concat_axis=0, tiled=True)]
    unnamed x70 -> x2, local copies, waits for them, and re-layouts: 16.6 us -> 0.65 us
    ppermute x16, starting transfers between devices: 45.9 us -> 30.9 us  [exchange(): lax.ppermute(b, axis, swaps(axis, first))]
    squeeze x5 -> x0, local copies, waits for them, and re-layouts: 4.11 us -> none  [the longest x1 0.96 us: shards(): edge_in_w[l]]
    another operation x6 -> x0, other arithmetic: 4 us -> none  [shards(): grads = [jnp.stack([w[a:b] for w in whole]) for a, b in cuts]]
    pallas_call x5 -> x9, Pallas kernels: 24.5 us -> 27.9 us  [call(): pl.pallas_call(kernel, out_shape=outs, in_specs=[pl.BlockSpec(memory_spac...]
  transfers between devices with their start and end apart: 22 -> 17, of which waited for: 7 -> 4; matrix products, arithmetic and copies ran while one was open for 3% -> 0% of each run, Pallas kernels for 4% -> 2%
where the time goes in v1:
time: 112 us
  blocking collectives  40 us (36%)
  starting transfers between devices  35 us (31%)
  Pallas kernels  27.9 us (25%)
  waiting for transfers between devices  7.32 us (7%)
    all_to_all x2, blocking collectives, swap_tiles(): return lax.all_to_all(x, axis, split_axis=0, concat_axis=0, tiled=True)  40 us
    ppermute x16, starting transfers between devices, exchange(): lax.ppermute(b, axis, swaps(axis, first))  30.9 us
    pallas_call x9, Pallas kernels, call(): pl.pallas_call(kernel, out_shape=outs, in_specs=[pl.BlockSpec(memory_spac...  27.9 us
    all_to_all x1, starting transfers between devices, swap_tiles(): return lax.all_to_all(x, axis, split_axis=0, concat_axis=0, tiled=True)  4.1 us
    all_to_all x1, waiting for transfers between devices, swap_tiles(): return lax.all_to_all(x, axis, split_axis=0, concat_axis=0, tiled=True)  3.85 us
    ppermute x16, waiting for transfers between devices, exchange(): lax.ppermute(b, axis, swaps(axis, first))  3.47 us
  transfers between devices with their start and end apart: 17, of which 4 were waited for; matrix products, arithmetic and copies ran while one was open for 0% of the time, Pallas kernels for 2%

profile of v1, /device:TPU:1, one launch (start us, length us, event | category | flops | bytes accessed | tf_op | source)
XLA Modules:
  0.0 111.6 jit_solution(12809576876807934207)
XLA Ops:
  0.6 1.3 %sends.1 = (bf16[128,128]{1,0:T(8,128)(2,1)S(1)}, bf16[128,128]{1,0:T(8,128)(2,1)S(1)}, bf16[128,128]{1,0:T(8,128)(2,1)S(1)}, bf16[128,128]{1,0:T(8,128)(2,1)S(1...) custom-call(s32[4,128]{1,0:T(4,128)} %bitcast.21, bf16[256,128]{1,0:T(8,128)(2,1)} %bitcast.18), custom_call_target="tpu_custom_call" | custom-call | tf_op jit(solution)/shard_map/sends/pallas_call | solution.py:292
  1.9 4.6 %collective-permute-start.1 = (bf16[128,128]{1,0:T(8,128)(2,1)S(1)}, bf16[128,128]{1,0:T(8,128)(2,1)S(1)}, u32[]{:S(2)}, u32[]{:S(2)}) collective-permute-start(bf16[128,128]{1,0:T(8,128)(2,1)S(1)} %get-tuple-element.63), channel_id=1, source_target_pairs={{8,16},{16,8},{24,32},{32,24},{40,48},{48,40},{56,64},{64,56},{72,... | collective-permute-start | bytes 98312 | tf_op jit(solution)/shard_map/ppermute | solution.py:310
  6.5 1.7 %collective-permute-start.2 = (bf16[128,128]{1,0:T(8,128)(2,1)S(1)}, bf16[128,128]{1,0:T(8,128)(2,1)S(1)}, u32[]{:S(2)}, u32[]{:S(2)}) collective-permute-start(bf16[128,128]{1,0:T(8,128)(2,1)S(1)} %get-tuple-element.64), channel_id=1, source_target_pairs={{0,1},{1,0},{2,3},{3,2},{4,5},{5,4},{6,7},{7,6},{8,9},{9,8},{10,11... | collective-permute-start | bytes 98312 | tf_op jit(solution)/shard_map/ppermute | solution.py:310
  8.2 0.7 collective-permute-start.3
  9.7 1.8 %load.1 = (s32[3,1,512]{2,1,0:T(1,128)S(1)}, s32[3,1,512]{2,1,0:T(1,128)S(1)}, bf16[1536,128]{1,0:T(8,128)(2,1)S(1)}, bf16[256,128]{1,0:T(8,128)(2,1)S(1)}, bf16...) custom-call(s32[4]{0:T(128)S(1)} %bitcast.14, ...), custom_call_target="tpu_custom_call" | custom-call | tf_op jit(solution)/shard_map/load/pallas_call | solution.py:292
  11.5 5.6 %layer0.1 = (bf16[1536,384]{1,0:T(8,128)(2,1)S(1)}, bf16[1536,128]{1,0:T(8,128)(2,1)S(1)}, f32[1536,128]{1,0:T(8,128)S(1)}, f32[1536,128]{1,0:T(8,128)S(1)}, f32...) custom-call(s32[3,1,512]{2,1,0:T(1,128)S(1)} %get-tuple-element.59.s, ...), custom_call_target="tpu_custom_call" | custom-call | tf_op jit(solution)/shard_map/layer0/pallas_call | solution.py:292
  17.8 3.1 %collective-permute-start.5 = (bf16[128,128]{1,0:T(8,128)(2,1)S(1)}, bf16[128,128]{1,0:T(8,128)(2,1)S(1)}, u32[]{:S(2)}, u32[]{:S(2)}) collective-permute-start(bf16[128,128]{1,0:T(8,128)(2,1)S(1)} %get-tuple-element.75), channel_id=1, source_target_pairs={{8,16},{16,8},{24,32},{32,24},{40,48},{48,40},{56,64},{64,56},{72,... | collective-permute-start | bytes 98312 | tf_op jit(solution)/shard_map/ppermute | solution.py:310
  20.9 4.6 %collective-permute-start.6 = (bf16[128,128]{1,0:T(8,128)(2,1)S(1)}, bf16[128,128]{1,0:T(8,128)(2,1)S(1)}, u32[]{:S(2)}, u32[]{:S(2)}) collective-permute-start(bf16[128,128]{1,0:T(8,128)(2,1)S(1)} %get-tuple-element.76), channel_id=1, source_target_pairs={{0,1},{1,0},{2,3},{3,2},{4,5},{5,4},{6,7},{7,6},{8,9},{9,8},{10,11... | collective-permute-start | bytes 98312 | tf_op jit(solution)/shard_map/ppermute | solution.py:310
  25.5 0.7 collective-permute-start.7
  26.8 10.4 %layer1.1 = (bf16[256,128]{1,0:T(8,128)(2,1)}, bf16[1536,128]{1,0:T(8,128)(2,1)S(1)}, f32[256,128]{1,0:T(8,128)S(1)}, bf16[128,128]{1,0:T(8,128)(2,1)S(1)}, bf16...) custom-call(s32[3,1,512]{2,1,0:T(1,128)S(1)} %get-tuple-element.59.s, ...), custom_call_target="tpu_custom_call" | custom-call | tf_op jit(solution)/shard_map/layer1/pallas_call | solution.py:292
  37.3 3.6 %collective-permute-start.9 = (bf16[128,128]{1,0:T(8,128)(2,1)S(1)}, bf16[128,128]{1,0:T(8,128)(2,1)S(1)}, u32[]{:S(2)}, u32[]{:S(2)}) collective-permute-start(bf16[128,128]{1,0:T(8,128)(2,1)S(1)} %get-tuple-element.84), channel_id=1, source_target_pairs={{8,16},{16,8},{24,32},{32,24},{40,48},{48,40},{56,64},{64,56},{72,... | collective-permute-start | bytes 98312 | tf_op jit(solution)/shard_map/ppermute | solution.py:310
  40.9 5.8 %collective-permute-start.10 = (bf16[128,128]{1,0:T(8,128)(2,1)S(1)}, bf16[128,128]{1,0:T(8,128)(2,1)S(1)}, u32[]{:S(2)}, u32[]{:S(2)}) collective-permute-start(bf16[128,128]{1,0:T(8,128)(2,1)S(1)} %get-tuple-element.85), channel_id=1, source_target_pairs={{0,1},{1,0},{2,3},{3,2},{4,5},{5,4},{6,7},{7,6},{8,9},{9,8},{10,11... | collective-permute-start | bytes 98312 | tf_op jit(solution)/shard_map/ppermute | solution.py:310
  46.7 0.7 collective-permute-start.11
  48.0 5.9 %back0.1 = (bf16[1536,128]{1,0:T(8,128)(2,1)}, f32[256,128]{1,0:T(8,128)S(1)}, bf16[128,128]{1,0:T(8,128)(2,1)S(1)}, bf16[128,128]{1,0:T(8,128)(2,1)S(1)}, bf16[...) custom-call(s32[3,1,512]{2,1,0:T(1,128)S(1)} %get-tuple-element.59.snd_ref, ...), custom_call_target="tpu_custom_call" | custom-call | tf_op jit(solution)/shard_map/back0/pallas_call | solution.py:292
  54.0 19.9 %all_to_all.15.x_ref = bf16[32,64,128]{2,1,0:T(8,128)(2,1)S(1)} all-to-all(bf16[32,64,128]{2,1,0:T(8,128)(2,1)S(1)} %bitcast.13), channel_id=1, replica_groups=mesh['dom'=32,'group'=8] {'dom'}, dimensions={0} | all-to-all | bytes 1048576 | tf_op jit(solution)/shard_map/all_to_all | solution.py:326
  74.0 20.0 %all_to_all.16.x_ref = bf16[8,64,128]{2,1,0:T(8,128)(2,1)S(1)} all-to-all(bf16[8,64,128]{2,1,0:T(8,128)(2,1)S(1)} %fold_dom.1), channel_id=1, replica_groups=mesh['dom'=32,'group'=8] {'group'}, dimensions={0} | all-to-all | bytes 262144 | tf_op jit(solution)/shard_map/all_to_all | solution.py:326
  94.0 0.9 fold_group.1
  94.9 4.1 %all-to-all-start.2 = ((bf16[32,64,128]{2,1,0:T(8,128)(2,1)}), bf16[32,64,128]{2,1,0:T(8,128)(2,1)S(1)}, u32[]{:S(2)}, u32[]{:S(2)}) async-start(bf16[32,64,128]{2,1,0:T(8,128)(2,1)} %fold_group.1), calls=%async_computation.2 | async-start | bytes 1048576 | tf_op jit(solution)/shard_map/all_to_all | solution.py:326
  99.4 3.3 %collective-permute-start.13 = (bf16[128,128]{1,0:T(8,128)(2,1)S(1)}, bf16[128,128]{1,0:T(8,128)(2,1)S(1)}, u32[]{:S(2)}, u32[]{:S(2)}) collective-permute-start(bf16[128,128]{1,0:T(8,128)(2,1)S(1)} %get-tuple-element.96), channel_id=1, source_target_pairs={{8,16},{16,8},{24,32},{32,24},{40,48},{48,40},{56,64},{64,56},{72,... | collective-permute-start | bytes 98312 | tf_op jit(solution)/shard_map/ppermute | solution.py:310
  103.1 0.7 collective-permute-start.15
  103.8 2.2 %collective-permute-done.13.t1 = bf16[128,128]{1,0:T(8,128)(2,1)S(1)} collective-permute-done((bf16[128,128]{1,0:T(8,128)(2,1)S(1)}, bf16[128,128]{1,0:T(8,128)(2,1)S(1)}, u32[]{:S(2)}, u32[]{:S(2)}) %collective-permute-start.13) | collective-permute-done | bytes 32800 | tf_op jit(solution)/shard_map/ppermute | solution.py:310
  106.0 0.9 finish.1
  106.8 3.9 %all-to-all-done.2 = bf16[32,64,128]{2,1,0:T(8,128)(2,1)S(1)} async-done(((bf16[32,64,128]{2,1,0:T(8,128)(2,1)}), bf16[32,64,128]{2,1,0:T(8,128)(2,1)S(1)}, u32[]{:S(2)}, u32[]{:S(2)}) %all-to-all-start.2) | async-done | bytes 524320 | tf_op jit(solution)/shard_map/all_to_all | solution.py:326
  110.7 0.9 unpack.1
  (23 shorter events, 3.6 us)
Async XLA Ops:
  1.9 9.6 %collective-permute-start.1 = (bf16[128,128]{1,0:T(8,128)(2,1)S(1)}, bf16[128,128]{1,0:T(8,128)(2,1)S(1)}, u32[]{:S(2)}, u32[]{:S(2)}) collective-permute-start(bf16[128,128]{1,0:T(8,128)(2,1)S(1)} %get-tuple-element.63), channel_id=1, source_target_pairs={{8,16},{16,8},{24,32},{32,24},{40,48},{48,40},{56,64},{64,56},{72,... | collective-permute-start | bytes 98312 | tf_op jit(solution)/shard_map/ppermute | solution.py:310
  6.5 5.0 %collective-permute-start.2 = (bf16[128,128]{1,0:T(8,128)(2,1)S(1)}, bf16[128,128]{1,0:T(8,128)(2,1)S(1)}, u32[]{:S(2)}, u32[]{:S(2)}) collective-permute-start(bf16[128,128]{1,0:T(8,128)(2,1)S(1)} %get-tuple-element.64), channel_id=1, source_target_pairs={{0,1},{1,0},{2,3},{3,2},{4,5},{5,4},{6,7},{7,6},{8,9},{9,8},{10,11... | collective-permute-start | bytes 98312 | tf_op jit(solution)/shard_map/ppermute | solution.py:310
  8.2 3.3 %collective-permute-start.3 = (bf16[128,128]{1,0:T(8,128)(2,1)S(1)}, bf16[128,128]{1,0:T(8,128)(2,1)S(1)}, u32[]{:S(2)}, u32[]{:S(2)}) collective-permute-start(bf16[128,128]{1,0:T(8,128)(2,1)S(1)} %get-tuple-element.65), channel_id=1, source_target_pairs={{1,2},{2,1},{3,4},{4,3},{5,6},{6,5},{9,10},{10,9},{11,12},{12,11},... | collective-permute-start | bytes 98312 | tf_op jit(solution)/shard_map/ppermute | solution.py:310
  8.9 2.6 %collective-permute-start = (bf16[128,128]{1,0:T(8,128)(2,1)S(1)}, bf16[128,128]{1,0:T(8,128)(2,1)S(1)}, u32[]{:S(2)}, u32[]{:S(2)}) collective-permute-start(bf16[128,128]{1,0:T(8,128)(2,1)S(1)} %get-tuple-element.58.token), channel_id=1, source_target_pairs={{0,8},{8,0},{16,24},{24,16},{32,40},{40,32},{48,56},{56,48},{64,72... | collective-permute-start | bytes 98312 | tf_op jit(solution)/shard_map/ppermute | solution.py:310
  9.0 0.7 copy-start
  17.2 9.0 %collective-permute-start.4 = (bf16[128,128]{1,0:T(8,128)(2,1)S(1)}, bf16[128,128]{1,0:T(8,128)(2,1)S(1)}, u32[]{:S(2)}, u32[]{:S(2)}) collective-permute-start(bf16[128,128]{1,0:T(8,128)(2,1)S(1)} %get-tuple-element.74), channel_id=1, source_target_pairs={{0,8},{8,0},{16,24},{24,16},{32,40},{40,32},{48,56},{56,48},{64,72... | collective-permute-start | bytes 98312 | tf_op jit(solution)/shard_map/ppermute | solution.py:310
  17.8 8.4 %collective-permute-start.5 = (bf16[128,128]{1,0:T(8,128)(2,1)S(1)}, bf16[128,128]{1,0:T(8,128)(2,1)S(1)}, u32[]{:S(2)}, u32[]{:S(2)}) collective-permute-start(bf16[128,128]{1,0:T(8,128)(2,1)S(1)} %get-tuple-element.75), channel_id=1, source_target_pairs={{8,16},{16,8},{24,32},{32,24},{40,48},{48,40},{56,64},{64,56},{72,... | collective-permute-start | bytes 98312 | tf_op jit(solution)/shard_map/ppermute | solution.py:310
  20.9 5.9 %collective-permute-start.6 = (bf16[128,128]{1,0:T(8,128)(2,1)S(1)}, bf16[128,128]{1,0:T(8,128)(2,1)S(1)}, u32[]{:S(2)}, u32[]{:S(2)}) collective-permute-start(bf16[128,128]{1,0:T(8,128)(2,1)S(1)} %get-tuple-element.76), channel_id=1, source_target_pairs={{0,1},{1,0},{2,3},{3,2},{4,5},{5,4},{6,7},{7,6},{8,9},{9,8},{10,11... | collective-permute-start | bytes 98312 | tf_op jit(solution)/shard_map/ppermute | solution.py:310
  25.5 1.3 %collective-permute-start.7 = (bf16[128,128]{1,0:T(8,128)(2,1)S(1)}, bf16[128,128]{1,0:T(8,128)(2,1)S(1)}, u32[]{:S(2)}, u32[]{:S(2)}) collective-permute-start(bf16[128,128]{1,0:T(8,128)(2,1)S(1)} %get-tuple-element.77), channel_id=1, source_target_pairs={{1,2},{2,1},{3,4},{4,3},{5,6},{6,5},{9,10},{10,9},{11,12},{12,11},... | collective-permute-start | bytes 98312 | tf_op jit(solution)/shard_map/ppermute | solution.py:310
  37.2 10.2 %collective-permute-start.8 = (bf16[128,128]{1,0:T(8,128)(2,1)S(1)}, bf16[128,128]{1,0:T(8,128)(2,1)S(1)}, u32[]{:S(2)}, u32[]{:S(2)}) collective-permute-start(bf16[128,128]{1,0:T(8,128)(2,1)S(1)} %get-tuple-element.83), channel_id=1, source_target_pairs={{0,8},{8,0},{16,24},{24,16},{32,40},{40,32},{48,56},{56,48},{64,72... | collective-permute-start | bytes 98312 | tf_op jit(solution)/shard_map/ppermute | solution.py:310
  37.3 10.1 %collective-permute-start.9 = (bf16[128,128]{1,0:T(8,128)(2,1)S(1)}, bf16[128,128]{1,0:T(8,128)(2,1)S(1)}, u32[]{:S(2)}, u32[]{:S(2)}) collective-permute-start(bf16[128,128]{1,0:T(8,128)(2,1)S(1)} %get-tuple-element.84), channel_id=1, source_target_pairs={{8,16},{16,8},{24,32},{32,24},{40,48},{48,40},{56,64},{64,56},{72,... | collective-permute-start | bytes 98312 | tf_op jit(solution)/shard_map/ppermute | solution.py:310
  40.9 7.1 %collective-permute-start.10 = (bf16[128,128]{1,0:T(8,128)(2,1)S(1)}, bf16[128,128]{1,0:T(8,128)(2,1)S(1)}, u32[]{:S(2)}, u32[]{:S(2)}) collective-permute-start(bf16[128,128]{1,0:T(8,128)(2,1)S(1)} %get-tuple-element.85), channel_id=1, source_target_pairs={{0,1},{1,0},{2,3},{3,2},{4,5},{5,4},{6,7},{7,6},{8,9},{9,8},{10,11... | collective-permute-start | bytes 98312 | tf_op jit(solution)/shard_map/ppermute | solution.py:310
  46.7 1.3 %collective-permute-start.11 = (bf16[128,128]{1,0:T(8,128)(2,1)S(1)}, bf16[128,128]{1,0:T(8,128)(2,1)S(1)}, u32[]{:S(2)}, u32[]{:S(2)}) collective-permute-start(bf16[128,128]{1,0:T(8,128)(2,1)S(1)} %get-tuple-element.86), channel_id=1, source_target_pairs={{1,2},{2,1},{3,4},{4,3},{5,6},{6,5},{9,10},{10,9},{11,12},{12,11},... | collective-permute-start | bytes 98312 | tf_op jit(solution)/shard_map/ppermute | solution.py:310
  94.9 15.8 %all-to-all-start.2 = ((bf16[32,64,128]{2,1,0:T(8,128)(2,1)}), bf16[32,64,128]{2,1,0:T(8,128)(2,1)S(1)}, u32[]{:S(2)}, u32[]{:S(2)}) async-start(bf16[32,64,128]{2,1,0:T(8,128)(2,1)} %fold_group.1), calls=%async_computation.2 | async-start | bytes 1048576 | tf_op jit(solution)/shard_map/all_to_all | solution.py:326
  99.0 4.8 %collective-permute-start.12 = (bf16[128,128]{1,0:T(8,128)(2,1)S(1)}, bf16[128,128]{1,0:T(8,128)(2,1)S(1)}, u32[]{:S(2)}, u32[]{:S(2)}) collective-permute-start(bf16[128,128]{1,0:T(8,128)(2,1)S(1)} %get-tuple-element.95), channel_id=1, source_target_pairs={{0,8},{8,0},{16,24},{24,16},{32,40},{40,32},{48,56},{56,48},{64,72... | collective-permute-start | bytes 98312 | tf_op jit(solution)/shard_map/ppermute | solution.py:310
  99.4 6.5 %collective-permute-start.13 = (bf16[128,128]{1,0:T(8,128)(2,1)S(1)}, bf16[128,128]{1,0:T(8,128)(2,1)S(1)}, u32[]{:S(2)}, u32[]{:S(2)}) collective-permute-start(bf16[128,128]{1,0:T(8,128)(2,1)S(1)} %get-tuple-element.96), channel_id=1, source_target_pairs={{8,16},{16,8},{24,32},{32,24},{40,48},{48,40},{56,64},{64,56},{72,... | collective-permute-start | bytes 98312 | tf_op jit(solution)/shard_map/ppermute | solution.py:310
  102.7 3.2 %collective-permute-start.14 = (bf16[128,128]{1,0:T(8,128)(2,1)S(1)}, bf16[128,128]{1,0:T(8,128)(2,1)S(1)}, u32[]{:S(2)}, u32[]{:S(2)}) collective-permute-start(bf16[128,128]{1,0:T(8,128)(2,1)S(1)} %get-tuple-element.97), channel_id=1, source_target_pairs={{0,1},{1,0},{2,3},{3,2},{4,5},{5,4},{6,7},{7,6},{8,9},{9,8},{10,11... | collective-permute-start | bytes 98312 | tf_op jit(solution)/shard_map/ppermute | solution.py:310
  103.1 2.9 %collective-permute-start.15 = (bf16[128,128]{1,0:T(8,128)(2,1)S(1)}, bf16[128,128]{1,0:T(8,128)(2,1)S(1)}, u32[]{:S(2)}, u32[]{:S(2)}) collective-permute-start(bf16[128,128]{1,0:T(8,128)(2,1)S(1)} %get-tuple-element.98), channel_id=1, source_target_pairs={{1,2},{2,1},{3,4},{4,3},{5,6},{6,5},{9,10},{10,9},{11,12},{12,11},... | collective-permute-start | bytes 98312 | tf_op jit(solution)/shard_map/ppermute | solution.py:310

commit v2 on v1

--- a/solution.py
+++ b/solution.py
@@ -159,7 +159,7 @@
         agg[...] += mm(spread_rows(rcv_ref[i], 256), new)
         return carry
 
-    lax.fori_loop(0, e_ref.shape[0] // BLOCK, step, 0)
+    lax.fori_loop(0, e_ref.shape[0] // BLOCK, step, 0, unroll=True)
 
 
 def node_forward(x, agg, wn1, wn2, b_ref, g_ref):
@@ -213,7 +213,7 @@
         sums[2:3, :] += total(cot * xh)
         return carry
 
-    lax.fori_loop(0, joined.shape[0] // BLOCK, step, 0)
+    lax.fori_loop(0, joined.shape[0] // BLOCK, step, 0, unroll=True)
     for k in range(3):
         grads[128 * k : 128 * k + 128, :] = jnp.transpose(acc1[:, 128 * k : 128 * k + 128]).astype(BF16)
     grads[384:512, :] = jnp.transpose(acc2[...]).astype(BF16)
@@ -310,7 +310,8 @@
     return [lax.ppermute(b, axis, swaps(axis, first)) for b, (axis, first) in zip(blocks, plan)]
 
 
-def fold_kernel(x_ref, o_ref):
+def fold_kernel(x_ref, *refs):
+    o_ref = refs[-1]
     out = jnp.sum(x_ref[...].astype(F32), axis=0).astype(BF16)
     for k in range(o_ref.shape[0]):
         o_ref[k] = out
@@ -326,13 +327,13 @@
     return lax.all_to_all(x, axis, split_axis=0, concat_axis=0, tiled=True)
 
 
-def reduce_grads(packed, scale):
+def reduce_grads(packed, scale, first, second):
     dom, group = lax.axis_size("dom"), lax.axis_size("group")
     rows = packed.shape[0] // dom
     tiles = swap_tiles(packed.reshape(dom, rows, H), "dom")
-    (tiles,) = call(fold_kernel, [shape(group, rows, H, dtype=BF16)], [], (tiles,), "fold_dom")
+    (tiles,) = call(fold_kernel, [shape(group, rows, H, dtype=BF16)], [], (tiles, *first), "fold_dom")
     tiles = swap_tiles(tiles, "group")
-    (tiles,) = call(fold_kernel, [shape(dom, rows, H, dtype=BF16)], [], (tiles,), "fold_group")
+    (tiles,) = call(fold_kernel, [shape(dom, rows, H, dtype=BF16)], [], (tiles, *second), "fold_group")
     whole = swap_tiles(tiles, "dom").reshape(dom * rows, H)
     return call(partial(unpack_kernel, scale), [shape(2, b - a, H) for a, b in CUTS], [], (whole,), "unpack")
 
@@ -410,7 +411,7 @@
     (node_grad,) = call(finish_kernel, [shape(256, H, dtype=BF16)], [], (send, own, *back), "finish")
 
     scale = (lax.axis_size("dom") * lax.axis_size("group") * x0.shape[0]) ** (-0.5)
-    grads = reduce_grads(packed, scale)
+    grads = reduce_grads(packed, scale, back[:2], back[2:])
     return (nodes_out[None], node_grad[None], edge_grad[None], *grads)
 
 

time: 112 us -> 109 us (0.973)
  blocking collectives: 40 us -> 0 us
  starting transfers between devices: 35 us -> 55.8 us
  waiting for transfers between devices: 7.32 us -> 26.9 us
  Pallas kernels: 27.9 us -> 23.9 us
    all_to_all x2 -> x0, blocking collectives: 40 us -> none  [swap_tiles(): return lax.all_to_all(x, axis, split_axis=0, concat_axis=0, tiled=True)]
    all_to_all x1 -> x3, starting transfers between devices: 4.1 us -> 23.8 us  [swap_tiles(): return lax.all_to_all(x, axis, split_axis=0, concat_axis=0, tiled=True)]
    all_to_all x1 -> x3, waiting for transfers between devices: 3.85 us -> 19.3 us  [swap_tiles(): return lax.all_to_all(x, axis, split_axis=0, concat_axis=0, tiled=True)]
    ppermute x16, waiting for transfers between devices: 3.47 us -> 7.65 us  [exchange(): lax.ppermute(b, axis, swaps(axis, first))]
    pallas_call x9, Pallas kernels: 27.9 us -> 23.9 us  [call(): pl.pallas_call(kernel, out_shape=outs, in_specs=[pl.BlockSpec(memory_spac...]
    ppermute x16, starting transfers between devices: 30.9 us -> 32.1 us  [exchange(): lax.ppermute(b, axis, swaps(axis, first))]
  transfers between devices with their start and end apart: 17 -> 19, of which waited for: 4 -> 7; matrix products, arithmetic and copies ran while one was open for 0% -> 0% of each run, Pallas kernels for 2% -> 3%
where the time goes in v2:
time: 109 us; the launch traced here: 108 us
  starting transfers between devices  55.8 us (51%)
  waiting for transfers between devices  26.9 us (25%)
  Pallas kernels  23.9 us (22%)
    ppermute x16, starting transfers between devices, exchange(): lax.ppermute(b, axis, swaps(axis, first))  32.1 us
    pallas_call x9, Pallas kernels, call(): pl.pallas_call(kernel, out_shape=outs, in_specs=[pl.BlockSpec(memory_spac...  23.9 us
    all_to_all x3, starting transfers between devices, swap_tiles(): return lax.all_to_all(x, axis, split_axis=0, concat_axis=0, tiled=True)  23.8 us
    all_to_all x3, waiting for transfers between devices, swap_tiles(): return lax.all_to_all(x, axis, split_axis=0, concat_axis=0, tiled=True)  19.3 us
    ppermute x16, waiting for transfers between devices, exchange(): lax.ppermute(b, axis, swaps(axis, first))  7.65 us
  transfers between devices with their start and end apart: 19, of which 7 were waited for; matrix products, arithmetic and copies ran while one was open for 0% of the time, Pallas kernels for 3%

profile of v2, /device:TPU:1, one launch (start us, length us, event | category | flops | bytes accessed | tf_op | source)
XLA Modules:
  0.0 108.2 jit_solution(3010362334746665223)
XLA Ops:
  0.6 1.3 %sends.1 = (bf16[128,128]{1,0:T(8,128)(2,1)S(1)}, bf16[128,128]{1,0:T(8,128)(2,1)S(1)}, bf16[128,128]{1,0:T(8,128)(2,1)S(1)}, bf16[128,128]{1,0:T(8,128)(2,1)S(1...) custom-call(s32[4,128]{1,0:T(4,128)} %bitcast.20, bf16[256,128]{1,0:T(8,128)(2,1)} %bitcast.17), custom_call_target="tpu_custom_call" | custom-call | tf_op jit(solution)/shard_map/sends/pallas_call | solution.py:292
  1.9 4.6 %collective-permute-start.1 = (bf16[128,128]{1,0:T(8,128)(2,1)S(1)}, bf16[128,128]{1,0:T(8,128)(2,1)S(1)}, u32[]{:S(2)}, u32[]{:S(2)}) collective-permute-start(bf16[128,128]{1,0:T(8,128)(2,1)S(1)} %get-tuple-element.63), channel_id=1, source_target_pairs={{8,16},{16,8},{24,32},{32,24},{40,48},{48,40},{56,64},{64,56},{72,... | collective-permute-start | bytes 98312 | tf_op jit(solution)/shard_map/ppermute | solution.py:310
  6.5 1.7 %collective-permute-start.2 = (bf16[128,128]{1,0:T(8,128)(2,1)S(1)}, bf16[128,128]{1,0:T(8,128)(2,1)S(1)}, u32[]{:S(2)}, u32[]{:S(2)}) collective-permute-start(bf16[128,128]{1,0:T(8,128)(2,1)S(1)} %get-tuple-element.64), channel_id=1, source_target_pairs={{0,1},{1,0},{2,3},{3,2},{4,5},{5,4},{6,7},{7,6},{8,9},{9,8},{10,11... | collective-permute-start | bytes 98312 | tf_op jit(solution)/shard_map/ppermute | solution.py:310
  9.7 1.8 %load.1 = (s32[3,1,512]{2,1,0:T(1,128)S(1)}, s32[3,1,512]{2,1,0:T(1,128)S(1)}, bf16[1536,128]{1,0:T(8,128)(2,1)S(1)}, bf16[256,128]{1,0:T(8,128)(2,1)S(1)}, bf16...) custom-call(s32[4]{0:T(128)S(1)} %bitcast.13, ...), custom_call_target="tpu_custom_call" | custom-call | tf_op jit(solution)/shard_map/load/pallas_call | solution.py:292
  11.5 4.7 %layer0.1 = (bf16[1536,384]{1,0:T(8,128)(2,1)S(1)}, bf16[1536,128]{1,0:T(8,128)(2,1)S(1)}, f32[1536,128]{1,0:T(8,128)S(1)}, f32[1536,128]{1,0:T(8,128)S(1)}, f32...) custom-call(s32[3,1,512]{2,1,0:T(1,128)S(1)} %get-tuple-element.59.s, ...), custom_call_target="tpu_custom_call" | custom-call | tf_op jit(solution)/shard_map/layer0/pallas_call | solution.py:292
  16.9 3.1 %collective-permute-start.5 = (bf16[128,128]{1,0:T(8,128)(2,1)S(1)}, bf16[128,128]{1,0:T(8,128)(2,1)S(1)}, u32[]{:S(2)}, u32[]{:S(2)}) collective-permute-start(bf16[128,128]{1,0:T(8,128)(2,1)S(1)} %get-tuple-element.75), channel_id=1, source_target_pairs={{8,16},{16,8},{24,32},{32,24},{40,48},{48,40},{56,64},{64,56},{72,... | collective-permute-start | bytes 98312 | tf_op jit(solution)/shard_map/ppermute | solution.py:310
  20.0 4.6 %collective-permute-start.6 = (bf16[128,128]{1,0:T(8,128)(2,1)S(1)}, bf16[128,128]{1,0:T(8,128)(2,1)S(1)}, u32[]{:S(2)}, u32[]{:S(2)}) collective-permute-start(bf16[128,128]{1,0:T(8,128)(2,1)S(1)} %get-tuple-element.76), channel_id=1, source_target_pairs={{0,1},{1,0},{2,3},{3,2},{4,5},{5,4},{6,7},{7,6},{8,9},{9,8},{10,11... | collective-permute-start | bytes 98312 | tf_op jit(solution)/shard_map/ppermute | solution.py:310
  25.9 8.0 %layer1.1 = (bf16[256,128]{1,0:T(8,128)(2,1)}, bf16[1536,128]{1,0:T(8,128)(2,1)S(1)}, f32[256,128]{1,0:T(8,128)S(1)}, bf16[128,128]{1,0:T(8,128)(2,1)S(1)}, bf16...) custom-call(s32[3,1,512]{2,1,0:T(1,128)S(1)} %get-tuple-element.59.s, ...), custom_call_target="tpu_custom_call" | custom-call | tf_op jit(solution)/shard_map/layer1/pallas_call | solution.py:292
  33.9 3.6 %collective-permute-start.9 = (bf16[128,128]{1,0:T(8,128)(2,1)S(1)}, bf16[128,128]{1,0:T(8,128)(2,1)S(1)}, u32[]{:S(2)}, u32[]{:S(2)}) collective-permute-start(bf16[128,128]{1,0:T(8,128)(2,1)S(1)} %get-tuple-element.84), channel_id=1, source_target_pairs={{8,16},{16,8},{24,32},{32,24},{40,48},{48,40},{56,64},{64,56},{72,... | collective-permute-start | bytes 98312 | tf_op jit(solution)/shard_map/ppermute | solution.py:310
  37.5 5.8 %collective-permute-start.10 = (bf16[128,128]{1,0:T(8,128)(2,1)S(1)}, bf16[128,128]{1,0:T(8,128)(2,1)S(1)}, u32[]{:S(2)}, u32[]{:S(2)}) collective-permute-start(bf16[128,128]{1,0:T(8,128)(2,1)S(1)} %get-tuple-element.85), channel_id=1, source_target_pairs={{0,1},{1,0},{2,3},{3,2},{4,5},{5,4},{6,7},{7,6},{8,9},{9,8},{10,11... | collective-permute-start | bytes 98312 | tf_op jit(solution)/shard_map/ppermute | solution.py:310
  44.6 4.7 %back0.1 = (bf16[1536,128]{1,0:T(8,128)(2,1)}, f32[256,128]{1,0:T(8,128)S(1)}, bf16[128,128]{1,0:T(8,128)(2,1)S(1)}, bf16[128,128]{1,0:T(8,128)(2,1)S(1)}, bf16[...) custom-call(s32[3,1,512]{2,1,0:T(1,128)S(1)} %get-tuple-element.59.snd_ref, ...), custom_call_target="tpu_custom_call" | custom-call | tf_op jit(solution)/shard_map/back0/pallas_call | solution.py:292
  49.3 8.6 %all-to-all-start = ((bf16[32,64,128]{2,1,0:T(8,128)(2,1)}), bf16[32,64,128]{2,1,0:T(8,128)(2,1)S(1)}, u32[]{:S(2)}, u32[]{:S(2)}) async-start(bf16[32,64,128]{2,1,0:T(8,128)(2,1)} %bitcast.10), calls=%async_computation | async-start | bytes 1048576 | tf_op jit(solution)/shard_map/all_to_all | solution.py:327
  58.2 3.4 %collective-permute-start.13 = (bf16[128,128]{1,0:T(8,128)(2,1)S(1)}, bf16[128,128]{1,0:T(8,128)(2,1)S(1)}, u32[]{:S(2)}, u32[]{:S(2)}) collective-permute-start(bf16[128,128]{1,0:T(8,128)(2,1)S(1)} %get-tuple-element.96), channel_id=1, source_target_pairs={{8,16},{16,8},{24,32},{32,24},{40,48},{48,40},{56,64},{64,56},{72,... | collective-permute-start | bytes 98312 | tf_op jit(solution)/shard_map/ppermute | solution.py:310
  61.6 3.1 %collective-permute-done.13.t1.refs_1_ = bf16[128,128]{1,0:T(8,128)(2,1)S(1)} collective-permute-done((bf16[128,128]{1,0:T(8,128)(2,1)S(1)}, bf16[128,128]{1,0:T(8,128)(2,1)S(1)}, u32[]{:S(2)}, u32[]{:S(2)}) %collective-permute-start.13) | collective-permute-done | bytes 32800 | tf_op jit(solution)/shard_map/ppermute | solution.py:310
  64.7 4.7 %all-to-all-done.x_ref = bf16[32,64,128]{2,1,0:T(8,128)(2,1)S(1)} async-done(((bf16[32,64,128]{2,1,0:T(8,128)(2,1)}), bf16[32,64,128]{2,1,0:T(8,128)(2,1)S(1)}, u32[]{:S(2)}, u32[]{:S(2)}) %all-to-all-start) | async-done | bytes 524320 | tf_op jit(solution)/shard_map/all_to_all | solution.py:327
  70.2 10.7 %all-to-all-start.1 = ((bf16[8,64,128]{2,1,0:T(8,128)(2,1)}), bf16[8,64,128]{2,1,0:T(8,128)(2,1)S(1)}, u32[]{:S(2)}, u32[]{:S(2)}) async-start(bf16[8,64,128]{2,1,0:T(8,128)(2,1)} %fold_dom.1), calls=%async_computation.1 | async-start | bytes 262144 | tf_op jit(solution)/shard_map/all_to_all | solution.py:327
  80.9 1.5 %collective-permute-start.14 = (bf16[128,128]{1,0:T(8,128)(2,1)S(1)}, bf16[128,128]{1,0:T(8,128)(2,1)S(1)}, u32[]{:S(2)}, u32[]{:S(2)}) collective-permute-start(bf16[128,128]{1,0:T(8,128)(2,1)S(1)} %get-tuple-element.97), channel_id=1, source_target_pairs={{0,1},{1,0},{2,3},{3,2},{4,5},{5,4},{6,7},{7,6},{8,9},{9,8},{10,11... | collective-permute-start | bytes 98312 | tf_op jit(solution)/shard_map/ppermute | solution.py:310
  83.0 3.4 %collective-permute-done.14.t2.refs_0_ = bf16[128,128]{1,0:T(8,128)(2,1)S(1)} collective-permute-done((bf16[128,128]{1,0:T(8,128)(2,1)S(1)}, bf16[128,128]{1,0:T(8,128)(2,1)S(1)}, u32[]{:S(2)}, u32[]{:S(2)}) %collective-permute-start.14) | collective-permute-done | bytes 32800 | tf_op jit(solution)/shard_map/ppermute | solution.py:310
  86.5 3.7 %all-to-all-done.1.x_ref = bf16[8,64,128]{2,1,0:T(8,128)(2,1)S(1)} async-done(((bf16[8,64,128]{2,1,0:T(8,128)(2,1)}), bf16[8,64,128]{2,1,0:T(8,128)(2,1)S(1)}, u32[]{:S(2)}, u32[]{:S(2)}) %all-to-all-start.1) | async-done | bytes 131104 | tf_op jit(solution)/shard_map/all_to_all | solution.py:327
  90.2 0.9 fold_group.1
  91.1 4.4 %all-to-all-start.2 = ((bf16[32,64,128]{2,1,0:T(8,128)(2,1)}), bf16[32,64,128]{2,1,0:T(8,128)(2,1)S(1)}, u32[]{:S(2)}, u32[]{:S(2)}) async-start(bf16[32,64,128]{2,1,0:T(8,128)(2,1)} %fold_group.1), calls=%async_computation.2 | async-start | bytes 1048576 | tf_op jit(solution)/shard_map/all_to_all | solution.py:327
  95.5 0.9 finish.1
  96.4 10.8 %all-to-all-done.2 = bf16[32,64,128]{2,1,0:T(8,128)(2,1)S(1)} async-done(((bf16[32,64,128]{2,1,0:T(8,128)(2,1)}), bf16[32,64,128]{2,1,0:T(8,128)(2,1)S(1)}, u32[]{:S(2)}, u32[]{:S(2)}) %all-to-all-start.2) | async-done | bytes 524320 | tf_op jit(solution)/shard_map/all_to_all | solution.py:327
  107.2 0.9 unpack.1
  (25 shorter events, 6.3 us)
Async XLA Ops:
  1.9 9.6 %collective-permute-start.1 = (bf16[128,128]{1,0:T(8,128)(2,1)S(1)}, bf16[128,128]{1,0:T(8,128)(2,1)S(1)}, u32[]{:S(2)}, u32[]{:S(2)}) collective-permute-start(bf16[128,128]{1,0:T(8,128)(2,1)S(1)} %get-tuple-element.63), channel_id=1, source_target_pairs={{8,16},{16,8},{24,32},{32,24},{40,48},{48,40},{56,64},{64,56},{72,... | collective-permute-start | bytes 98312 | tf_op jit(solution)/shard_map/ppermute | solution.py:310
  6.5 5.0 %collective-permute-start.2 = (bf16[128,128]{1,0:T(8,128)(2,1)S(1)}, bf16[128,128]{1,0:T(8,128)(2,1)S(1)}, u32[]{:S(2)}, u32[]{:S(2)}) collective-permute-start(bf16[128,128]{1,0:T(8,128)(2,1)S(1)} %get-tuple-element.64), channel_id=1, source_target_pairs={{0,1},{1,0},{2,3},{3,2},{4,5},{5,4},{6,7},{7,6},{8,9},{9,8},{10,11... | collective-permute-start | bytes 98312 | tf_op jit(solution)/shard_map/ppermute | solution.py:310
  8.2 3.3 %collective-permute-start.3 = (bf16[128,128]{1,0:T(8,128)(2,1)S(1)}, bf16[128,128]{1,0:T(8,128)(2,1)S(1)}, u32[]{:S(2)}, u32[]{:S(2)}) collective-permute-start(bf16[128,128]{1,0:T(8,128)(2,1)S(1)} %get-tuple-element.65), channel_id=1, source_target_pairs={{1,2},{2,1},{3,4},{4,3},{5,6},{6,5},{9,10},{10,9},{11,12},{12,11},... | collective-permute-start | bytes 98312 | tf_op jit(solution)/shard_map/ppermute | solution.py:310
  8.9 2.6 %collective-permute-start = (bf16[128,128]{1,0:T(8,128)(2,1)S(1)}, bf16[128,128]{1,0:T(8,128)(2,1)S(1)}, u32[]{:S(2)}, u32[]{:S(2)}) collective-permute-start(bf16[128,128]{1,0:T(8,128)(2,1)S(1)} %get-tuple-element.58.token), channel_id=1, source_target_pairs={{0,8},{8,0},{16,24},{24,16},{32,40},{40,32},{48,56},{56,48},{64,72... | collective-permute-start | bytes 98312 | tf_op jit(solution)/shard_map/ppermute | solution.py:310
  9.0 0.7 copy-start
  16.3 9.1 %collective-permute-start.4 = (bf16[128,128]{1,0:T(8,128)(2,1)S(1)}, bf16[128,128]{1,0:T(8,128)(2,1)S(1)}, u32[]{:S(2)}, u32[]{:S(2)}) collective-permute-start(bf16[128,128]{1,0:T(8,128)(2,1)S(1)} %get-tuple-element.74), channel_id=1, source_target_pairs={{0,8},{8,0},{16,24},{24,16},{32,40},{40,32},{48,56},{56,48},{64,72... | collective-permute-start | bytes 98312 | tf_op jit(solution)/shard_map/ppermute | solution.py:310
  16.9 8.6 %collective-permute-start.5 = (bf16[128,128]{1,0:T(8,128)(2,1)S(1)}, bf16[128,128]{1,0:T(8,128)(2,1)S(1)}, u32[]{:S(2)}, u32[]{:S(2)}) collective-permute-start(bf16[128,128]{1,0:T(8,128)(2,1)S(1)} %get-tuple-element.75), channel_id=1, source_target_pairs={{8,16},{16,8},{24,32},{32,24},{40,48},{48,40},{56,64},{64,56},{72,... | collective-permute-start | bytes 98312 | tf_op jit(solution)/shard_map/ppermute | solution.py:310
  20.0 5.9 %collective-permute-start.6 = (bf16[128,128]{1,0:T(8,128)(2,1)S(1)}, bf16[128,128]{1,0:T(8,128)(2,1)S(1)}, u32[]{:S(2)}, u32[]{:S(2)}) collective-permute-start(bf16[128,128]{1,0:T(8,128)(2,1)S(1)} %get-tuple-element.76), channel_id=1, source_target_pairs={{0,1},{1,0},{2,3},{3,2},{4,5},{5,4},{6,7},{7,6},{8,9},{9,8},{10,11... | collective-permute-start | bytes 98312 | tf_op jit(solution)/shard_map/ppermute | solution.py:310
  24.6 1.3 %collective-permute-start.7 = (bf16[128,128]{1,0:T(8,128)(2,1)S(1)}, bf16[128,128]{1,0:T(8,128)(2,1)S(1)}, u32[]{:S(2)}, u32[]{:S(2)}) collective-permute-start(bf16[128,128]{1,0:T(8,128)(2,1)S(1)} %get-tuple-element.77), channel_id=1, source_target_pairs={{1,2},{2,1},{3,4},{4,3},{5,6},{6,5},{9,10},{10,9},{11,12},{12,11},... | collective-permute-start | bytes 98312 | tf_op jit(solution)/shard_map/ppermute | solution.py:310
  33.9 10.1 %collective-permute-start.8 = (bf16[128,128]{1,0:T(8,128)(2,1)S(1)}, bf16[128,128]{1,0:T(8,128)(2,1)S(1)}, u32[]{:S(2)}, u32[]{:S(2)}) collective-permute-start(bf16[128,128]{1,0:T(8,128)(2,1)S(1)} %get-tuple-element.83), channel_id=1, source_target_pairs={{0,8},{8,0},{16,24},{24,16},{32,40},{40,32},{48,56},{56,48},{64,72... | collective-permute-start | bytes 98312 | tf_op jit(solution)/shard_map/ppermute | solution.py:310
  33.9 10.1 %collective-permute-start.9 = (bf16[128,128]{1,0:T(8,128)(2,1)S(1)}, bf16[128,128]{1,0:T(8,128)(2,1)S(1)}, u32[]{:S(2)}, u32[]{:S(2)}) collective-permute-start(bf16[128,128]{1,0:T(8,128)(2,1)S(1)} %get-tuple-element.84), channel_id=1, source_target_pairs={{8,16},{16,8},{24,32},{32,24},{40,48},{48,40},{56,64},{64,56},{72,... | collective-permute-start | bytes 98312 | tf_op jit(solution)/shard_map/ppermute | solution.py:310
  37.5 7.1 %collective-permute-start.10 = (bf16[128,128]{1,0:T(8,128)(2,1)S(1)}, bf16[128,128]{1,0:T(8,128)(2,1)S(1)}, u32[]{:S(2)}, u32[]{:S(2)}) collective-permute-start(bf16[128,128]{1,0:T(8,128)(2,1)S(1)} %get-tuple-element.85), channel_id=1, source_target_pairs={{0,1},{1,0},{2,3},{3,2},{4,5},{5,4},{6,7},{7,6},{8,9},{9,8},{10,11... | collective-permute-start | bytes 98312 | tf_op jit(solution)/shard_map/ppermute | solution.py:310
  43.2 1.3 %collective-permute-start.11 = (bf16[128,128]{1,0:T(8,128)(2,1)S(1)}, bf16[128,128]{1,0:T(8,128)(2,1)S(1)}, u32[]{:S(2)}, u32[]{:S(2)}) collective-permute-start(bf16[128,128]{1,0:T(8,128)(2,1)S(1)} %get-tuple-element.86), channel_id=1, source_target_pairs={{1,2},{2,1},{3,4},{4,3},{5,6},{6,5},{9,10},{10,9},{11,12},{12,11},... | collective-permute-start | bytes 98312 | tf_op jit(solution)/shard_map/ppermute | solution.py:310
  49.3 20.2 %all-to-all-start = ((bf16[32,64,128]{2,1,0:T(8,128)(2,1)}), bf16[32,64,128]{2,1,0:T(8,128)(2,1)S(1)}, u32[]{:S(2)}, u32[]{:S(2)}) async-start(bf16[32,64,128]{2,1,0:T(8,128)(2,1)} %bitcast.10), calls=%async_computation | async-start | bytes 1048576 | tf_op jit(solution)/shard_map/all_to_all | solution.py:327
  57.9 3.7 %collective-permute-start.12 = (bf16[128,128]{1,0:T(8,128)(2,1)S(1)}, bf16[128,128]{1,0:T(8,128)(2,1)S(1)}, u32[]{:S(2)}, u32[]{:S(2)}) collective-permute-start(bf16[128,128]{1,0:T(8,128)(2,1)S(1)} %get-tuple-element.95), channel_id=1, source_target_pairs={{0,8},{8,0},{16,24},{24,16},{32,40},{40,32},{48,56},{56,48},{64,72... | collective-permute-start | bytes 98312 | tf_op jit(solution)/shard_map/ppermute | solution.py:310
  58.2 6.5 %collective-permute-start.13 = (bf16[128,128]{1,0:T(8,128)(2,1)S(1)}, bf16[128,128]{1,0:T(8,128)(2,1)S(1)}, u32[]{:S(2)}, u32[]{:S(2)}) collective-permute-start(bf16[128,128]{1,0:T(8,128)(2,1)S(1)} %get-tuple-element.96), channel_id=1, source_target_pairs={{8,16},{16,8},{24,32},{32,24},{40,48},{48,40},{56,64},{64,56},{72,... | collective-permute-start | bytes 98312 | tf_op jit(solution)/shard_map/ppermute | solution.py:310
  70.2 20.0 %all-to-all-start.1 = ((bf16[8,64,128]{2,1,0:T(8,128)(2,1)}), bf16[8,64,128]{2,1,0:T(8,128)(2,1)S(1)}, u32[]{:S(2)}, u32[]{:S(2)}) async-start(bf16[8,64,128]{2,1,0:T(8,128)(2,1)} %fold_dom.1), calls=%async_computation.1 | async-start | bytes 262144 | tf_op jit(solution)/shard_map/all_to_all | solution.py:327
  80.9 5.6 %collective-permute-start.14 = (bf16[128,128]{1,0:T(8,128)(2,1)S(1)}, bf16[128,128]{1,0:T(8,128)(2,1)S(1)}, u32[]{:S(2)}, u32[]{:S(2)}) collective-permute-start(bf16[128,128]{1,0:T(8,128)(2,1)S(1)} %get-tuple-element.97), channel_id=1, source_target_pairs={{0,1},{1,0},{2,3},{3,2},{4,5},{5,4},{6,7},{7,6},{8,9},{9,8},{10,11... | collective-permute-start | bytes 98312 | tf_op jit(solution)/shard_map/ppermute | solution.py:310
  82.4 4.1 %collective-permute-start.15 = (bf16[128,128]{1,0:T(8,128)(2,1)S(1)}, bf16[128,128]{1,0:T(8,128)(2,1)S(1)}, u32[]{:S(2)}, u32[]{:S(2)}) collective-permute-start(bf16[128,128]{1,0:T(8,128)(2,1)S(1)} %get-tuple-element.98), channel_id=1, source_target_pairs={{1,2},{2,1},{3,4},{4,3},{5,6},{6,5},{9,10},{10,9},{11,12},{12,11},... | collective-permute-start | bytes 98312 | tf_op jit(solution)/shard_map/ppermute | solution.py:310
  91.1 16.1 %all-to-all-start.2 = ((bf16[32,64,128]{2,1,0:T(8,128)(2,1)}), bf16[32,64,128]{2,1,0:T(8,128)(2,1)S(1)}, u32[]{:S(2)}, u32[]{:S(2)}) async-start(bf16[32,64,128]{2,1,0:T(8,128)(2,1)} %fold_group.1), calls=%async_computation.2 | async-start | bytes 1048576 | tf_op jit(solution)/shard_map/all_to_all | solution.py:327

commit v3 on v2

--- a/solution.py
+++ b/solution.py
@@ -124,14 +124,14 @@
     write_sends(send_ref, x_ref[...], (o0, o1, o2, o3))
 
 
-def load_kernel(cnt, token, *refs):
-    sems = refs[-1]
-    n = (len(refs) - 1) // 2
-    copies = fetch(tuple(zip(refs[:n], refs[n:-1])), sems)
+def load_kernel(cnt_hbm, token, *refs):
+    cnt_ref, sems = refs[-2:]
+    n = len(refs) // 2 - 1
+    copies = fetch(((cnt_hbm, cnt_ref), *zip(refs[:n], refs[n:-2])), sems)
     for c in copies:
         c.wait()
     snd_ref = refs[n]
-    snd_ref[...] = slot_ids(snd_ref[...], (cnt[0], cnt[1], cnt[2]))
+    snd_ref[...] = slot_ids(snd_ref[...], [cnt_ref[0, k] for k in range(3)])
 
 
 def edge_forward(snd_ref, rcv_ref, table, e_ref, w1, w2, b_ref, g_ref, joined, hidden, slope, xhat, scale, e_new, agg):
@@ -171,7 +171,7 @@
     return new, (joined, act, slo, xh, sc)
 
 
-def node_backward(cot, saved, wn1, wn2, g_ref, grads):
+def node_backward(cot, saved, wn1, wn2, g_ref):
     joined, act, slo, xh, sc = saved
     cot = cot.astype(F32)
     back = norm_back(cot, xh, sc, g_ref[1:2, :])
@@ -179,16 +179,12 @@
     dpre = mm_nt(back_b, wn2[...]).astype(BF16).astype(F32) * slo
     dpre_b = dpre.astype(BF16)
     djoined = mm_nt(dpre_b, wn1[...]).astype(BF16)
-    grads[512:768, :] = mm_tn(joined, dpre_b).astype(BF16)
-    grads[768:896, :] = mm_tn(act, back_b).astype(BF16)
     small = (total(dpre), total(back), total(cot * xh))
-    return cot + djoined[:, 0:128].astype(F32), djoined[:, 128:256], small
-
-
-def edge_backward(snd_ref, rcv_ref, w1, w2, g_ref, joined, hidden, slope, xhat, scale, dagg, e_cot, e_grad, acc, acc1, acc2, sums, grads):
+    return cot + djoined[:, 0:128].astype(F32), djoined[:, 128:256], (joined, dpre_b, act, back_b), small
+
+
+def edge_backward(snd_ref, rcv_ref, w1, w2, g_ref, slope, xhat, scale, dagg, e_cot, e_grad, acc, dpres, backs, sums):
     acc[...] = jnp.zeros(acc.shape, F32)
-    acc1[...] = jnp.zeros(acc1.shape, F32)
-    acc2[...] = jnp.zeros(acc2.shape, F32)
     sums[...] = jnp.zeros(sums.shape, F32)
 
     def step(i, carry):
@@ -203,27 +199,38 @@
         dpre_b = dpre.astype(BF16)
         djoined = mm_nt(dpre_b, w1[...]).astype(BF16)
         e_grad[rows, :] = (cot + djoined[:, 0:128].astype(F32)).astype(BF16)
-        ids = snd_ref[i]
-        acc[...] += mm(spread_rows(ids, 768), djoined[:, 128:256])
+        acc[...] += mm(spread_rows(snd_ref[i], 768), djoined[:, 128:256])
         acc[0:256, :] += mm(spread_rows(rcv_ref[i], 256), djoined[:, 256:384])
-        acc1[...] += mm_tn(dpre_b, joined[rows, :])
-        acc2[...] += mm_tn(back_b, hidden[rows, :])
+        dpres[rows, :] = dpre_b
+        backs[rows, :] = back_b
         sums[0:1, :] += total(dpre)
         sums[1:2, :] += total(back)
         sums[2:3, :] += total(cot * xh)
         return carry
 
-    lax.fori_loop(0, joined.shape[0] // BLOCK, step, 0, unroll=True)
+    lax.fori_loop(0, slope.shape[0] // BLOCK, step, 0, unroll=True)
+
+
+def weight_grads(node_ops, joined, dpres, hidden, backs, grads):
+    joined_n, dpre_n, act_n, back_n = node_ops
+    first = mm_tn(dpres[...], joined[...])
     for k in range(3):
-        grads[128 * k : 128 * k + 128, :] = jnp.transpose(acc1[:, 128 * k : 128 * k + 128]).astype(BF16)
-    grads[384:512, :] = jnp.transpose(acc2[...]).astype(BF16)
-
-
-def write_small(grads, sums, small):
+        grads[128 * k : 128 * k + 128, :] = jnp.transpose(first[:, 128 * k : 128 * k + 128]).astype(BF16)
+    grads[384:512, :] = jnp.transpose(mm_tn(backs[...], hidden[...])).astype(BF16)
+    grads[512:768, :] = mm_tn(joined_n, dpre_n).astype(BF16)
+    grads[768:896, :] = mm_tn(act_n, back_n).astype(BF16)
+
+
+def grads_kernel(joined_n, dpre_n, act_n, back_n, joined, dpres, hidden, backs, tail, grads):
+    weight_grads((joined_n[...], dpre_n[...], act_n[...], back_n[...]), joined, dpres, hidden, backs, grads)
+    grads[896:GRAD_ROWS, :] = tail[...]
+
+
+def small_rows(sums, small):
     tail = jnp.concatenate(
         [sums[0:2, :], small[0], small[1], sums[2:3, :], small[2], jnp.zeros((GRAD_ROWS - 902, H), F32)], axis=0
     )
-    grads[896:GRAD_ROWS, :] = tail.astype(BF16)
+    return tail.astype(BF16)
 
 
 def first_kernel(
@@ -241,17 +248,19 @@
 
 def last_kernel(
     snd_ref, rcv_ref, x_ref, r0, r1, r2, r3, e_ref, w1, w2, wn1, wn2, b_ref, g_ref, cot_ref,
-    x_new, e_grad, x_grad, c0, c1, c2, c3, grads,
-    table, agg, joined, hidden, slope, xhat, scale, acc, acc1, acc2, sums,
+    x_new, e_grad, x_grad, c0, c1, c2, c3, joined_n, dpre_n, act_n, back_n, joined, dpres, hidden, backs, tail,
+    table, agg, slope, xhat, scale, acc, sums,
 ):
     w1, w2, wn1, wn2, b_ref, g_ref = (r.at[1] for r in (w1, w2, wn1, wn2, b_ref, g_ref))
     fill_table(table, x_ref, (r0, r1, r2, r3))
     edge_forward(snd_ref, rcv_ref, table, e_ref, w1, w2, b_ref, g_ref, joined, hidden, slope, xhat, scale, None, agg)
     new, saved = node_forward(x_ref[...], agg[...], wn1, wn2, b_ref, g_ref)
     x_new[...] = new
-    dx, dagg, small = node_backward(cot_ref[...], saved, wn1, wn2, g_ref, grads)
-    edge_backward(snd_ref, rcv_ref, w1, w2, g_ref, joined, hidden, slope, xhat, scale, dagg, None, e_grad, acc, acc1, acc2, sums, grads)
-    write_small(grads, sums, small)
+    dx, dagg, node_ops, small = node_backward(cot_ref[...], saved, wn1, wn2, g_ref)
+    for out, op in zip((joined_n, dpre_n, act_n, back_n), node_ops):
+        out[...] = op
+    edge_backward(snd_ref, rcv_ref, w1, w2, g_ref, slope, xhat, scale, dagg, None, e_grad, acc, dpres, backs, sums)
+    tail[...] = small_rows(sums, small)
     x_grad[...] = dx + acc[0:256, :]
     write_backs(acc, (c0, c1, c2, c3))
 
@@ -259,15 +268,16 @@
 def back_kernel(
     snd_ref, rcv_ref, send_ref, x_ref, agg_b, own_ref, t0, t1, t2, t3, joined, hidden, slope, xhat, scale, e_cot, late,
     w1, w2, wn1, wn2, b_ref, g_ref,
-    e_grad, x_grad, c0, c1, c2, c3, grads, acc, acc1, acc2, sums,
+    e_grad, x_grad, c0, c1, c2, c3, grads, acc, dpres, backs, sums,
 ):
     w1, w2, wn1, wn2, b_ref, g_ref = (r.at[0] for r in (w1, w2, wn1, wn2, b_ref, g_ref))
     grads[GRAD_ROWS:, :] = late[...]
     cot = (own_ref[...] + add_returns(send_ref, (t0, t1, t2, t3))).astype(BF16)
     new, saved = node_forward(x_ref[...], agg_b[...], wn1, wn2, b_ref, g_ref)
-    dx, dagg, small = node_backward(cot, saved, wn1, wn2, g_ref, grads)
-    edge_backward(snd_ref, rcv_ref, w1, w2, g_ref, joined, hidden, slope, xhat, scale, dagg, e_cot, e_grad, acc, acc1, acc2, sums, grads)
-    write_small(grads, sums, small)
+    dx, dagg, node_ops, small = node_backward(cot, saved, wn1, wn2, g_ref)
+    edge_backward(snd_ref, rcv_ref, w1, w2, g_ref, slope, xhat, scale, dagg, e_cot, e_grad, acc, dpres, backs, sums)
+    weight_grads(node_ops, joined, dpres, hidden, backs, grads)
+    grads[896:GRAD_ROWS, :] = small_rows(sums, small)
     x_grad[...] = dx + acc[0:256, :]
     write_backs(acc, (c0, c1, c2, c3))
 
@@ -294,7 +304,7 @@
         out_shape=outs,
         in_specs=[pl.BlockSpec(memory_space=m) for m in spaces],
         out_specs=[pl.BlockSpec(memory_space=VMEM)] * len(outs),
-        scratch_shapes=[VMEM(s.shape, s.dtype) for s in scratch] + extra,
+        scratch_shapes=[s if s.__class__ is not jax.ShapeDtypeStruct else VMEM(s.shape, s.dtype) for s in scratch] + extra,
         compiler_params=pltpu.CompilerParams(vmem_limit_bytes=VMEM_LIMIT),
         name=name,
     )(*args)
@@ -342,7 +352,6 @@
     x0 = nodes[0]
     e0 = edges[0]
     send = send_index[0]
-    counts = halo_count[0]
     n_edge = e0.shape[0]
     snd = senders[0].reshape(n_edge // BLOCK, 1, BLOCK)
     rcv = receivers[0].reshape(n_edge // BLOCK, 1, BLOCK)
@@ -355,7 +364,9 @@
         shape(n_edge, H),
         shape(n_edge, 1),
     ]
-    accs = [shape(768, H), shape(H, 3 * H), shape(H, H), shape(8, H)]
+    low = shape(n_edge, H, dtype=BF16)
+    small = shape(256, H, dtype=BF16)
+    operands = [shape(256, 2 * H, dtype=BF16), small, small, small, residuals[0], low, low, low, shape(GRAD_ROWS - 896, H, dtype=BF16)]
     table = shape(768, H, dtype=BF16)
 
     *sent, send, x0 = call(
@@ -371,11 +382,11 @@
     loaded = call(
         load_kernel,
         [shape(*a.shape, dtype=a.dtype) for a in raw],
-        [],
-        (counts, sent[0], *raw),
+        [SMEM((1, 4), jnp.int32)],
+        (halo_count, sent[0], *raw),
         "load",
-        [SMEM, VMEM] + [HBM] * len(raw),
-        len(raw),
+        [HBM, VMEM] + [HBM] * len(raw),
+        1 + len(raw),
     )
     snd, rcv, e0, cot, *weights = loaded
     got = exchange(sent)
@@ -390,18 +401,18 @@
     got = exchange(sent)
     out = call(
         last_kernel,
-        [shape(256, H, dtype=BF16), shape(n_edge, H, dtype=BF16), shape(256, H)] + rows4 + [shape(GRAD_ROWS, H, dtype=BF16)],
-        [table, shape(256, H)] + residuals + accs,
+        [shape(256, H, dtype=BF16), shape(n_edge, H, dtype=BF16), shape(256, H)] + rows4 + operands,
+        [table, shape(256, H)] + residuals[2:] + [shape(768, H), shape(8, H)],
         (snd, rcv, x1, *got, e1, *weights, cot),
         "layer1",
     )
     nodes_out, e_cot, own = out[:3]
-    grads1 = out[7]
     back = exchange(out[3:7])
+    (grads1,) = call(grads_kernel, [shape(GRAD_ROWS, H, dtype=BF16)], [], out[7:], "wgrad1")
     out = call(
         back_kernel,
         [shape(n_edge, H, dtype=BF16), shape(256, H)] + rows4 + [shape(2 * GRAD_ROWS, H, dtype=BF16)],
-        accs,
+        [shape(768, H), low, low, shape(8, H)],
         (snd, rcv, send, x0, agg0, own, *back, *saved, e_cot, grads1, *weights),
         "back0",
     )
@@ -411,7 +422,7 @@
     (node_grad,) = call(finish_kernel, [shape(256, H, dtype=BF16)], [], (send, own, *back), "finish")
 
     scale = (lax.axis_size("dom") * lax.axis_size("group") * x0.shape[0]) ** (-0.5)
-    grads = reduce_grads(packed, scale, back[:2], back[2:])
+    grads = reduce_grads(packed, scale, back[:2], ())
     return (nodes_out[None], node_grad[None], edge_grad[None], *grads)
 
 

time: 109 us -> 108 us (level)
  blocking collectives: 0 us -> 20.8 us
  starting transfers between devices: 55.8 us -> 43.9 us
  waiting for transfers between devices: 26.9 us -> 18.1 us
    all_to_all x0 -> x1, blocking collectives: none -> 20.8 us  [swap_tiles(): return lax.all_to_all(x, axis, split_axis=0, concat_axis=0, tiled=True)]
    all_to_all x3 -> x2, starting transfers between devices: 23.8 us -> 13 us  [swap_tiles(): return lax.all_to_all(x, axis, split_axis=0, concat_axis=0, tiled=True)]
    all_to_all x3 -> x2, waiting for transfers between devices: 19.3 us -> 12.7 us  [swap_tiles(): return lax.all_to_all(x, axis, split_axis=0, concat_axis=0, tiled=True)]
    ppermute x16, waiting for transfers between devices: 7.65 us -> 5.46 us  [exchange(): lax.ppermute(b, axis, swaps(axis, first))]
    ppermute x16, starting transfers between devices: 32.1 us -> 31 us  [exchange(): lax.ppermute(b, axis, swaps(axis, first))]
    pallas_call x9 -> x10, Pallas kernels: 23.9 us -> 23.2 us  [call(): pl.pallas_call(kernel, out_shape=outs, in_specs=[pl.BlockSpec(memory_spac...]
  transfers between devices with their start and end apart: 19 -> 18, of which waited for: 7 -> 5; matrix products, arithmetic and copies ran while one was open for 0% -> 0% of each run, Pallas kernels for 3% -> 3%
where the time goes in v3:
time: 108 us; the launch traced here: 107 us
  starting transfers between devices  43.9 us (41%)
  Pallas kernels  23.2 us (21%)
  blocking collectives  20.8 us (19%)
  waiting for transfers between devices  18.1 us (17%)
    ppermute x16, starting transfers between devices, exchange(): lax.ppermute(b, axis, swaps(axis, first))  31 us
    pallas_call x10, Pallas kernels, call(): pl.pallas_call(kernel, out_shape=outs, in_specs=[pl.BlockSpec(memory_spac...  23.2 us
    all_to_all x1, blocking collectives, swap_tiles(): return lax.all_to_all(x, axis, split_axis=0, concat_axis=0, tiled=True)  20.8 us
    all_to_all x2, starting transfers between devices, swap_tiles(): return lax.all_to_all(x, axis, split_axis=0, concat_axis=0, tiled=True)  13 us
    all_to_all x2, waiting for transfers between devices, swap_tiles(): return lax.all_to_all(x, axis, split_axis=0, concat_axis=0, tiled=True)  12.7 us
    ppermute x16, waiting for transfers between devices, exchange(): lax.ppermute(b, axis, swaps(axis, first))  5.46 us
  transfers between devices with their start and end apart: 18, of which 5 were waited for; matrix products, arithmetic and copies ran while one was open for 0% of the time, Pallas kernels for 3%

profile of v3, /device:TPU:1, one launch (start us, length us, event | category | flops | bytes accessed | tf_op | source)
XLA Modules:
  0.0 106.9 jit_solution(8277243930301985371)
XLA Ops:
  0.6 1.3 %sends.1 = (bf16[128,128]{1,0:T(8,128)(2,1)S(1)}, bf16[128,128]{1,0:T(8,128)(2,1)S(1)}, bf16[128,128]{1,0:T(8,128)(2,1)S(1)}, bf16[128,128]{1,0:T(8,128)(2,1)S(1...) custom-call(s32[4,128]{1,0:T(4,128)} %bitcast.18, bf16[256,128]{1,0:T(8,128)(2,1)} %bitcast.15), custom_call_target="tpu_custom_call" | custom-call | tf_op jit(solution)/shard_map/sends/pallas_call | solution.py:302
  1.9 4.6 %collective-permute-start.1 = (bf16[128,128]{1,0:T(8,128)(2,1)S(1)}, bf16[128,128]{1,0:T(8,128)(2,1)S(1)}, u32[]{:S(2)}, u32[]{:S(2)}) collective-permute-start(bf16[128,128]{1,0:T(8,128)(2,1)S(1)} %get-tuple-element.71), channel_id=1, source_target_pairs={{8,16},{16,8},{24,32},{32,24},{40,48},{48,40},{56,64},{64,56},{72,... | collective-permute-start | bytes 98312 | tf_op jit(solution)/shard_map/ppermute | solution.py:320
  6.5 1.7 %collective-permute-start.2 = (bf16[128,128]{1,0:T(8,128)(2,1)S(1)}, bf16[128,128]{1,0:T(8,128)(2,1)S(1)}, u32[]{:S(2)}, u32[]{:S(2)}) collective-permute-start(bf16[128,128]{1,0:T(8,128)(2,1)S(1)} %get-tuple-element.72), channel_id=1, source_target_pairs={{0,1},{1,0},{2,3},{3,2},{4,5},{5,4},{6,7},{7,6},{8,9},{9,8},{10,11... | collective-permute-start | bytes 98312 | tf_op jit(solution)/shard_map/ppermute | solution.py:320
  8.2 0.7 collective-permute-start.3
  9.0 1.3 %load.1 = (s32[3,1,512]{2,1,0:T(1,128)S(1)}, s32[3,1,512]{2,1,0:T(1,128)S(1)}, bf16[1536,128]{1,0:T(8,128)(2,1)S(1)}, bf16[256,128]{1,0:T(8,128)(2,1)S(1)}, bf16...) custom-call(s32[1,4]{1,0:T(1,128)} %cnt_hbm.1, ...), custom_call_target="tpu_custom_call" | custom-call | tf_op jit(solution)/shard_map/load/pallas_call | solution.py:302
  10.4 4.7 %layer0.1 = (bf16[1536,384]{1,0:T(8,128)(2,1)S(1)}, bf16[1536,128]{1,0:T(8,128)(2,1)S(1)}, f32[1536,128]{1,0:T(8,128)S(1)}, f32[1536,128]{1,0:T(8,128)S(1)}, f32...) custom-call(s32[3,1,512]{2,1,0:T(1,128)S(1)} %get-tuple-element.67.s, ...), custom_call_target="tpu_custom_call" | custom-call | tf_op jit(solution)/shard_map/layer0/pallas_call | solution.py:302
  15.7 3.1 %collective-permute-start.5 = (bf16[128,128]{1,0:T(8,128)(2,1)S(1)}, bf16[128,128]{1,0:T(8,128)(2,1)S(1)}, u32[]{:S(2)}, u32[]{:S(2)}) collective-permute-start(bf16[128,128]{1,0:T(8,128)(2,1)S(1)} %get-tuple-element.83), channel_id=1, source_target_pairs={{8,16},{16,8},{24,32},{32,24},{40,48},{48,40},{56,64},{64,56},{72,... | collective-permute-start | bytes 98312 | tf_op jit(solution)/shard_map/ppermute | solution.py:320
  18.8 4.6 %collective-permute-start.6 = (bf16[128,128]{1,0:T(8,128)(2,1)S(1)}, bf16[128,128]{1,0:T(8,128)(2,1)S(1)}, u32[]{:S(2)}, u32[]{:S(2)}) collective-permute-start(bf16[128,128]{1,0:T(8,128)(2,1)S(1)} %get-tuple-element.84), channel_id=1, source_target_pairs={{0,1},{1,0},{2,3},{3,2},{4,5},{5,4},{6,7},{7,6},{8,9},{9,8},{10,11... | collective-permute-start | bytes 98312 | tf_op jit(solution)/shard_map/ppermute | solution.py:320
  23.4 0.8 collective-permute-start.7
  24.7 7.9 %layer1.1 = (bf16[256,128]{1,0:T(8,128)(2,1)}, bf16[1536,128]{1,0:T(8,128)(2,1)S(1)}, f32[256,128]{1,0:T(8,128)S(1)}, bf16[128,128]{1,0:T(8,128)(2,1)S(1)}, bf16...) custom-call(s32[3,1,512]{2,1,0:T(1,128)S(1)} %get-tuple-element.67.s, ...), custom_call_target="tpu_custom_call" | custom-call | tf_op jit(solution)/shard_map/layer1/pallas_call | solution.py:302
  32.6 3.6 %collective-permute-start.9 = (bf16[128,128]{1,0:T(8,128)(2,1)S(1)}, bf16[128,128]{1,0:T(8,128)(2,1)S(1)}, u32[]{:S(2)}, u32[]{:S(2)}) collective-permute-start(bf16[128,128]{1,0:T(8,128)(2,1)S(1)} %get-tuple-element.92), channel_id=1, source_target_pairs={{8,16},{16,8},{24,32},{32,24},{40,48},{48,40},{56,64},{64,56},{72,... | collective-permute-start | bytes 98312 | tf_op jit(solution)/shard_map/ppermute | solution.py:320
  36.2 5.8 %collective-permute-start.10 = (bf16[128,128]{1,0:T(8,128)(2,1)S(1)}, bf16[128,128]{1,0:T(8,128)(2,1)S(1)}, u32[]{:S(2)}, u32[]{:S(2)}) collective-permute-start(bf16[128,128]{1,0:T(8,128)(2,1)S(1)} %get-tuple-element.93), channel_id=1, source_target_pairs={{0,1},{1,0},{2,3},{3,2},{4,5},{5,4},{6,7},{7,6},{8,9},{9,8},{10,11... | collective-permute-start | bytes 98312 | tf_op jit(solution)/shard_map/ppermute | solution.py:320
  43.3 4.6 %back0.1 = (bf16[1536,128]{1,0:T(8,128)(2,1)}, f32[256,128]{1,0:T(8,128)S(1)}, bf16[128,128]{1,0:T(8,128)(2,1)S(1)}, bf16[128,128]{1,0:T(8,128)(2,1)S(1)}, bf16[...) custom-call(s32[3,1,512]{2,1,0:T(1,128)S(1)} %get-tuple-element.67.snd_ref, ...), custom_call_target="tpu_custom_call" | custom-call | tf_op jit(solution)/shard_map/back0/pallas_call | solution.py:302
  47.9 8.9 %all-to-all-start = ((bf16[32,64,128]{2,1,0:T(8,128)(2,1)}), bf16[32,64,128]{2,1,0:T(8,128)(2,1)S(1)}, u32[]{:S(2)}, u32[]{:S(2)}) async-start(bf16[32,64,128]{2,1,0:T(8,128)(2,1)} %bitcast.9), calls=%async_computation | async-start | bytes 1048576 | tf_op jit(solution)/shard_map/all_to_all | solution.py:337
  57.1 3.4 %collective-permute-start.13 = (bf16[128,128]{1,0:T(8,128)(2,1)S(1)}, bf16[128,128]{1,0:T(8,128)(2,1)S(1)}, u32[]{:S(2)}, u32[]{:S(2)}) collective-permute-start(bf16[128,128]{1,0:T(8,128)(2,1)S(1)} %get-tuple-element.112), channel_id=1, source_target_pairs={{8,16},{16,8},{24,32},{32,24},{40,48},{48,40},{56,64},{64,56},{72,... | collective-permute-start | bytes 98312 | tf_op jit(solution)/shard_map/ppermute | solution.py:320
  60.5 3.1 %collective-permute-done.13.t1.refs_1_ = bf16[128,128]{1,0:T(8,128)(2,1)S(1)} collective-permute-done((bf16[128,128]{1,0:T(8,128)(2,1)S(1)}, bf16[128,128]{1,0:T(8,128)(2,1)S(1)}, u32[]{:S(2)}, u32[]{:S(2)}) %collective-permute-start.13) | collective-permute-done | bytes 32800 | tf_op jit(solution)/shard_map/ppermute | solution.py:320
  63.6 4.7 %all-to-all-done.x_ref = bf16[32,64,128]{2,1,0:T(8,128)(2,1)S(1)} async-done(((bf16[32,64,128]{2,1,0:T(8,128)(2,1)}), bf16[32,64,128]{2,1,0:T(8,128)(2,1)S(1)}, u32[]{:S(2)}, u32[]{:S(2)}) %all-to-all-start) | async-done | bytes 524320 | tf_op jit(solution)/shard_map/all_to_all | solution.py:337
  68.5 20.8 %all_to_all.15.x_ref = bf16[8,64,128]{2,1,0:T(8,128)(2,1)S(1)} all-to-all(bf16[8,64,128]{2,1,0:T(8,128)(2,1)S(1)} %fold_dom.1), channel_id=1, replica_groups=mesh['dom'=32,'group'=8] {'group'}, dimensions={0} | all-to-all | bytes 262144 | tf_op jit(solution)/shard_map/all_to_all | solution.py:337
  89.3 0.9 fold_group.1
  90.2 4.1 %all-to-all-start.2 = ((bf16[32,64,128]{2,1,0:T(8,128)(2,1)}), bf16[32,64,128]{2,1,0:T(8,128)(2,1)S(1)}, u32[]{:S(2)}, u32[]{:S(2)}) async-start(bf16[32,64,128]{2,1,0:T(8,128)(2,1)} %fold_group.1), calls=%async_computation.2 | async-start | bytes 1048576 | tf_op jit(solution)/shard_map/all_to_all | solution.py:337
  95.3 1.8 %collective-permute-done.14.t2 = bf16[128,128]{1,0:T(8,128)(2,1)S(1)} collective-permute-done((bf16[128,128]{1,0:T(8,128)(2,1)S(1)}, bf16[128,128]{1,0:T(8,128)(2,1)S(1)}, u32[]{:S(2)}, u32[]{:S(2)}) %collective-permute-start.14) | collective-permute-done | bytes 32800 | tf_op jit(solution)/shard_map/ppermute | solution.py:320
  97.2 0.9 finish.1
  98.0 8.0 %all-to-all-done.2 = bf16[32,64,128]{2,1,0:T(8,128)(2,1)S(1)} async-done(((bf16[32,64,128]{2,1,0:T(8,128)(2,1)}), bf16[32,64,128]{2,1,0:T(8,128)(2,1)S(1)}, u32[]{:S(2)}, u32[]{:S(2)}) %all-to-all-start.2) | async-done | bytes 524320 | tf_op jit(solution)/shard_map/all_to_all | solution.py:337
  106.0 0.9 unpack.1
  (23 shorter events, 3.8 us)
Async XLA Ops:
  1.9 8.4 %collective-permute-start.1 = (bf16[128,128]{1,0:T(8,128)(2,1)S(1)}, bf16[128,128]{1,0:T(8,128)(2,1)S(1)}, u32[]{:S(2)}, u32[]{:S(2)}) collective-permute-start(bf16[128,128]{1,0:T(8,128)(2,1)S(1)} %get-tuple-element.71), channel_id=1, source_target_pairs={{8,16},{16,8},{24,32},{32,24},{40,48},{48,40},{56,64},{64,56},{72,... | collective-permute-start | bytes 98312 | tf_op jit(solution)/shard_map/ppermute | solution.py:320
  6.5 3.8 %collective-permute-start.2 = (bf16[128,128]{1,0:T(8,128)(2,1)S(1)}, bf16[128,128]{1,0:T(8,128)(2,1)S(1)}, u32[]{:S(2)}, u32[]{:S(2)}) collective-permute-start(bf16[128,128]{1,0:T(8,128)(2,1)S(1)} %get-tuple-element.72), channel_id=1, source_target_pairs={{0,1},{1,0},{2,3},{3,2},{4,5},{5,4},{6,7},{7,6},{8,9},{9,8},{10,11... | collective-permute-start | bytes 98312 | tf_op jit(solution)/shard_map/ppermute | solution.py:320
  8.2 2.1 %collective-permute-start.3 = (bf16[128,128]{1,0:T(8,128)(2,1)S(1)}, bf16[128,128]{1,0:T(8,128)(2,1)S(1)}, u32[]{:S(2)}, u32[]{:S(2)}) collective-permute-start(bf16[128,128]{1,0:T(8,128)(2,1)S(1)} %get-tuple-element.73), channel_id=1, source_target_pairs={{1,2},{2,1},{3,4},{4,3},{5,6},{6,5},{9,10},{10,9},{11,12},{12,11},... | collective-permute-start | bytes 98312 | tf_op jit(solution)/shard_map/ppermute | solution.py:320
  8.9 1.5 %collective-permute-start = (bf16[128,128]{1,0:T(8,128)(2,1)S(1)}, bf16[128,128]{1,0:T(8,128)(2,1)S(1)}, u32[]{:S(2)}, u32[]{:S(2)}) collective-permute-start(bf16[128,128]{1,0:T(8,128)(2,1)S(1)} %get-tuple-element.66.token), channel_id=1, source_target_pairs={{0,8},{8,0},{16,24},{24,16},{32,40},{40,32},{48,56},{56,48},{64,72... | collective-permute-start | bytes 98312 | tf_op jit(solution)/shard_map/ppermute | solution.py:320
  15.1 9.1 %collective-permute-start.4 = (bf16[128,128]{1,0:T(8,128)(2,1)S(1)}, bf16[128,128]{1,0:T(8,128)(2,1)S(1)}, u32[]{:S(2)}, u32[]{:S(2)}) collective-permute-start(bf16[128,128]{1,0:T(8,128)(2,1)S(1)} %get-tuple-element.82), channel_id=1, source_target_pairs={{0,8},{8,0},{16,24},{24,16},{32,40},{40,32},{48,56},{56,48},{64,72... | collective-permute-start | bytes 98312 | tf_op jit(solution)/shard_map/ppermute | solution.py:320
  15.7 8.6 %collective-permute-start.5 = (bf16[128,128]{1,0:T(8,128)(2,1)S(1)}, bf16[128,128]{1,0:T(8,128)(2,1)S(1)}, u32[]{:S(2)}, u32[]{:S(2)}) collective-permute-start(bf16[128,128]{1,0:T(8,128)(2,1)S(1)} %get-tuple-element.83), channel_id=1, source_target_pairs={{8,16},{16,8},{24,32},{32,24},{40,48},{48,40},{56,64},{64,56},{72,... | collective-permute-start | bytes 98312 | tf_op jit(solution)/shard_map/ppermute | solution.py:320
  18.8 5.9 %collective-permute-start.6 = (bf16[128,128]{1,0:T(8,128)(2,1)S(1)}, bf16[128,128]{1,0:T(8,128)(2,1)S(1)}, u32[]{:S(2)}, u32[]{:S(2)}) collective-permute-start(bf16[128,128]{1,0:T(8,128)(2,1)S(1)} %get-tuple-element.84), channel_id=1, source_target_pairs={{0,1},{1,0},{2,3},{3,2},{4,5},{5,4},{6,7},{7,6},{8,9},{9,8},{10,11... | collective-permute-start | bytes 98312 | tf_op jit(solution)/shard_map/ppermute | solution.py:320
  23.4 1.3 %collective-permute-start.7 = (bf16[128,128]{1,0:T(8,128)(2,1)S(1)}, bf16[128,128]{1,0:T(8,128)(2,1)S(1)}, u32[]{:S(2)}, u32[]{:S(2)}) collective-permute-start(bf16[128,128]{1,0:T(8,128)(2,1)S(1)} %get-tuple-element.85), channel_id=1, source_target_pairs={{1,2},{2,1},{3,4},{4,3},{5,6},{6,5},{9,10},{10,9},{11,12},{12,11},... | collective-permute-start | bytes 98312 | tf_op jit(solution)/shard_map/ppermute | solution.py:320
  32.6 10.7 %collective-permute-start.8 = (bf16[128,128]{1,0:T(8,128)(2,1)S(1)}, bf16[128,128]{1,0:T(8,128)(2,1)S(1)}, u32[]{:S(2)}, u32[]{:S(2)}) collective-permute-start(bf16[128,128]{1,0:T(8,128)(2,1)S(1)} %get-tuple-element.91), channel_id=1, source_target_pairs={{0,8},{8,0},{16,24},{24,16},{32,40},{40,32},{48,56},{56,48},{64,72... | collective-permute-start | bytes 98312 | tf_op jit(solution)/shard_map/ppermute | solution.py:320
  32.6 10.7 %collective-permute-start.9 = (bf16[128,128]{1,0:T(8,128)(2,1)S(1)}, bf16[128,128]{1,0:T(8,128)(2,1)S(1)}, u32[]{:S(2)}, u32[]{:S(2)}) collective-permute-start(bf16[128,128]{1,0:T(8,128)(2,1)S(1)} %get-tuple-element.92), channel_id=1, source_target_pairs={{8,16},{16,8},{24,32},{32,24},{40,48},{48,40},{56,64},{64,56},{72,... | collective-permute-start | bytes 98312 | tf_op jit(solution)/shard_map/ppermute | solution.py:320
  36.2 7.1 %collective-permute-start.10 = (bf16[128,128]{1,0:T(8,128)(2,1)S(1)}, bf16[128,128]{1,0:T(8,128)(2,1)S(1)}, u32[]{:S(2)}, u32[]{:S(2)}) collective-permute-start(bf16[128,128]{1,0:T(8,128)(2,1)S(1)} %get-tuple-element.93), channel_id=1, source_target_pairs={{0,1},{1,0},{2,3},{3,2},{4,5},{5,4},{6,7},{7,6},{8,9},{9,8},{10,11... | collective-permute-start | bytes 98312 | tf_op jit(solution)/shard_map/ppermute | solution.py:320
  42.0 1.3 %collective-permute-start.11 = (bf16[128,128]{1,0:T(8,128)(2,1)S(1)}, bf16[128,128]{1,0:T(8,128)(2,1)S(1)}, u32[]{:S(2)}, u32[]{:S(2)}) collective-permute-start(bf16[128,128]{1,0:T(8,128)(2,1)S(1)} %get-tuple-element.94), channel_id=1, source_target_pairs={{1,2},{2,1},{3,4},{4,3},{5,6},{6,5},{9,10},{10,9},{11,12},{12,11},... | collective-permute-start | bytes 98312 | tf_op jit(solution)/shard_map/ppermute | solution.py:320
  47.9 20.5 %all-to-all-start = ((bf16[32,64,128]{2,1,0:T(8,128)(2,1)}), bf16[32,64,128]{2,1,0:T(8,128)(2,1)S(1)}, u32[]{:S(2)}, u32[]{:S(2)}) async-start(bf16[32,64,128]{2,1,0:T(8,128)(2,1)} %bitcast.9), calls=%async_computation | async-start | bytes 1048576 | tf_op jit(solution)/shard_map/all_to_all | solution.py:337
  56.8 3.7 %collective-permute-start.12 = (bf16[128,128]{1,0:T(8,128)(2,1)S(1)}, bf16[128,128]{1,0:T(8,128)(2,1)S(1)}, u32[]{:S(2)}, u32[]{:S(2)}) collective-permute-start(bf16[128,128]{1,0:T(8,128)(2,1)S(1)} %get-tuple-element.111), channel_id=1, source_target_pairs={{0,8},{8,0},{16,24},{24,16},{32,40},{40,32},{48,56},{56,48},{64,72... | collective-permute-start | bytes 98312 | tf_op jit(solution)/shard_map/ppermute | solution.py:320
  57.1 6.5 %collective-permute-start.13 = (bf16[128,128]{1,0:T(8,128)(2,1)S(1)}, bf16[128,128]{1,0:T(8,128)(2,1)S(1)}, u32[]{:S(2)}, u32[]{:S(2)}) collective-permute-start(bf16[128,128]{1,0:T(8,128)(2,1)S(1)} %get-tuple-element.112), channel_id=1, source_target_pairs={{8,16},{16,8},{24,32},{32,24},{40,48},{48,40},{56,64},{64,56},{72,... | collective-permute-start | bytes 98312 | tf_op jit(solution)/shard_map/ppermute | solution.py:320
  90.2 15.8 %all-to-all-start.2 = ((bf16[32,64,128]{2,1,0:T(8,128)(2,1)}), bf16[32,64,128]{2,1,0:T(8,128)(2,1)S(1)}, u32[]{:S(2)}, u32[]{:S(2)}) async-start(bf16[32,64,128]{2,1,0:T(8,128)(2,1)} %fold_group.1), calls=%async_computation.2 | async-start | bytes 1048576 | tf_op jit(solution)/shard_map/all_to_all | solution.py:337
  94.3 2.9 %collective-permute-start.14 = (bf16[128,128]{1,0:T(8,128)(2,1)S(1)}, bf16[128,128]{1,0:T(8,128)(2,1)S(1)}, u32[]{:S(2)}, u32[]{:S(2)}) collective-permute-start(bf16[128,128]{1,0:T(8,128)(2,1)S(1)} %get-tuple-element.113), channel_id=1, source_target_pairs={{0,1},{1,0},{2,3},{3,2},{4,5},{5,4},{6,7},{7,6},{8,9},{9,8},{10,11... | collective-permute-start | bytes 98312 | tf_op jit(solution)/shard_map/ppermute | solution.py:320
  94.6 2.5 %collective-permute-start.15 = (bf16[128,128]{1,0:T(8,128)(2,1)S(1)}, bf16[128,128]{1,0:T(8,128)(2,1)S(1)}, u32[]{:S(2)}, u32[]{:S(2)}) collective-permute-start(bf16[128,128]{1,0:T(8,128)(2,1)S(1)} %get-tuple-element.114), channel_id=1, source_target_pairs={{1,2},{2,1},{3,4},{4,3},{5,6},{6,5},{9,10},{10,9},{11,12},{12,11},... | collective-permute-start | bytes 98312 | tf_op jit(solution)/shard_map/ppermute | solution.py:320

commit v4 on v3

--- a/solution.py
+++ b/solution.py
@@ -8,7 +8,7 @@
 from jax.sharding import PartitionSpec as P
 
 H = 128
-BLOCK = 512
+BLOCK = 768
 GRAD_ROWS = 1024
 VMEM_LIMIT = 28 << 20
 CUTS = ((0, 384), (384, 512), (512, 768), (768, 896), (896, 900), (900, 902))
@@ -135,18 +135,15 @@
 
 
 def edge_forward(snd_ref, rcv_ref, table, e_ref, w1, w2, b_ref, g_ref, joined, hidden, slope, xhat, scale, e_new, agg):
-    agg[...] = jnp.zeros((256, H), F32)
-
-    def step(i, carry):
-        rows = pl.ds(pl.multiple_of(i * BLOCK, BLOCK), BLOCK)
-        ids = snd_ref[i]
-        sent = mm(pick_rows(ids, 768), table[...]).astype(BF16)
-        recv = mm(pick_rows(rcv_ref[i], 256), table[0:256, :]).astype(BF16)
+    def gather(i):
+        rows = pl.ds(i * BLOCK, BLOCK)
         joined[rows, 0:128] = e_ref[rows, :]
-        joined[rows, 128:256] = sent
-        joined[rows, 256:384] = recv
-        pre = mm(joined[rows, :], w1[...]) + b_ref[0:1, :]
-        act, slo = silu_parts(pre)
+        joined[rows, 128:256] = mm(pick_rows(snd_ref[i], 768), table[...]).astype(BF16)
+        joined[rows, 256:384] = mm(pick_rows(rcv_ref[i], 256), table[0:256, :]).astype(BF16)
+
+    def update(i):
+        rows = pl.ds(i * BLOCK, BLOCK)
+        act, slo = silu_parts(mm(joined[rows, :], w1[...]) + b_ref[0:1, :])
         act = act.astype(BF16)
         hidden[rows, :] = act
         slope[rows, :] = slo
@@ -156,10 +153,16 @@
         new = (e_ref[rows, :].astype(F32) + xh * g_ref[0:1, :]).astype(BF16)
         if e_new is not None:
             e_new[rows, :] = new
-        agg[...] += mm(spread_rows(rcv_ref[i], 256), new)
-        return carry
-
-    lax.fori_loop(0, e_ref.shape[0] // BLOCK, step, 0, unroll=True)
+        return mm(spread_rows(rcv_ref[i], 256), new)
+
+    blocks = e_ref.shape[0] // BLOCK
+    gather(0)
+    out = 0.0
+    for i in range(blocks):
+        if i + 1 < blocks:
+            gather(i + 1)
+        out = out + update(i)
+    agg[...] = out
 
 
 def node_forward(x, agg, wn1, wn2, b_ref, g_ref):
@@ -266,12 +269,11 @@
 
 
 def back_kernel(
-    snd_ref, rcv_ref, send_ref, x_ref, agg_b, own_ref, t0, t1, t2, t3, joined, hidden, slope, xhat, scale, e_cot, late,
+    snd_ref, rcv_ref, send_ref, x_ref, agg_b, own_ref, t0, t1, t2, t3, joined, hidden, slope, xhat, scale, e_cot,
     w1, w2, wn1, wn2, b_ref, g_ref,
     e_grad, x_grad, c0, c1, c2, c3, grads, acc, dpres, backs, sums,
 ):
     w1, w2, wn1, wn2, b_ref, g_ref = (r.at[0] for r in (w1, w2, wn1, wn2, b_ref, g_ref))
-    grads[GRAD_ROWS:, :] = late[...]
     cot = (own_ref[...] + add_returns(send_ref, (t0, t1, t2, t3))).astype(BF16)
     new, saved = node_forward(x_ref[...], agg_b[...], wn1, wn2, b_ref, g_ref)
     dx, dagg, node_ops, small = node_backward(cot, saved, wn1, wn2, g_ref)
@@ -327,25 +329,45 @@
         o_ref[k] = out
 
 
-def unpack_kernel(scale, x_ref, *outs):
+def join_kernel(own0, own1, got1, got0, o_ref):
+    core = lax.axis_index("dom") % 2
+
+    @pl.when(core == 0)
+    def _():
+        o_ref[...] = (own0[...].astype(F32) + got0[...].astype(F32)).astype(BF16)
+
+    @pl.when(core == 1)
+    def _():
+        o_ref[...] = (own1[...].astype(F32) + got1[...].astype(F32)).astype(BF16)
+
+
+def unpack_kernel(scale, mine, other, *outs):
+    core = lax.axis_index("dom") % 2
     for out, (a, b) in zip(outs, CUTS):
-        for l in range(2):
-            out[l] = x_ref[GRAD_ROWS * l + a : GRAD_ROWS * l + b, :].astype(F32) * scale
-
-
-def swap_tiles(x, axis):
-    return lax.all_to_all(x, axis, split_axis=0, concat_axis=0, tiled=True)
-
-
-def reduce_grads(packed, scale, first, second):
+        out[core] = mine[a:b, :].astype(F32) * scale
+        out[1 - core] = other[a:b, :].astype(F32) * scale
+
+
+def on_chip(core):
+    return [(i + core, i + 1 - core) for i in range(0, lax.axis_size("dom"), 2)]
+
+
+def swap_tiles(x):
     dom, group = lax.axis_size("dom"), lax.axis_size("group")
-    rows = packed.shape[0] // dom
-    tiles = swap_tiles(packed.reshape(dom, rows, H), "dom")
-    (tiles,) = call(fold_kernel, [shape(group, rows, H, dtype=BF16)], [], (tiles, *first), "fold_dom")
-    tiles = swap_tiles(tiles, "group")
-    (tiles,) = call(fold_kernel, [shape(dom, rows, H, dtype=BF16)], [], (tiles, *second), "fold_group")
-    whole = swap_tiles(tiles, "dom").reshape(dom * rows, H)
-    return call(partial(unpack_kernel, scale), [shape(2, b - a, H) for a, b in CUTS], [], (whole,), "unpack")
+    sets = [[d * group + g for d in range(c, dom, 2) for g in range(group)] for c in range(2)]
+    return lax.all_to_all(x, ("dom", "group"), split_axis=0, concat_axis=0, axis_index_groups=sets, tiled=True)
+
+
+def reduce_grads(grads0, grads1, early, scale, first, second):
+    late = lax.ppermute(grads0, "dom", on_chip(1))
+    (joined,) = call(join_kernel, [shape(GRAD_ROWS, H, dtype=BF16)], [], (grads0, grads1, early, late), "join")
+    count = lax.axis_size("dom") * lax.axis_size("group") // 2
+    tiles = swap_tiles(joined.reshape(count, -1, H))
+    (tiles,) = call(fold_kernel, [shape(*tiles.shape, dtype=BF16)], [], (tiles, *first), "fold")
+    mine, _ = lax.optimization_barrier((swap_tiles(tiles), second))
+    mine = mine.reshape(GRAD_ROWS, H)
+    other = lax.ppermute(mine, "dom", swaps("dom", 0))
+    return call(partial(unpack_kernel, scale), [shape(2, b - a, H) for a, b in CUTS], [], (mine, other), "unpack")
 
 
 def shards(nodes, edges, node_cot, send_index, halo_count, senders, receivers, edge_in_w, edge_out_w, node_in_w, node_out_w, biases, gains):
@@ -409,20 +431,21 @@
     nodes_out, e_cot, own = out[:3]
     back = exchange(out[3:7])
     (grads1,) = call(grads_kernel, [shape(GRAD_ROWS, H, dtype=BF16)], [], out[7:], "wgrad1")
+    early = lax.ppermute(grads1, "dom", on_chip(0))
     out = call(
         back_kernel,
-        [shape(n_edge, H, dtype=BF16), shape(256, H)] + rows4 + [shape(2 * GRAD_ROWS, H, dtype=BF16)],
+        [shape(n_edge, H, dtype=BF16), shape(256, H)] + rows4 + [shape(GRAD_ROWS, H, dtype=BF16)],
         [shape(768, H), low, low, shape(8, H)],
-        (snd, rcv, send, x0, agg0, own, *back, *saved, e_cot, grads1, *weights),
+        (snd, rcv, send, x0, agg0, own, *back, *saved, e_cot, *weights),
         "back0",
     )
     edge_grad, own = out[:2]
-    packed = out[6]
+    grads0 = out[6]
     back = exchange(out[2:6])
     (node_grad,) = call(finish_kernel, [shape(256, H, dtype=BF16)], [], (send, own, *back), "finish")
 
     scale = (lax.axis_size("dom") * lax.axis_size("group") * x0.shape[0]) ** (-0.5)
-    grads = reduce_grads(packed, scale, back[:2], ())
+    grads = reduce_grads(grads0, grads1, early, scale, back[:2], back[2:])
     return (nodes_out[None], node_grad[None], edge_grad[None], *grads)
 
 

time: 108 us -> 110 us (1.019)
  blocking collectives: 20.8 us -> 0 us
  starting transfers between devices: 43.9 us -> 62.7 us
  waiting for transfers between devices: 18.1 us -> 25.6 us
  Pallas kernels: 23.2 us -> 20.6 us
    all_to_all x1 -> x0, blocking collectives: 20.8 us -> none  [swap_tiles(): return lax.all_to_all(x, axis, split_axis=0, concat_axis=0, tiled=True)]
    all_to_all x2, starting transfers between devices: 13 us -> 25.2 us  [swap_tiles(): lax.all_to_all(x, ('dom', 'group'), split_axis=0, concat_axis=0, axis_ind...]
    ppermute x0 -> x3, starting transfers between devices: none -> 6.69 us  [the longest x1 3.05 us: reduce_grads(): late = lax.ppermute(grads0, 'dom', on_chip(1))]
    ppermute x16, waiting for transfers between devices: 5.46 us -> 8.67 us  [exchange(): lax.ppermute(b, axis, swaps(axis, first))]
    all_to_all x2, waiting for transfers between devices: 12.7 us -> 15.5 us  [swap_tiles(): lax.all_to_all(x, ('dom', 'group'), split_axis=0, concat_axis=0, axis_ind...]
    pallas_call x10, Pallas kernels: 23.2 us -> 20.6 us  [call(): pl.pallas_call(kernel, out_shape=outs, in_specs=[pl.BlockSpec(memory_spac...]
    ppermute x0 -> x3, waiting for transfers between devices: none -> 1.41 us  [the longest x1 1.12 us: reduce_grads(): late = lax.ppermute(grads0, 'dom', on_chip(1))]
  transfers between devices with their start and end apart: 18 -> 21, of which waited for: 5 -> 8; matrix products, arithmetic and copies ran while one was open for 0% -> 0% of each run, Pallas kernels for 3% -> 6%
where the time goes in v4:
time: 110 us
  starting transfers between devices  62.7 us (57%)
  waiting for transfers between devices  25.6 us (23%)
  Pallas kernels  20.6 us (19%)
    ppermute x16, starting transfers between devices, exchange(): lax.ppermute(b, axis, swaps(axis, first))  30.8 us
    all_to_all x2, starting transfers between devices, swap_tiles(): lax.all_to_all(x, ('dom', 'group'), split_axis=0, concat_axis=0, axis_ind...  25.2 us
    pallas_call x10, Pallas kernels, call(): pl.pallas_call(kernel, out_shape=outs, in_specs=[pl.BlockSpec(memory_spac...  20.6 us
    all_to_all x2, waiting for transfers between devices, swap_tiles(): lax.all_to_all(x, ('dom', 'group'), split_axis=0, concat_axis=0, axis_ind...  15.5 us
    ppermute x16, waiting for transfers between devices, exchange(): lax.ppermute(b, axis, swaps(axis, first))  8.67 us
    ppermute x1, starting transfers between devices, reduce_grads(): late = lax.ppermute(grads0, 'dom', on_chip(1))  3.05 us
    ppermute x1, starting transfers between devices, reduce_grads(): other = lax.ppermute(mine, 'dom', swaps('dom', 0))  2.35 us
  transfers between devices with their start and end apart: 21, of which 8 were waited for; matrix products, arithmetic and copies ran while one was open for 0% of the time, Pallas kernels for 6%

profile of v4, /device:TPU:1, one launch (start us, length us, event | category | flops | bytes accessed | tf_op | source)
XLA Modules:
  0.0 109.7 jit_solution(14810816574396274348)
XLA Ops:
  0.6 1.3 %sends.1 = (bf16[128,128]{1,0:T(8,128)(2,1)S(1)}, bf16[128,128]{1,0:T(8,128)(2,1)S(1)}, bf16[128,128]{1,0:T(8,128)(2,1)S(1)}, bf16[128,128]{1,0:T(8,128)(2,1)S(1...) custom-call(s32[4,128]{1,0:T(4,128)} %bitcast.19, bf16[256,128]{1,0:T(8,128)(2,1)} %bitcast.16), custom_call_target="tpu_custom_call" | custom-call | tf_op jit(solution)/shard_map/sends/pallas_call | solution.py:304
  1.9 3.3 %collective-permute-start = (bf16[128,128]{1,0:T(8,128)(2,1)S(1)}, bf16[128,128]{1,0:T(8,128)(2,1)S(1)}, u32[]{:S(2)}, u32[]{:S(2)}) collective-permute-start(bf16[128,128]{1,0:T(8,128)(2,1)S(1)} %get-tuple-element.67.token), channel_id=1, source_target_pairs={{0,8},{8,0},{16,24},{24,16},{32,40},{40,32},{48,56},{56,48},{64,72... | collective-permute-start | bytes 98312 | tf_op jit(solution)/shard_map/ppermute | solution.py:322
  5.2 1.9 %collective-permute-start.1 = (bf16[128,128]{1,0:T(8,128)(2,1)S(1)}, bf16[128,128]{1,0:T(8,128)(2,1)S(1)}, u32[]{:S(2)}, u32[]{:S(2)}) collective-permute-start(bf16[128,128]{1,0:T(8,128)(2,1)S(1)} %get-tuple-element.72), channel_id=1, source_target_pairs={{8,16},{16,8},{24,32},{32,24},{40,48},{48,40},{56,64},{64,56},{72,... | collective-permute-start | bytes 98312 | tf_op jit(solution)/shard_map/ppermute | solution.py:322
  7.1 1.2 %collective-permute-start.2 = (bf16[128,128]{1,0:T(8,128)(2,1)S(1)}, bf16[128,128]{1,0:T(8,128)(2,1)S(1)}, u32[]{:S(2)}, u32[]{:S(2)}) collective-permute-start(bf16[128,128]{1,0:T(8,128)(2,1)S(1)} %get-tuple-element.73), channel_id=1, source_target_pairs={{0,1},{1,0},{2,3},{3,2},{4,5},{5,4},{6,7},{7,6},{8,9},{9,8},{10,11... | collective-permute-start | bytes 98312 | tf_op jit(solution)/shard_map/ppermute | solution.py:322
  9.0 1.3 %load.1 = (s32[2,1,768]{2,1,0:T(1,128)S(1)}, s32[2,1,768]{2,1,0:T(1,128)S(1)}, bf16[1536,128]{1,0:T(8,128)(2,1)S(1)}, bf16[256,128]{1,0:T(8,128)(2,1)S(1)}, bf16...) custom-call(s32[1,4]{1,0:T(1,128)} %cnt_hbm.1, ...), custom_call_target="tpu_custom_call" | custom-call | tf_op jit(solution)/shard_map/load/pallas_call | solution.py:304
  10.4 3.5 %layer0.1 = (bf16[1536,384]{1,0:T(8,128)(2,1)S(1)}, bf16[1536,128]{1,0:T(8,128)(2,1)S(1)}, f32[1536,128]{1,0:T(8,128)S(1)}, f32[1536,128]{1,0:T(8,128)S(1)}, f32...) custom-call(s32[2,1,768]{2,1,0:T(1,128)S(1)} %get-tuple-element.68.s, ...), custom_call_target="tpu_custom_call" | custom-call | tf_op jit(solution)/shard_map/layer0/pallas_call | solution.py:304
  14.0 4.3 %collective-permute-start.5 = (bf16[128,128]{1,0:T(8,128)(2,1)S(1)}, bf16[128,128]{1,0:T(8,128)(2,1)S(1)}, u32[]{:S(2)}, u32[]{:S(2)}) collective-permute-start(bf16[128,128]{1,0:T(8,128)(2,1)S(1)} %get-tuple-element.84), channel_id=1, source_target_pairs={{8,16},{16,8},{24,32},{32,24},{40,48},{48,40},{56,64},{64,56},{72,... | collective-permute-start | bytes 98312 | tf_op jit(solution)/shard_map/ppermute | solution.py:322
  18.3 4.0 %collective-permute-start.6 = (bf16[128,128]{1,0:T(8,128)(2,1)S(1)}, bf16[128,128]{1,0:T(8,128)(2,1)S(1)}, u32[]{:S(2)}, u32[]{:S(2)}) collective-permute-start(bf16[128,128]{1,0:T(8,128)(2,1)S(1)} %get-tuple-element.85), channel_id=1, source_target_pairs={{0,1},{1,0},{2,3},{3,2},{4,5},{5,4},{6,7},{7,6},{8,9},{9,8},{10,11... | collective-permute-start | bytes 98312 | tf_op jit(solution)/shard_map/ppermute | solution.py:322
  23.6 6.4 %layer1.1 = (bf16[256,128]{1,0:T(8,128)(2,1)}, bf16[1536,128]{1,0:T(8,128)(2,1)S(1)}, f32[256,128]{1,0:T(8,128)S(1)}, bf16[128,128]{1,0:T(8,128)(2,1)S(1)}, bf16...) custom-call(s32[2,1,768]{2,1,0:T(1,128)S(1)} %get-tuple-element.68.s, ...), custom_call_target="tpu_custom_call" | custom-call | tf_op jit(solution)/shard_map/layer1/pallas_call | solution.py:304
  30.0 5.5 %collective-permute-start.10 = (bf16[128,128]{1,0:T(8,128)(2,1)S(1)}, bf16[128,128]{1,0:T(8,128)(2,1)S(1)}, u32[]{:S(2)}, u32[]{:S(2)}) collective-permute-start(bf16[128,128]{1,0:T(8,128)(2,1)S(1)} %get-tuple-element.94), channel_id=1, source_target_pairs={{0,1},{1,0},{2,3},{3,2},{4,5},{5,4},{6,7},{7,6},{8,9},{9,8},{10,11... | collective-permute-start | bytes 98312 | tf_op jit(solution)/shard_map/ppermute | solution.py:322
  36.4 3.6 %collective-permute-start.9 = (bf16[128,128]{1,0:T(8,128)(2,1)S(1)}, bf16[128,128]{1,0:T(8,128)(2,1)S(1)}, u32[]{:S(2)}, u32[]{:S(2)}) collective-permute-start(bf16[128,128]{1,0:T(8,128)(2,1)S(1)} %get-tuple-element.93), channel_id=1, source_target_pairs={{8,16},{16,8},{24,32},{32,24},{40,48},{48,40},{56,64},{64,56},{72,... | collective-permute-start | bytes 98312 | tf_op jit(solution)/shard_map/ppermute | solution.py:322
  40.6 1.3 %collective-permute-start.16 = (bf16[1024,128]{1,0:T(8,128)(2,1)S(1)}, bf16[1024,128]{1,0:T(8,128)(2,1)S(1)}, u32[]{:S(2)}, u32[]{:S(2)}) collective-permute-start(bf16[1024,128]{1,0:T(8,128)(2,1)S(1)} %wgrad1.1.own1), channel_id=1, source_target_pairs={{0,8},{16,24},{32,40},{48,56},{64,72},{80,88},{96,104},{112,120},{... | collective-permute-start | bytes 786440 | tf_op jit(solution)/shard_map/ppermute | solution.py:434
  41.9 4.1 %back0.1 = (bf16[1536,128]{1,0:T(8,128)(2,1)}, f32[256,128]{1,0:T(8,128)S(1)}, bf16[128,128]{1,0:T(8,128)(2,1)S(1)}, bf16[128,128]{1,0:T(8,128)(2,1)S(1)}, bf16[...) custom-call(s32[2,1,768]{2,1,0:T(1,128)S(1)} %get-tuple-element.68.snd_ref, ...), custom_call_target="tpu_custom_call" | custom-call | tf_op jit(solution)/shard_map/back0/pallas_call | solution.py:304
  46.1 3.0 %collective-permute-start.17 = (bf16[1024,128]{1,0:T(8,128)(2,1)S(1)}, bf16[1024,128]{1,0:T(8,128)(2,1)S(1)}, u32[]{:S(2)}, u32[]{:S(2)}) collective-permute-start(bf16[1024,128]{1,0:T(8,128)(2,1)S(1)} %get-tuple-element.108.own0), channel_id=1, source_target_pairs={{8,0},{24,16},{40,32},{56,48},{72,64},{88,80},{104,96},{120,112},{... | collective-permute-start | bytes 786440 | tf_op jit(solution)/shard_map/ppermute | solution.py:362
  49.1 1.1 %collective-permute-done.17.got0 = bf16[1024,128]{1,0:T(8,128)(2,1)S(1)} collective-permute-done((bf16[1024,128]{1,0:T(8,128)(2,1)S(1)}, bf16[1024,128]{1,0:T(8,128)(2,1)S(1)}, u32[]{:S(2)}, u32[]{:S(2)}) %collective-permute-start.17) | collective-permute-done | bytes 262176 | tf_op jit(solution)/shard_map/ppermute | solution.py:362
  51.0 18.0 %all-to-all-start = ((bf16[128,8,128]{2,1,0:T(8,128)(2,1)}), bf16[128,8,128]{2,1,0:T(8,128)(2,1)S(1)}, u32[]{:S(2)}, u32[]{:S(2)}) async-start(bf16[128,8,128]{2,1,0:T(8,128)(2,1)} %bitcast.9), calls=%async_computation | async-start | bytes 524288 | tf_op jit(solution)/shard_map/all_to_all | solution.py:358
  69.7 2.7 %collective-permute-start.13 = (bf16[128,128]{1,0:T(8,128)(2,1)S(1)}, bf16[128,128]{1,0:T(8,128)(2,1)S(1)}, u32[]{:S(2)}, u32[]{:S(2)}) collective-permute-start(bf16[128,128]{1,0:T(8,128)(2,1)S(1)} %get-tuple-element.104), channel_id=1, source_target_pairs={{8,16},{16,8},{24,32},{32,24},{40,48},{48,40},{56,64},{64,56},{72,... | collective-permute-start | bytes 98312 | tf_op jit(solution)/shard_map/ppermute | solution.py:322
  72.4 3.0 %collective-permute-done.13.t1.refs_1_ = bf16[128,128]{1,0:T(8,128)(2,1)S(1)} collective-permute-done((bf16[128,128]{1,0:T(8,128)(2,1)S(1)}, bf16[128,128]{1,0:T(8,128)(2,1)S(1)}, u32[]{:S(2)}, u32[]{:S(2)}) %collective-permute-start.13) | collective-permute-done | bytes 32800 | tf_op jit(solution)/shard_map/ppermute | solution.py:322
  75.4 7.7 %all-to-all-done.x_ref = bf16[128,8,128]{2,1,0:T(8,128)(2,1)S(1)} async-done(((bf16[128,8,128]{2,1,0:T(8,128)(2,1)}), bf16[128,8,128]{2,1,0:T(8,128)(2,1)S(1)}, u32[]{:S(2)}, u32[]{:S(2)}) %all-to-all-start) | async-done | bytes 262176 | tf_op jit(solution)/shard_map/all_to_all | solution.py:358
  84.0 7.2 %all-to-all-start.1 = ((bf16[128,8,128]{2,1,0:T(8,128)(2,1)}), bf16[128,8,128]{2,1,0:T(8,128)(2,1)S(1)}, u32[]{:S(2)}, u32[]{:S(2)}) async-start(bf16[128,8,128]{2,1,0:T(8,128)(2,1)} %fold.1), calls=%async_computation.1 | async-start | bytes 524288 | tf_op jit(solution)/shard_map/all_to_all | solution.py:358
  92.6 4.9 %collective-permute-done.14.t2 = bf16[128,128]{1,0:T(8,128)(2,1)S(1)} collective-permute-done((bf16[128,128]{1,0:T(8,128)(2,1)S(1)}, bf16[128,128]{1,0:T(8,128)(2,1)S(1)}, u32[]{:S(2)}, u32[]{:S(2)}) %collective-permute-start.14) | collective-permute-done | bytes 32800 | tf_op jit(solution)/shard_map/ppermute | solution.py:322
  97.5 7.8 %all-to-all-done.1 = bf16[128,8,128]{2,1,0:T(8,128)(2,1)S(1)} async-done(((bf16[128,8,128]{2,1,0:T(8,128)(2,1)}), bf16[128,8,128]{2,1,0:T(8,128)(2,1)S(1)}, u32[]{:S(2)}, u32[]{:S(2)}) %all-to-all-start.1) | async-done | bytes 262176 | tf_op jit(solution)/shard_map/all_to_all | solution.py:358
  105.3 2.4 %collective-permute-start.18 = (bf16[1024,128]{1,0:T(8,128)(2,1)S(1)}, bf16[1024,128]{1,0:T(8,128)(2,1)S(1)}, u32[]{:S(2)}, u32[]{:S(2)}) collective-permute-start(bf16[1024,128]{1,0:T(8,128)(2,1)S(1)} %bitcast.11), channel_id=1, source_target_pairs={{0,8},{8,0},{16,24},{24,16},{32,40},{40,32},{48,56},{56,48},{64,72... | collective-permute-start | bytes 786440 | tf_op jit(solution)/shard_map/ppermute | solution.py:369
  108.8 1.0 unpack.1
  (28 shorter events, 8.5 us)
Async XLA Ops:
  1.9 8.4 %collective-permute-start = (bf16[128,128]{1,0:T(8,128)(2,1)S(1)}, bf16[128,128]{1,0:T(8,128)(2,1)S(1)}, u32[]{:S(2)}, u32[]{:S(2)}) collective-permute-start(bf16[128,128]{1,0:T(8,128)(2,1)S(1)} %get-tuple-element.67.token), channel_id=1, source_target_pairs={{0,8},{8,0},{16,24},{24,16},{32,40},{40,32},{48,56},{56,48},{64,72... | collective-permute-start | bytes 98312 | tf_op jit(solution)/shard_map/ppermute | solution.py:322
  5.2 5.2 %collective-permute-start.1 = (bf16[128,128]{1,0:T(8,128)(2,1)S(1)}, bf16[128,128]{1,0:T(8,128)(2,1)S(1)}, u32[]{:S(2)}, u32[]{:S(2)}) collective-permute-start(bf16[128,128]{1,0:T(8,128)(2,1)S(1)} %get-tuple-element.72), channel_id=1, source_target_pairs={{8,16},{16,8},{24,32},{32,24},{40,48},{48,40},{56,64},{64,56},{72,... | collective-permute-start | bytes 98312 | tf_op jit(solution)/shard_map/ppermute | solution.py:322
  7.1 3.3 %collective-permute-start.2 = (bf16[128,128]{1,0:T(8,128)(2,1)S(1)}, bf16[128,128]{1,0:T(8,128)(2,1)S(1)}, u32[]{:S(2)}, u32[]{:S(2)}) collective-permute-start(bf16[128,128]{1,0:T(8,128)(2,1)S(1)} %get-tuple-element.73), channel_id=1, source_target_pairs={{0,1},{1,0},{2,3},{3,2},{4,5},{5,4},{6,7},{7,6},{8,9},{9,8},{10,11... | collective-permute-start | bytes 98312 | tf_op jit(solution)/shard_map/ppermute | solution.py:322
  8.3 2.1 %collective-permute-start.3 = (bf16[128,128]{1,0:T(8,128)(2,1)S(1)}, bf16[128,128]{1,0:T(8,128)(2,1)S(1)}, u32[]{:S(2)}, u32[]{:S(2)}) collective-permute-start(bf16[128,128]{1,0:T(8,128)(2,1)S(1)} %get-tuple-element.74), channel_id=1, source_target_pairs={{1,2},{2,1},{3,4},{4,3},{5,6},{6,5},{9,10},{10,9},{11,12},{12,11},... | collective-permute-start | bytes 98312 | tf_op jit(solution)/shard_map/ppermute | solution.py:322
  13.9 9.1 %collective-permute-start.4 = (bf16[128,128]{1,0:T(8,128)(2,1)S(1)}, bf16[128,128]{1,0:T(8,128)(2,1)S(1)}, u32[]{:S(2)}, u32[]{:S(2)}) collective-permute-start(bf16[128,128]{1,0:T(8,128)(2,1)S(1)} %get-tuple-element.83), channel_id=1, source_target_pairs={{0,8},{8,0},{16,24},{24,16},{32,40},{40,32},{48,56},{56,48},{64,72... | collective-permute-start | bytes 98312 | tf_op jit(solution)/shard_map/ppermute | solution.py:322
  14.0 9.0 %collective-permute-start.5 = (bf16[128,128]{1,0:T(8,128)(2,1)S(1)}, bf16[128,128]{1,0:T(8,128)(2,1)S(1)}, u32[]{:S(2)}, u32[]{:S(2)}) collective-permute-start(bf16[128,128]{1,0:T(8,128)(2,1)S(1)} %get-tuple-element.84), channel_id=1, source_target_pairs={{8,16},{16,8},{24,32},{32,24},{40,48},{48,40},{56,64},{64,56},{72,... | collective-permute-start | bytes 98312 | tf_op jit(solution)/shard_map/ppermute | solution.py:322
  18.3 5.3 %collective-permute-start.6 = (bf16[128,128]{1,0:T(8,128)(2,1)S(1)}, bf16[128,128]{1,0:T(8,128)(2,1)S(1)}, u32[]{:S(2)}, u32[]{:S(2)}) collective-permute-start(bf16[128,128]{1,0:T(8,128)(2,1)S(1)} %get-tuple-element.85), channel_id=1, source_target_pairs={{0,1},{1,0},{2,3},{3,2},{4,5},{5,4},{6,7},{7,6},{8,9},{9,8},{10,11... | collective-permute-start | bytes 98312 | tf_op jit(solution)/shard_map/ppermute | solution.py:322
  22.3 1.3 %collective-permute-start.7 = (bf16[128,128]{1,0:T(8,128)(2,1)S(1)}, bf16[128,128]{1,0:T(8,128)(2,1)S(1)}, u32[]{:S(2)}, u32[]{:S(2)}) collective-permute-start(bf16[128,128]{1,0:T(8,128)(2,1)S(1)} %get-tuple-element.86), channel_id=1, source_target_pairs={{1,2},{2,1},{3,4},{4,3},{5,6},{6,5},{9,10},{10,9},{11,12},{12,11},... | collective-permute-start | bytes 98312 | tf_op jit(solution)/shard_map/ppermute | solution.py:322
  30.0 11.9 %collective-permute-start.10 = (bf16[128,128]{1,0:T(8,128)(2,1)S(1)}, bf16[128,128]{1,0:T(8,128)(2,1)S(1)}, u32[]{:S(2)}, u32[]{:S(2)}) collective-permute-start(bf16[128,128]{1,0:T(8,128)(2,1)S(1)} %get-tuple-element.94), channel_id=1, source_target_pairs={{0,1},{1,0},{2,3},{3,2},{4,5},{5,4},{6,7},{7,6},{8,9},{9,8},{10,11... | collective-permute-start | bytes 98312 | tf_op jit(solution)/shard_map/ppermute | solution.py:322
  35.5 6.4 %collective-permute-start.11 = (bf16[128,128]{1,0:T(8,128)(2,1)S(1)}, bf16[128,128]{1,0:T(8,128)(2,1)S(1)}, u32[]{:S(2)}, u32[]{:S(2)}) collective-permute-start(bf16[128,128]{1,0:T(8,128)(2,1)S(1)} %get-tuple-element.95), channel_id=1, source_target_pairs={{1,2},{2,1},{3,4},{4,3},{5,6},{6,5},{9,10},{10,9},{11,12},{12,11},... | collective-permute-start | bytes 98312 | tf_op jit(solution)/shard_map/ppermute | solution.py:322
  36.1 5.8 %collective-permute-start.8 = (bf16[128,128]{1,0:T(8,128)(2,1)S(1)}, bf16[128,128]{1,0:T(8,128)(2,1)S(1)}, u32[]{:S(2)}, u32[]{:S(2)}) collective-permute-start(bf16[128,128]{1,0:T(8,128)(2,1)S(1)} %get-tuple-element.92), channel_id=1, source_target_pairs={{0,8},{8,0},{16,24},{24,16},{32,40},{40,32},{48,56},{56,48},{64,72... | collective-permute-start | bytes 98312 | tf_op jit(solution)/shard_map/ppermute | solution.py:322
  36.4 5.5 %collective-permute-start.9 = (bf16[128,128]{1,0:T(8,128)(2,1)S(1)}, bf16[128,128]{1,0:T(8,128)(2,1)S(1)}, u32[]{:S(2)}, u32[]{:S(2)}) collective-permute-start(bf16[128,128]{1,0:T(8,128)(2,1)S(1)} %get-tuple-element.93), channel_id=1, source_target_pairs={{8,16},{16,8},{24,32},{32,24},{40,48},{48,40},{56,64},{64,56},{72,... | collective-permute-start | bytes 98312 | tf_op jit(solution)/shard_map/ppermute | solution.py:322
  40.6 8.5 %collective-permute-start.16 = (bf16[1024,128]{1,0:T(8,128)(2,1)S(1)}, bf16[1024,128]{1,0:T(8,128)(2,1)S(1)}, u32[]{:S(2)}, u32[]{:S(2)}) collective-permute-start(bf16[1024,128]{1,0:T(8,128)(2,1)S(1)} %wgrad1.1.own1), channel_id=1, source_target_pairs={{0,8},{16,24},{32,40},{48,56},{64,72},{80,88},{96,104},{112,120},{... | collective-permute-start | bytes 786440 | tf_op jit(solution)/shard_map/ppermute | solution.py:434
  46.1 4.2 %collective-permute-start.17 = (bf16[1024,128]{1,0:T(8,128)(2,1)S(1)}, bf16[1024,128]{1,0:T(8,128)(2,1)S(1)}, u32[]{:S(2)}, u32[]{:S(2)}) collective-permute-start(bf16[1024,128]{1,0:T(8,128)(2,1)S(1)} %get-tuple-element.108.own0), channel_id=1, source_target_pairs={{8,0},{24,16},{40,32},{56,48},{72,64},{88,80},{104,96},{120,112},{... | collective-permute-start | bytes 786440 | tf_op jit(solution)/shard_map/ppermute | solution.py:362
  51.0 32.1 %all-to-all-start = ((bf16[128,8,128]{2,1,0:T(8,128)(2,1)}), bf16[128,8,128]{2,1,0:T(8,128)(2,1)S(1)}, u32[]{:S(2)}, u32[]{:S(2)}) async-start(bf16[128,8,128]{2,1,0:T(8,128)(2,1)} %bitcast.9), calls=%async_computation | async-start | bytes 524288 | tf_op jit(solution)/shard_map/all_to_all | solution.py:358
  69.0 3.4 %collective-permute-start.12 = (bf16[128,128]{1,0:T(8,128)(2,1)S(1)}, bf16[128,128]{1,0:T(8,128)(2,1)S(1)}, u32[]{:S(2)}, u32[]{:S(2)}) collective-permute-start(bf16[128,128]{1,0:T(8,128)(2,1)S(1)} %get-tuple-element.103), channel_id=1, source_target_pairs={{0,8},{8,0},{16,24},{24,16},{32,40},{40,32},{48,56},{56,48},{64,72... | collective-permute-start | bytes 98312 | tf_op jit(solution)/shard_map/ppermute | solution.py:322
  69.7 5.7 %collective-permute-start.13 = (bf16[128,128]{1,0:T(8,128)(2,1)S(1)}, bf16[128,128]{1,0:T(8,128)(2,1)S(1)}, u32[]{:S(2)}, u32[]{:S(2)}) collective-permute-start(bf16[128,128]{1,0:T(8,128)(2,1)S(1)} %get-tuple-element.104), channel_id=1, source_target_pairs={{8,16},{16,8},{24,32},{32,24},{40,48},{48,40},{56,64},{64,56},{72,... | collective-permute-start | bytes 98312 | tf_op jit(solution)/shard_map/ppermute | solution.py:322
  84.0 21.2 %all-to-all-start.1 = ((bf16[128,8,128]{2,1,0:T(8,128)(2,1)}), bf16[128,8,128]{2,1,0:T(8,128)(2,1)S(1)}, u32[]{:S(2)}, u32[]{:S(2)}) async-start(bf16[128,8,128]{2,1,0:T(8,128)(2,1)} %fold.1), calls=%async_computation.1 | async-start | bytes 524288 | tf_op jit(solution)/shard_map/all_to_all | solution.py:358
  91.2 6.2 %collective-permute-start.14 = (bf16[128,128]{1,0:T(8,128)(2,1)S(1)}, bf16[128,128]{1,0:T(8,128)(2,1)S(1)}, u32[]{:S(2)}, u32[]{:S(2)}) collective-permute-start(bf16[128,128]{1,0:T(8,128)(2,1)S(1)} %get-tuple-element.105), channel_id=1, source_target_pairs={{0,1},{1,0},{2,3},{3,2},{4,5},{5,4},{6,7},{7,6},{8,9},{9,8},{10,11... | collective-permute-start | bytes 98312 | tf_op jit(solution)/shard_map/ppermute | solution.py:322
  91.9 5.6 %collective-permute-start.15 = (bf16[128,128]{1,0:T(8,128)(2,1)S(1)}, bf16[128,128]{1,0:T(8,128)(2,1)S(1)}, u32[]{:S(2)}, u32[]{:S(2)}) collective-permute-start(bf16[128,128]{1,0:T(8,128)(2,1)S(1)} %get-tuple-element.106), channel_id=1, source_target_pairs={{1,2},{2,1},{3,4},{4,3},{5,6},{6,5},{9,10},{10,9},{11,12},{12,11},... | collective-permute-start | bytes 98312 | tf_op jit(solution)/shard_map/ppermute | solution.py:322
  105.3 3.5 %collective-permute-start.18 = (bf16[1024,128]{1,0:T(8,128)(2,1)S(1)}, bf16[1024,128]{1,0:T(8,128)(2,1)S(1)}, u32[]{:S(2)}, u32[]{:S(2)}) collective-permute-start(bf16[1024,128]{1,0:T(8,128)(2,1)S(1)} %bitcast.11), channel_id=1, source_target_pairs={{0,8},{8,0},{16,24},{24,16},{32,40},{40,32},{48,56},{56,48},{64,72... | collective-permute-start | bytes 786440 | tf_op jit(solution)/shard_map/ppermute | solution.py:369

commit v5 on v3

--- a/solution.py
+++ b/solution.py
@@ -8,7 +8,7 @@
 from jax.sharding import PartitionSpec as P
 
 H = 128
-BLOCK = 512
+BLOCK = 768
 GRAD_ROWS = 1024
 VMEM_LIMIT = 28 << 20
 CUTS = ((0, 384), (384, 512), (512, 768), (768, 896), (896, 900), (900, 902))
@@ -134,32 +134,36 @@
     snd_ref[...] = slot_ids(snd_ref[...], [cnt_ref[0, k] for k in range(3)])
 
 
-def edge_forward(snd_ref, rcv_ref, table, e_ref, w1, w2, b_ref, g_ref, joined, hidden, slope, xhat, scale, e_new, agg):
-    agg[...] = jnp.zeros((256, H), F32)
-
-    def step(i, carry):
-        rows = pl.ds(pl.multiple_of(i * BLOCK, BLOCK), BLOCK)
-        ids = snd_ref[i]
-        sent = mm(pick_rows(ids, 768), table[...]).astype(BF16)
-        recv = mm(pick_rows(rcv_ref[i], 256), table[0:256, :]).astype(BF16)
-        joined[rows, 0:128] = e_ref[rows, :]
-        joined[rows, 128:256] = sent
-        joined[rows, 256:384] = recv
-        pre = mm(joined[rows, :], w1[...]) + b_ref[0:1, :]
-        act, slo = silu_parts(pre)
+def gather_own(i, snd_ref, rcv_ref, x_ref, e_ref, joined):
+    rows = pl.ds(i * BLOCK, BLOCK)
+    joined[rows, 0:128] = e_ref[rows, :]
+    joined[rows, 128:256] = mm(pick_rows(snd_ref[i], 256), x_ref[0:256, :]).astype(BF16)
+    joined[rows, 256:384] = mm(pick_rows(rcv_ref[i], 256), x_ref[0:256, :]).astype(BF16)
+
+
+def edge_forward(gather, pre_of, rcv_ref, e_ref, w2, b_ref, g_ref, hidden, slope, xhat, scale, e_new, agg):
+    def update(i):
+        rows = pl.ds(i * BLOCK, BLOCK)
+        act, slo = silu_parts(pre_of(rows))
         act = act.astype(BF16)
         hidden[rows, :] = act
         slope[rows, :] = slo
         xh, sc = norm_parts(mm(act, w2[...]) + b_ref[1:2, :])
         xhat[rows, :] = xh
         scale[rows, :] = sc
-        new = (e_ref[rows, :].astype(F32) + xh * g_ref[0:1, :]).astype(BF16)
+        new = (e_ref[rows, 0:128].astype(F32) + xh * g_ref[0:1, :]).astype(BF16)
         if e_new is not None:
             e_new[rows, :] = new
-        agg[...] += mm(spread_rows(rcv_ref[i], 256), new)
-        return carry
-
-    lax.fori_loop(0, e_ref.shape[0] // BLOCK, step, 0, unroll=True)
+        return mm(spread_rows(rcv_ref[i], 256), new)
+
+    blocks = e_ref.shape[0] // BLOCK
+    gather(0)
+    out = 0.0
+    for i in range(blocks):
+        if i + 1 < blocks:
+            gather(i + 1)
+        out = out + update(i)
+    agg[...] = out
 
 
 def node_forward(x, agg, wn1, wn2, b_ref, g_ref):
@@ -221,9 +225,24 @@
     grads[768:896, :] = mm_tn(act_n, back_n).astype(BF16)
 
 
-def grads_kernel(joined_n, dpre_n, act_n, back_n, joined, dpres, hidden, backs, tail, grads):
-    weight_grads((joined_n[...], dpre_n[...], act_n[...], back_n[...]), joined, dpres, hidden, backs, grads)
+def own_kernel(snd_ref, rcv_ref, x_ref, e_ref, w1, b_ref, joined, pre_own):
+    for i in range(e_ref.shape[0] // BLOCK):
+        rows = pl.ds(i * BLOCK, BLOCK)
+        gather_own(i, snd_ref, rcv_ref, x_ref, e_ref, joined)
+        pre_own[rows, :] = mm(joined[rows, :], w1[1]) + b_ref[1, 0:1, :]
+
+
+def grads_kernel(
+    joined_n, dpre_n, act_n, back_n, halo, dpres, hidden, backs, tail, joined, x_ref, agg_b, wn1, wn2, b_ref, g_ref,
+    grads, *node_saved,
+):
+    first = joined[...]
+    first = jnp.concatenate([first[:, 0:128], first[:, 128:256] + halo[...], first[:, 256:384]], axis=1)
+    weight_grads((joined_n[...], dpre_n[...], act_n[...], back_n[...]), first, dpres, hidden, backs, grads)
     grads[896:GRAD_ROWS, :] = tail[...]
+    _, saved = node_forward(x_ref[...], agg_b[...], wn1.at[0], wn2.at[0], b_ref.at[0], g_ref.at[0])
+    for out, value in zip(node_saved, saved):
+        out[...] = value
 
 
 def small_rows(sums, small):
@@ -239,7 +258,17 @@
 ):
     w1, w2, wn1, wn2, b_ref, g_ref = (r.at[0] for r in (w1, w2, wn1, wn2, b_ref, g_ref))
     fill_table(table, x_ref, (r0, r1, r2, r3))
-    edge_forward(snd_ref, rcv_ref, table, e_ref, w1, w2, b_ref, g_ref, joined, hidden, slope, xhat, scale, e_new, agg)
+
+    def gather(i):
+        rows = pl.ds(i * BLOCK, BLOCK)
+        joined[rows, 0:128] = e_ref[rows, :]
+        joined[rows, 128:256] = mm(pick_rows(snd_ref[i], 768), table[...]).astype(BF16)
+        joined[rows, 256:384] = mm(pick_rows(rcv_ref[i], 256), table[0:256, :]).astype(BF16)
+
+    def pre_of(rows):
+        return mm(joined[rows, :], w1[...]) + b_ref[0:1, :]
+
+    edge_forward(gather, pre_of, rcv_ref, e_ref, w2, b_ref, g_ref, hidden, slope, xhat, scale, e_new, agg)
     new, saved = node_forward(x_ref[...], agg[...], wn1, wn2, b_ref, g_ref)
     agg_b[...] = agg[...].astype(BF16)
     x_new[...] = new
@@ -247,13 +276,21 @@
 
 
 def last_kernel(
-    snd_ref, rcv_ref, x_ref, r0, r1, r2, r3, e_ref, w1, w2, wn1, wn2, b_ref, g_ref, cot_ref,
-    x_new, e_grad, x_grad, c0, c1, c2, c3, joined_n, dpre_n, act_n, back_n, joined, dpres, hidden, backs, tail,
+    snd_ref, rcv_ref, x_ref, r0, r1, r2, r3, joined, pre_own, w1, w2, wn1, wn2, b_ref, g_ref, cot_ref,
+    x_new, e_grad, x_grad, c0, c1, c2, c3, joined_n, dpre_n, act_n, back_n, halo, dpres, hidden, backs, tail,
     table, agg, slope, xhat, scale, acc, sums,
 ):
     w1, w2, wn1, wn2, b_ref, g_ref = (r.at[1] for r in (w1, w2, wn1, wn2, b_ref, g_ref))
     fill_table(table, x_ref, (r0, r1, r2, r3))
-    edge_forward(snd_ref, rcv_ref, table, e_ref, w1, w2, b_ref, g_ref, joined, hidden, slope, xhat, scale, None, agg)
+
+    def gather(i):
+        picked = mm(pick_rows(snd_ref[i] - 256, 512), table[256:768, :])
+        halo[pl.ds(i * BLOCK, BLOCK), :] = picked.astype(BF16)
+
+    def pre_of(rows):
+        return pre_own[rows, :] + mm(halo[rows, :], w1[128:256, :])
+
+    edge_forward(gather, pre_of, rcv_ref, joined, w2, b_ref, g_ref, hidden, slope, xhat, scale, None, agg)
     new, saved = node_forward(x_ref[...], agg[...], wn1, wn2, b_ref, g_ref)
     x_new[...] = new
     dx, dagg, node_ops, small = node_backward(cot_ref[...], saved, wn1, wn2, g_ref)
@@ -266,14 +303,14 @@
 
 
 def back_kernel(
-    snd_ref, rcv_ref, send_ref, x_ref, agg_b, own_ref, t0, t1, t2, t3, joined, hidden, slope, xhat, scale, e_cot, late,
+    snd_ref, rcv_ref, send_ref, n0, n1, n2, n3, n4, own_ref, t0, t1, t2, t3, joined, hidden, slope, xhat, scale, e_cot, late,
     w1, w2, wn1, wn2, b_ref, g_ref,
     e_grad, x_grad, c0, c1, c2, c3, grads, acc, dpres, backs, sums,
 ):
     w1, w2, wn1, wn2, b_ref, g_ref = (r.at[0] for r in (w1, w2, wn1, wn2, b_ref, g_ref))
     grads[GRAD_ROWS:, :] = late[...]
     cot = (own_ref[...] + add_returns(send_ref, (t0, t1, t2, t3))).astype(BF16)
-    new, saved = node_forward(x_ref[...], agg_b[...], wn1, wn2, b_ref, g_ref)
+    saved = tuple(r[...] for r in (n0, n1, n2, n3, n4))
     dx, dagg, node_ops, small = node_backward(cot, saved, wn1, wn2, g_ref)
     edge_backward(snd_ref, rcv_ref, w1, w2, g_ref, slope, xhat, scale, dagg, e_cot, e_grad, acc, dpres, backs, sums)
     weight_grads(node_ops, joined, dpres, hidden, backs, grads)
@@ -366,7 +403,7 @@
     ]
     low = shape(n_edge, H, dtype=BF16)
     small = shape(256, H, dtype=BF16)
-    operands = [shape(256, 2 * H, dtype=BF16), small, small, small, residuals[0], low, low, low, shape(GRAD_ROWS - 896, H, dtype=BF16)]
+    operands = [shape(256, 2 * H, dtype=BF16), small, small, small, low, low, low, low, shape(GRAD_ROWS - 896, H, dtype=BF16)]
     table = shape(768, H, dtype=BF16)
 
     *sent, send, x0 = call(
@@ -399,21 +436,34 @@
     )
     saved, (e1, agg0, x1), sent = out[:5], out[5:8], out[8:]
     got = exchange(sent)
+    joined1, pre1 = call(
+        own_kernel,
+        [residuals[0], shape(n_edge, H)],
+        [],
+        (snd, rcv, x1, e1, weights[0], weights[4]),
+        "own1",
+    )
     out = call(
         last_kernel,
         [shape(256, H, dtype=BF16), shape(n_edge, H, dtype=BF16), shape(256, H)] + rows4 + operands,
         [table, shape(256, H)] + residuals[2:] + [shape(768, H), shape(8, H)],
-        (snd, rcv, x1, *got, e1, *weights, cot),
+        (snd, rcv, x1, *got, joined1, pre1, *weights, cot),
         "layer1",
     )
     nodes_out, e_cot, own = out[:3]
     back = exchange(out[3:7])
-    (grads1,) = call(grads_kernel, [shape(GRAD_ROWS, H, dtype=BF16)], [], out[7:], "wgrad1")
+    grads1, *node0 = call(
+        grads_kernel,
+        [shape(GRAD_ROWS, H, dtype=BF16), shape(256, 2 * H, dtype=BF16), small, shape(256, H), shape(256, H), shape(256, 1)],
+        [],
+        (*out[7:], joined1, x0, agg0, *weights[2:]),
+        "wgrad1",
+    )
     out = call(
         back_kernel,
         [shape(n_edge, H, dtype=BF16), shape(256, H)] + rows4 + [shape(2 * GRAD_ROWS, H, dtype=BF16)],
         [shape(768, H), low, low, shape(8, H)],
-        (snd, rcv, send, x0, agg0, own, *back, *saved, e_cot, grads1, *weights),
+        (snd, rcv, send, *node0, own, *back, *saved, e_cot, grads1, *weights),
         "back0",
     )
     edge_grad, own = out[:2]

time: 108 us -> 104 us (0.963)
  Pallas kernels: 23.2 us -> 21.1 us
  starting transfers between devices: 43.9 us -> 42.8 us
    pallas_call x10 -> x11, Pallas kernels: 23.2 us -> 21.1 us  [call(): pl.pallas_call(kernel, out_shape=outs, in_specs=[pl.BlockSpec(memory_spac...]
  transfers between devices with their start and end apart: 18 -> 18, of which waited for: 5 -> 4; matrix products, arithmetic and copies ran while one was open for 0% -> 0% of each run, Pallas kernels for 3% -> 4%
where the time goes in v5:
time: 104 us; the launch traced here: 103 us
  starting transfers between devices  42.8 us (41%)
  Pallas kernels  21.1 us (20%)
  blocking collectives  20.7 us (20%)
  waiting for transfers between devices  17.7 us (17%)
    ppermute x16, starting transfers between devices, exchange(): lax.ppermute(b, axis, swaps(axis, first))  30 us
    pallas_call x11, Pallas kernels, call(): pl.pallas_call(kernel, out_shape=outs, in_specs=[pl.BlockSpec(memory_spac...  21.1 us
    all_to_all x1, blocking collectives, swap_tiles(): return lax.all_to_all(x, axis, split_axis=0, concat_axis=0, tiled=True)  20.7 us
    all_to_all x2, starting transfers between devices, swap_tiles(): return lax.all_to_all(x, axis, split_axis=0, concat_axis=0, tiled=True)  12.9 us
    all_to_all x2, waiting for transfers between devices, swap_tiles(): return lax.all_to_all(x, axis, split_axis=0, concat_axis=0, tiled=True)  12.7 us
    ppermute x16, waiting for transfers between devices, exchange(): lax.ppermute(b, axis, swaps(axis, first))  4.99 us
  transfers between devices with their start and end apart: 18, of which 4 were waited for; matrix products, arithmetic and copies ran while one was open for 0% of the time, Pallas kernels for 4%

profile of v5, /device:TPU:1, one launch (start us, length us, event | category | flops | bytes accessed | tf_op | source)
XLA Modules:
  0.0 103.1 jit_solution(11067862429536829192)
XLA Ops:
  0.6 1.3 %sends.1 = (bf16[128,128]{1,0:T(8,128)(2,1)S(1)}, bf16[128,128]{1,0:T(8,128)(2,1)S(1)}, bf16[128,128]{1,0:T(8,128)(2,1)S(1)}, bf16[128,128]{1,0:T(8,128)(2,1)S(1...) custom-call(s32[4,128]{1,0:T(4,128)} %bitcast.18, bf16[256,128]{1,0:T(8,128)(2,1)} %bitcast.15), custom_call_target="tpu_custom_call" | custom-call | tf_op jit(solution)/shard_map/sends/pallas_call | solution.py:339
  1.9 4.6 %collective-permute-start.1 = (bf16[128,128]{1,0:T(8,128)(2,1)S(1)}, bf16[128,128]{1,0:T(8,128)(2,1)S(1)}, u32[]{:S(2)}, u32[]{:S(2)}) collective-permute-start(bf16[128,128]{1,0:T(8,128)(2,1)S(1)} %get-tuple-element.79), channel_id=1, source_target_pairs={{8,16},{16,8},{24,32},{32,24},{40,48},{48,40},{56,64},{64,56},{72,... | collective-permute-start | bytes 98312 | tf_op jit(solution)/shard_map/ppermute | solution.py:357
  6.5 1.7 %collective-permute-start.2 = (bf16[128,128]{1,0:T(8,128)(2,1)S(1)}, bf16[128,128]{1,0:T(8,128)(2,1)S(1)}, u32[]{:S(2)}, u32[]{:S(2)}) collective-permute-start(bf16[128,128]{1,0:T(8,128)(2,1)S(1)} %get-tuple-element.80), channel_id=1, source_target_pairs={{0,1},{1,0},{2,3},{3,2},{4,5},{5,4},{6,7},{7,6},{8,9},{9,8},{10,11... | collective-permute-start | bytes 98312 | tf_op jit(solution)/shard_map/ppermute | solution.py:357
  9.0 1.3 %load.1 = (s32[2,1,768]{2,1,0:T(1,128)S(1)}, s32[2,1,768]{2,1,0:T(1,128)S(1)}, bf16[1536,128]{1,0:T(8,128)(2,1)S(1)}, bf16[256,128]{1,0:T(8,128)(2,1)S(1)}, bf16...) custom-call(s32[1,4]{1,0:T(1,128)} %cnt_hbm.1, ...), custom_call_target="tpu_custom_call" | custom-call | tf_op jit(solution)/shard_map/load/pallas_call | solution.py:339
  10.4 3.5 %layer0.1 = (bf16[1536,384]{1,0:T(8,128)(2,1)S(1)}, bf16[1536,128]{1,0:T(8,128)(2,1)S(1)}, f32[1536,128]{1,0:T(8,128)S(1)}, f32[1536,128]{1,0:T(8,128)S(1)}, f32...) custom-call(s32[2,1,768]{2,1,0:T(1,128)S(1)} %get-tuple-element.75.s, ...), custom_call_target="tpu_custom_call" | custom-call | tf_op jit(solution)/shard_map/layer0/pallas_call | solution.py:339
  14.4 3.1 %collective-permute-start.5 = (bf16[128,128]{1,0:T(8,128)(2,1)S(1)}, bf16[128,128]{1,0:T(8,128)(2,1)S(1)}, u32[]{:S(2)}, u32[]{:S(2)}) collective-permute-start(bf16[128,128]{1,0:T(8,128)(2,1)S(1)} %get-tuple-element.91), channel_id=1, source_target_pairs={{8,16},{16,8},{24,32},{32,24},{40,48},{48,40},{56,64},{64,56},{72,... | collective-permute-start | bytes 98312 | tf_op jit(solution)/shard_map/ppermute | solution.py:357
  17.5 4.6 %collective-permute-start.6 = (bf16[128,128]{1,0:T(8,128)(2,1)S(1)}, bf16[128,128]{1,0:T(8,128)(2,1)S(1)}, u32[]{:S(2)}, u32[]{:S(2)}) collective-permute-start(bf16[128,128]{1,0:T(8,128)(2,1)S(1)} %get-tuple-element.92), channel_id=1, source_target_pairs={{0,1},{1,0},{2,3},{3,2},{4,5},{5,4},{6,7},{7,6},{8,9},{9,8},{10,11... | collective-permute-start | bytes 98312 | tf_op jit(solution)/shard_map/ppermute | solution.py:357
  22.8 1.4 %own1.1 = (bf16[1536,384]{1,0:T(8,128)(2,1)S(1)}, f32[1536,128]{1,0:T(8,128)S(1)}) custom-call(s32[2,1,768]{2,1,0:T(1,128)S(1)} %get-tuple-element.75.snd_ref, s32[2,1,768]{2,1,0:T(1,128)S(1)} %get-tuple-element.76.rcv_ref, bf16[256,128]{1,0:T(8,128)(2,1)S(1)} %get-tuple-element.89.x_ref, bf16[1536,128]{1,0:T(8,128)(2,1)S(1)} %get-tuple-element.94.e_ref, ...), custom_call_target="tpu_custom_call" | custom-call | tf_op jit(solution)/shard_map/own1/pallas_call | solution.py:339
  24.2 5.7 %layer1.1 = (bf16[256,128]{1,0:T(8,128)(2,1)}, bf16[1536,128]{1,0:T(8,128)(2,1)S(1)}, f32[256,128]{1,0:T(8,128)S(1)}, bf16[128,128]{1,0:T(8,128)(2,1)S(1)}, bf16...) custom-call(s32[2,1,768]{2,1,0:T(1,128)S(1)} %get-tuple-element.75.s, ...), custom_call_target="tpu_custom_call" | custom-call | tf_op jit(solution)/shard_map/layer1/pallas_call | solution.py:339
  29.9 3.3 %collective-permute-start.9 = (bf16[128,128]{1,0:T(8,128)(2,1)S(1)}, bf16[128,128]{1,0:T(8,128)(2,1)S(1)}, u32[]{:S(2)}, u32[]{:S(2)}) collective-permute-start(bf16[128,128]{1,0:T(8,128)(2,1)S(1)} %get-tuple-element.116), channel_id=1, source_target_pairs={{8,16},{16,8},{24,32},{32,24},{40,48},{48,40},{56,64},{64,56},{72,... | collective-permute-start | bytes 98312 | tf_op jit(solution)/shard_map/ppermute | solution.py:357
  33.2 5.3 %collective-permute-start.10 = (bf16[128,128]{1,0:T(8,128)(2,1)S(1)}, bf16[128,128]{1,0:T(8,128)(2,1)S(1)}, u32[]{:S(2)}, u32[]{:S(2)}) collective-permute-start(bf16[128,128]{1,0:T(8,128)(2,1)S(1)} %get-tuple-element.117), channel_id=1, source_target_pairs={{0,1},{1,0},{2,3},{3,2},{4,5},{5,4},{6,7},{7,6},{8,9},{9,8},{10,11... | collective-permute-start | bytes 98312 | tf_op jit(solution)/shard_map/ppermute | solution.py:357
  39.1 0.9 wgrad1.1
  40.1 4.3 %back0.1 = (bf16[1536,128]{1,0:T(8,128)(2,1)}, f32[256,128]{1,0:T(8,128)S(1)}, bf16[128,128]{1,0:T(8,128)(2,1)S(1)}, bf16[128,128]{1,0:T(8,128)(2,1)S(1)}, bf16[...) custom-call(s32[2,1,768]{2,1,0:T(1,128)S(1)} %get-tuple-element.75.snd_ref, ...), custom_call_target="tpu_custom_call" | custom-call | tf_op jit(solution)/shard_map/back0/pallas_call | solution.py:339
  44.4 8.8 %all-to-all-start = ((bf16[32,64,128]{2,1,0:T(8,128)(2,1)}), bf16[32,64,128]{2,1,0:T(8,128)(2,1)S(1)}, u32[]{:S(2)}, u32[]{:S(2)}) async-start(bf16[32,64,128]{2,1,0:T(8,128)(2,1)} %bitcast.9), calls=%async_computation | async-start | bytes 1048576 | tf_op jit(solution)/shard_map/all_to_all | solution.py:374
  53.5 3.4 %collective-permute-start.13 = (bf16[128,128]{1,0:T(8,128)(2,1)S(1)}, bf16[128,128]{1,0:T(8,128)(2,1)S(1)}, u32[]{:S(2)}, u32[]{:S(2)}) collective-permute-start(bf16[128,128]{1,0:T(8,128)(2,1)S(1)} %get-tuple-element.128), channel_id=1, source_target_pairs={{8,16},{16,8},{24,32},{32,24},{40,48},{48,40},{56,64},{64,56},{72,... | collective-permute-start | bytes 98312 | tf_op jit(solution)/shard_map/ppermute | solution.py:357
  56.9 3.1 %collective-permute-done.13.t1.refs_1_ = bf16[128,128]{1,0:T(8,128)(2,1)S(1)} collective-permute-done((bf16[128,128]{1,0:T(8,128)(2,1)S(1)}, bf16[128,128]{1,0:T(8,128)(2,1)S(1)}, u32[]{:S(2)}, u32[]{:S(2)}) %collective-permute-start.13) | collective-permute-done | bytes 32800 | tf_op jit(solution)/shard_map/ppermute | solution.py:357
  60.0 4.7 %all-to-all-done.x_ref = bf16[32,64,128]{2,1,0:T(8,128)(2,1)S(1)} async-done(((bf16[32,64,128]{2,1,0:T(8,128)(2,1)}), bf16[32,64,128]{2,1,0:T(8,128)(2,1)S(1)}, u32[]{:S(2)}, u32[]{:S(2)}) %all-to-all-start) | async-done | bytes 524320 | tf_op jit(solution)/shard_map/all_to_all | solution.py:374
  64.9 20.7 %all_to_all.15.x_ref = bf16[8,64,128]{2,1,0:T(8,128)(2,1)S(1)} all-to-all(bf16[8,64,128]{2,1,0:T(8,128)(2,1)S(1)} %fold_dom.1), channel_id=1, replica_groups=mesh['dom'=32,'group'=8] {'group'}, dimensions={0} | all-to-all | bytes 262144 | tf_op jit(solution)/shard_map/all_to_all | solution.py:374
  85.5 0.9 fold_group.1
  86.4 4.1 %all-to-all-start.2 = ((bf16[32,64,128]{2,1,0:T(8,128)(2,1)}), bf16[32,64,128]{2,1,0:T(8,128)(2,1)S(1)}, u32[]{:S(2)}, u32[]{:S(2)}) async-start(bf16[32,64,128]{2,1,0:T(8,128)(2,1)} %fold_group.1), calls=%async_computation.2 | async-start | bytes 1048576 | tf_op jit(solution)/shard_map/all_to_all | solution.py:374
  91.5 1.8 %collective-permute-done.14.t2 = bf16[128,128]{1,0:T(8,128)(2,1)S(1)} collective-permute-done((bf16[128,128]{1,0:T(8,128)(2,1)S(1)}, bf16[128,128]{1,0:T(8,128)(2,1)S(1)}, u32[]{:S(2)}, u32[]{:S(2)}) %collective-permute-start.14) | collective-permute-done | bytes 32800 | tf_op jit(solution)/shard_map/ppermute | solution.py:357
  93.4 0.9 finish.1
  94.2 8.0 %all-to-all-done.2 = bf16[32,64,128]{2,1,0:T(8,128)(2,1)S(1)} async-done(((bf16[32,64,128]{2,1,0:T(8,128)(2,1)}), bf16[32,64,128]{2,1,0:T(8,128)(2,1)S(1)}, u32[]{:S(2)}, u32[]{:S(2)}) %all-to-all-start.2) | async-done | bytes 524320 | tf_op jit(solution)/shard_map/all_to_all | solution.py:374
  102.2 0.9 unpack.1
  (24 shorter events, 4.1 us)
Async XLA Ops:
  1.9 8.4 %collective-permute-start.1 = (bf16[128,128]{1,0:T(8,128)(2,1)S(1)}, bf16[128,128]{1,0:T(8,128)(2,1)S(1)}, u32[]{:S(2)}, u32[]{:S(2)}) collective-permute-start(bf16[128,128]{1,0:T(8,128)(2,1)S(1)} %get-tuple-element.79), channel_id=1, source_target_pairs={{8,16},{16,8},{24,32},{32,24},{40,48},{48,40},{56,64},{64,56},{72,... | collective-permute-start | bytes 98312 | tf_op jit(solution)/shard_map/ppermute | solution.py:357
  6.5 3.8 %collective-permute-start.2 = (bf16[128,128]{1,0:T(8,128)(2,1)S(1)}, bf16[128,128]{1,0:T(8,128)(2,1)S(1)}, u32[]{:S(2)}, u32[]{:S(2)}) collective-permute-start(bf16[128,128]{1,0:T(8,128)(2,1)S(1)} %get-tuple-element.80), channel_id=1, source_target_pairs={{0,1},{1,0},{2,3},{3,2},{4,5},{5,4},{6,7},{7,6},{8,9},{9,8},{10,11... | collective-permute-start | bytes 98312 | tf_op jit(solution)/shard_map/ppermute | solution.py:357
  8.2 2.1 %collective-permute-start.3 = (bf16[128,128]{1,0:T(8,128)(2,1)S(1)}, bf16[128,128]{1,0:T(8,128)(2,1)S(1)}, u32[]{:S(2)}, u32[]{:S(2)}) collective-permute-start(bf16[128,128]{1,0:T(8,128)(2,1)S(1)} %get-tuple-element.81), channel_id=1, source_target_pairs={{1,2},{2,1},{3,4},{4,3},{5,6},{6,5},{9,10},{10,9},{11,12},{12,11},... | collective-permute-start | bytes 98312 | tf_op jit(solution)/shard_map/ppermute | solution.py:357
  8.9 1.5 %collective-permute-start = (bf16[128,128]{1,0:T(8,128)(2,1)S(1)}, bf16[128,128]{1,0:T(8,128)(2,1)S(1)}, u32[]{:S(2)}, u32[]{:S(2)}) collective-permute-start(bf16[128,128]{1,0:T(8,128)(2,1)S(1)} %get-tuple-element.74.token), channel_id=1, source_target_pairs={{0,8},{8,0},{16,24},{24,16},{32,40},{40,32},{48,56},{56,48},{64,72... | collective-permute-start | bytes 98312 | tf_op jit(solution)/shard_map/ppermute | solution.py:357
  13.9 10.4 %collective-permute-start.4 = (bf16[128,128]{1,0:T(8,128)(2,1)S(1)}, bf16[128,128]{1,0:T(8,128)(2,1)S(1)}, u32[]{:S(2)}, u32[]{:S(2)}) collective-permute-start(bf16[128,128]{1,0:T(8,128)(2,1)S(1)} %get-tuple-element.90), channel_id=1, source_target_pairs={{0,8},{8,0},{16,24},{24,16},{32,40},{40,32},{48,56},{56,48},{64,72... | collective-permute-start | bytes 98312 | tf_op jit(solution)/shard_map/ppermute | solution.py:357
  14.4 9.8 %collective-permute-start.5 = (bf16[128,128]{1,0:T(8,128)(2,1)S(1)}, bf16[128,128]{1,0:T(8,128)(2,1)S(1)}, u32[]{:S(2)}, u32[]{:S(2)}) collective-permute-start(bf16[128,128]{1,0:T(8,128)(2,1)S(1)} %get-tuple-element.91), channel_id=1, source_target_pairs={{8,16},{16,8},{24,32},{32,24},{40,48},{48,40},{56,64},{64,56},{72,... | collective-permute-start | bytes 98312 | tf_op jit(solution)/shard_map/ppermute | solution.py:357
  17.5 6.7 %collective-permute-start.6 = (bf16[128,128]{1,0:T(8,128)(2,1)S(1)}, bf16[128,128]{1,0:T(8,128)(2,1)S(1)}, u32[]{:S(2)}, u32[]{:S(2)}) collective-permute-start(bf16[128,128]{1,0:T(8,128)(2,1)S(1)} %get-tuple-element.92), channel_id=1, source_target_pairs={{0,1},{1,0},{2,3},{3,2},{4,5},{5,4},{6,7},{7,6},{8,9},{9,8},{10,11... | collective-permute-start | bytes 98312 | tf_op jit(solution)/shard_map/ppermute | solution.py:357
  22.1 2.1 %collective-permute-start.7 = (bf16[128,128]{1,0:T(8,128)(2,1)S(1)}, bf16[128,128]{1,0:T(8,128)(2,1)S(1)}, u32[]{:S(2)}, u32[]{:S(2)}) collective-permute-start(bf16[128,128]{1,0:T(8,128)(2,1)S(1)} %get-tuple-element.93), channel_id=1, source_target_pairs={{1,2},{2,1},{3,4},{4,3},{5,6},{6,5},{9,10},{10,9},{11,12},{12,11},... | collective-permute-start | bytes 98312 | tf_op jit(solution)/shard_map/ppermute | solution.py:357
  29.9 10.2 %collective-permute-start.8 = (bf16[128,128]{1,0:T(8,128)(2,1)S(1)}, bf16[128,128]{1,0:T(8,128)(2,1)S(1)}, u32[]{:S(2)}, u32[]{:S(2)}) collective-permute-start(bf16[128,128]{1,0:T(8,128)(2,1)S(1)} %get-tuple-element.115), channel_id=1, source_target_pairs={{0,8},{8,0},{16,24},{24,16},{32,40},{40,32},{48,56},{56,48},{64,72... | collective-permute-start | bytes 98312 | tf_op jit(solution)/shard_map/ppermute | solution.py:357
  29.9 10.2 %collective-permute-start.9 = (bf16[128,128]{1,0:T(8,128)(2,1)S(1)}, bf16[128,128]{1,0:T(8,128)(2,1)S(1)}, u32[]{:S(2)}, u32[]{:S(2)}) collective-permute-start(bf16[128,128]{1,0:T(8,128)(2,1)S(1)} %get-tuple-element.116), channel_id=1, source_target_pairs={{8,16},{16,8},{24,32},{32,24},{40,48},{48,40},{56,64},{64,56},{72,... | collective-permute-start | bytes 98312 | tf_op jit(solution)/shard_map/ppermute | solution.py:357
  33.2 6.9 %collective-permute-start.10 = (bf16[128,128]{1,0:T(8,128)(2,1)S(1)}, bf16[128,128]{1,0:T(8,128)(2,1)S(1)}, u32[]{:S(2)}, u32[]{:S(2)}) collective-permute-start(bf16[128,128]{1,0:T(8,128)(2,1)S(1)} %get-tuple-element.117), channel_id=1, source_target_pairs={{0,1},{1,0},{2,3},{3,2},{4,5},{5,4},{6,7},{7,6},{8,9},{9,8},{10,11... | collective-permute-start | bytes 98312 | tf_op jit(solution)/shard_map/ppermute | solution.py:357
  38.5 1.6 %collective-permute-start.11 = (bf16[128,128]{1,0:T(8,128)(2,1)S(1)}, bf16[128,128]{1,0:T(8,128)(2,1)S(1)}, u32[]{:S(2)}, u32[]{:S(2)}) collective-permute-start(bf16[128,128]{1,0:T(8,128)(2,1)S(1)} %get-tuple-element.118), channel_id=1, source_target_pairs={{1,2},{2,1},{3,4},{4,3},{5,6},{6,5},{9,10},{10,9},{11,12},{12,11},... | collective-permute-start | bytes 98312 | tf_op jit(solution)/shard_map/ppermute | solution.py:357
  44.4 20.4 %all-to-all-start = ((bf16[32,64,128]{2,1,0:T(8,128)(2,1)}), bf16[32,64,128]{2,1,0:T(8,128)(2,1)S(1)}, u32[]{:S(2)}, u32[]{:S(2)}) async-start(bf16[32,64,128]{2,1,0:T(8,128)(2,1)} %bitcast.9), calls=%async_computation | async-start | bytes 1048576 | tf_op jit(solution)/shard_map/all_to_all | solution.py:374
  53.2 3.7 %collective-permute-start.12 = (bf16[128,128]{1,0:T(8,128)(2,1)S(1)}, bf16[128,128]{1,0:T(8,128)(2,1)S(1)}, u32[]{:S(2)}, u32[]{:S(2)}) collective-permute-start(bf16[128,128]{1,0:T(8,128)(2,1)S(1)} %get-tuple-element.127), channel_id=1, source_target_pairs={{0,8},{8,0},{16,24},{24,16},{32,40},{40,32},{48,56},{56,48},{64,72... | collective-permute-start | bytes 98312 | tf_op jit(solution)/shard_map/ppermute | solution.py:357
  53.5 6.5 %collective-permute-start.13 = (bf16[128,128]{1,0:T(8,128)(2,1)S(1)}, bf16[128,128]{1,0:T(8,128)(2,1)S(1)}, u32[]{:S(2)}, u32[]{:S(2)}) collective-permute-start(bf16[128,128]{1,0:T(8,128)(2,1)S(1)} %get-tuple-element.128), channel_id=1, source_target_pairs={{8,16},{16,8},{24,32},{32,24},{40,48},{48,40},{56,64},{64,56},{72,... | collective-permute-start | bytes 98312 | tf_op jit(solution)/shard_map/ppermute | solution.py:357
  86.4 15.8 %all-to-all-start.2 = ((bf16[32,64,128]{2,1,0:T(8,128)(2,1)}), bf16[32,64,128]{2,1,0:T(8,128)(2,1)S(1)}, u32[]{:S(2)}, u32[]{:S(2)}) async-start(bf16[32,64,128]{2,1,0:T(8,128)(2,1)} %fold_group.1), calls=%async_computation.2 | async-start | bytes 1048576 | tf_op jit(solution)/shard_map/all_to_all | solution.py:374
  90.5 2.9 %collective-permute-start.14 = (bf16[128,128]{1,0:T(8,128)(2,1)S(1)}, bf16[128,128]{1,0:T(8,128)(2,1)S(1)}, u32[]{:S(2)}, u32[]{:S(2)}) collective-permute-start(bf16[128,128]{1,0:T(8,128)(2,1)S(1)} %get-tuple-element.129), channel_id=1, source_target_pairs={{0,1},{1,0},{2,3},{3,2},{4,5},{5,4},{6,7},{7,6},{8,9},{9,8},{10,11... | collective-permute-start | bytes 98312 | tf_op jit(solution)/shard_map/ppermute | solution.py:357
  90.9 2.5 %collective-permute-start.15 = (bf16[128,128]{1,0:T(8,128)(2,1)S(1)}, bf16[128,128]{1,0:T(8,128)(2,1)S(1)}, u32[]{:S(2)}, u32[]{:S(2)}) collective-permute-start(bf16[128,128]{1,0:T(8,128)(2,1)S(1)} %get-tuple-element.130), channel_id=1, source_target_pairs={{1,2},{2,1},{3,4},{4,3},{5,6},{6,5},{9,10},{10,9},{11,12},{12,11},... | collective-permute-start | bytes 98312 | tf_op jit(solution)/shard_map/ppermute | solution.py:357

commit v6 on v5

--- a/solution.py
+++ b/solution.py
@@ -472,7 +472,7 @@
     (node_grad,) = call(finish_kernel, [shape(256, H, dtype=BF16)], [], (send, own, *back), "finish")
 
     scale = (lax.axis_size("dom") * lax.axis_size("group") * x0.shape[0]) ** (-0.5)
-    grads = reduce_grads(packed, scale, back[:2], ())
+    grads = reduce_grads(packed, scale, back[:2], back[2:3])
     return (nodes_out[None], node_grad[None], edge_grad[None], *grads)
 
 

time: 104 us -> 105 us (level)
  blocking collectives: 20.7 us -> 0 us
  starting transfers between devices: 42.8 us -> 55.6 us
  waiting for transfers between devices: 17.7 us -> 25.9 us
    all_to_all x1 -> x0, blocking collectives: 20.7 us -> none  [swap_tiles(): return lax.all_to_all(x, axis, split_axis=0, concat_axis=0, tiled=True)]
    all_to_all x2 -> x3, starting transfers between devices: 12.9 us -> 24.6 us  [swap_tiles(): return lax.all_to_all(x, axis, split_axis=0, concat_axis=0, tiled=True)]
    all_to_all x2 -> x3, waiting for transfers between devices: 12.7 us -> 18.6 us  [swap_tiles(): return lax.all_to_all(x, axis, split_axis=0, concat_axis=0, tiled=True)]
    ppermute x16, waiting for transfers between devices: 4.99 us -> 7.24 us  [exchange(): lax.ppermute(b, axis, swaps(axis, first))]
    ppermute x16, starting transfers between devices: 30 us -> 31.1 us  [exchange(): lax.ppermute(b, axis, swaps(axis, first))]
  transfers between devices with their start and end apart: 18 -> 19, of which waited for: 4 -> 5; matrix products, arithmetic and copies ran while one was open for 0% -> 0% of each run, Pallas kernels for 4% -> 4%
where the time goes in v6:
time: 105 us; the launch traced here: 104 us
  starting transfers between devices  55.6 us (53%)
  waiting for transfers between devices  25.9 us (25%)
  Pallas kernels  21.8 us (21%)
    ppermute x16, starting transfers between devices, exchange(): lax.ppermute(b, axis, swaps(axis, first))  31.1 us
    all_to_all x3, starting transfers between devices, swap_tiles(): return lax.all_to_all(x, axis, split_axis=0, concat_axis=0, tiled=True)  24.6 us
    pallas_call x11, Pallas kernels, call(): pl.pallas_call(kernel, out_shape=outs, in_specs=[pl.BlockSpec(memory_spac...  21.8 us
    all_to_all x3, waiting for transfers between devices, swap_tiles(): return lax.all_to_all(x, axis, split_axis=0, concat_axis=0, tiled=True)  18.6 us
    ppermute x16, waiting for transfers between devices, exchange(): lax.ppermute(b, axis, swaps(axis, first))  7.24 us
  transfers between devices with their start and end apart: 19, of which 5 were waited for; matrix products, arithmetic and copies ran while one was open for 0% of the time, Pallas kernels for 4%

profile of v6, /device:TPU:1, one launch (start us, length us, event | category | flops | bytes accessed | tf_op | source)
XLA Modules:
  0.0 104.2 jit_solution(11852618713250712970)
XLA Ops:
  0.6 1.3 %sends.1 = (bf16[128,128]{1,0:T(8,128)(2,1)S(1)}, bf16[128,128]{1,0:T(8,128)(2,1)S(1)}, bf16[128,128]{1,0:T(8,128)(2,1)S(1)}, bf16[128,128]{1,0:T(8,128)(2,1)S(1...) custom-call(s32[4,128]{1,0:T(4,128)} %bitcast.18, bf16[256,128]{1,0:T(8,128)(2,1)} %bitcast.15), custom_call_target="tpu_custom_call" | custom-call | tf_op jit(solution)/shard_map/sends/pallas_call | solution.py:339
  1.9 4.6 %collective-permute-start.1 = (bf16[128,128]{1,0:T(8,128)(2,1)S(1)}, bf16[128,128]{1,0:T(8,128)(2,1)S(1)}, u32[]{:S(2)}, u32[]{:S(2)}) collective-permute-start(bf16[128,128]{1,0:T(8,128)(2,1)S(1)} %get-tuple-element.79), channel_id=1, source_target_pairs={{8,16},{16,8},{24,32},{32,24},{40,48},{48,40},{56,64},{64,56},{72,... | collective-permute-start | bytes 98312 | tf_op jit(solution)/shard_map/ppermute | solution.py:357
  6.5 1.7 %collective-permute-start.2 = (bf16[128,128]{1,0:T(8,128)(2,1)S(1)}, bf16[128,128]{1,0:T(8,128)(2,1)S(1)}, u32[]{:S(2)}, u32[]{:S(2)}) collective-permute-start(bf16[128,128]{1,0:T(8,128)(2,1)S(1)} %get-tuple-element.80), channel_id=1, source_target_pairs={{0,1},{1,0},{2,3},{3,2},{4,5},{5,4},{6,7},{7,6},{8,9},{9,8},{10,11... | collective-permute-start | bytes 98312 | tf_op jit(solution)/shard_map/ppermute | solution.py:357
  9.0 1.3 %load.1 = (s32[2,1,768]{2,1,0:T(1,128)S(1)}, s32[2,1,768]{2,1,0:T(1,128)S(1)}, bf16[1536,128]{1,0:T(8,128)(2,1)S(1)}, bf16[256,128]{1,0:T(8,128)(2,1)S(1)}, bf16...) custom-call(s32[1,4]{1,0:T(1,128)} %cnt_hbm.1, ...), custom_call_target="tpu_custom_call" | custom-call | tf_op jit(solution)/shard_map/load/pallas_call | solution.py:339
  10.4 3.5 %layer0.1 = (bf16[1536,384]{1,0:T(8,128)(2,1)S(1)}, bf16[1536,128]{1,0:T(8,128)(2,1)S(1)}, f32[1536,128]{1,0:T(8,128)S(1)}, f32[1536,128]{1,0:T(8,128)S(1)}, f32...) custom-call(s32[2,1,768]{2,1,0:T(1,128)S(1)} %get-tuple-element.75.s, ...), custom_call_target="tpu_custom_call" | custom-call | tf_op jit(solution)/shard_map/layer0/pallas_call | solution.py:339
  14.4 3.1 %collective-permute-start.5 = (bf16[128,128]{1,0:T(8,128)(2,1)S(1)}, bf16[128,128]{1,0:T(8,128)(2,1)S(1)}, u32[]{:S(2)}, u32[]{:S(2)}) collective-permute-start(bf16[128,128]{1,0:T(8,128)(2,1)S(1)} %get-tuple-element.91), channel_id=1, source_target_pairs={{8,16},{16,8},{24,32},{32,24},{40,48},{48,40},{56,64},{64,56},{72,... | collective-permute-start | bytes 98312 | tf_op jit(solution)/shard_map/ppermute | solution.py:357
  17.5 4.6 %collective-permute-start.6 = (bf16[128,128]{1,0:T(8,128)(2,1)S(1)}, bf16[128,128]{1,0:T(8,128)(2,1)S(1)}, u32[]{:S(2)}, u32[]{:S(2)}) collective-permute-start(bf16[128,128]{1,0:T(8,128)(2,1)S(1)} %get-tuple-element.92), channel_id=1, source_target_pairs={{0,1},{1,0},{2,3},{3,2},{4,5},{5,4},{6,7},{7,6},{8,9},{9,8},{10,11... | collective-permute-start | bytes 98312 | tf_op jit(solution)/shard_map/ppermute | solution.py:357
  22.8 1.4 %own1.1 = (bf16[1536,384]{1,0:T(8,128)(2,1)S(1)}, f32[1536,128]{1,0:T(8,128)S(1)}) custom-call(s32[2,1,768]{2,1,0:T(1,128)S(1)} %get-tuple-element.75.snd_ref, s32[2,1,768]{2,1,0:T(1,128)S(1)} %get-tuple-element.76.rcv_ref, bf16[256,128]{1,0:T(8,128)(2,1)S(1)} %get-tuple-element.89.x_ref, bf16[1536,128]{1,0:T(8,128)(2,1)S(1)} %get-tuple-element.94.e_ref, ...), custom_call_target="tpu_custom_call" | custom-call | tf_op jit(solution)/shard_map/own1/pallas_call | solution.py:339
  24.2 5.7 %layer1.1 = (bf16[256,128]{1,0:T(8,128)(2,1)}, bf16[1536,128]{1,0:T(8,128)(2,1)S(1)}, f32[256,128]{1,0:T(8,128)S(1)}, bf16[128,128]{1,0:T(8,128)(2,1)S(1)}, bf16...) custom-call(s32[2,1,768]{2,1,0:T(1,128)S(1)} %get-tuple-element.75.s, ...), custom_call_target="tpu_custom_call" | custom-call | tf_op jit(solution)/shard_map/layer1/pallas_call | solution.py:339
  29.9 3.3 %collective-permute-start.9 = (bf16[128,128]{1,0:T(8,128)(2,1)S(1)}, bf16[128,128]{1,0:T(8,128)(2,1)S(1)}, u32[]{:S(2)}, u32[]{:S(2)}) collective-permute-start(bf16[128,128]{1,0:T(8,128)(2,1)S(1)} %get-tuple-element.116), channel_id=1, source_target_pairs={{8,16},{16,8},{24,32},{32,24},{40,48},{48,40},{56,64},{64,56},{72,... | collective-permute-start | bytes 98312 | tf_op jit(solution)/shard_map/ppermute | solution.py:357
  33.2 5.3 %collective-permute-start.10 = (bf16[128,128]{1,0:T(8,128)(2,1)S(1)}, bf16[128,128]{1,0:T(8,128)(2,1)S(1)}, u32[]{:S(2)}, u32[]{:S(2)}) collective-permute-start(bf16[128,128]{1,0:T(8,128)(2,1)S(1)} %get-tuple-element.117), channel_id=1, source_target_pairs={{0,1},{1,0},{2,3},{3,2},{4,5},{5,4},{6,7},{7,6},{8,9},{9,8},{10,11... | collective-permute-start | bytes 98312 | tf_op jit(solution)/shard_map/ppermute | solution.py:357
  39.1 0.9 wgrad1.1
  40.1 4.3 %back0.1 = (bf16[1536,128]{1,0:T(8,128)(2,1)}, f32[256,128]{1,0:T(8,128)S(1)}, bf16[128,128]{1,0:T(8,128)(2,1)S(1)}, bf16[128,128]{1,0:T(8,128)(2,1)S(1)}, bf16[...) custom-call(s32[2,1,768]{2,1,0:T(1,128)S(1)} %get-tuple-element.75.snd_ref, ...), custom_call_target="tpu_custom_call" | custom-call | tf_op jit(solution)/shard_map/back0/pallas_call | solution.py:339
  44.4 8.8 %all-to-all-start = ((bf16[32,64,128]{2,1,0:T(8,128)(2,1)}), bf16[32,64,128]{2,1,0:T(8,128)(2,1)S(1)}, u32[]{:S(2)}, u32[]{:S(2)}) async-start(bf16[32,64,128]{2,1,0:T(8,128)(2,1)} %bitcast.9), calls=%async_computation | async-start | bytes 1048576 | tf_op jit(solution)/shard_map/all_to_all | solution.py:374
  53.5 3.4 %collective-permute-start.13 = (bf16[128,128]{1,0:T(8,128)(2,1)S(1)}, bf16[128,128]{1,0:T(8,128)(2,1)S(1)}, u32[]{:S(2)}, u32[]{:S(2)}) collective-permute-start(bf16[128,128]{1,0:T(8,128)(2,1)S(1)} %get-tuple-element.128), channel_id=1, source_target_pairs={{8,16},{16,8},{24,32},{32,24},{40,48},{48,40},{56,64},{64,56},{72,... | collective-permute-start | bytes 98312 | tf_op jit(solution)/shard_map/ppermute | solution.py:357
  56.9 3.1 %collective-permute-done.13.t1.refs_1_ = bf16[128,128]{1,0:T(8,128)(2,1)S(1)} collective-permute-done((bf16[128,128]{1,0:T(8,128)(2,1)S(1)}, bf16[128,128]{1,0:T(8,128)(2,1)S(1)}, u32[]{:S(2)}, u32[]{:S(2)}) %collective-permute-start.13) | collective-permute-done | bytes 32800 | tf_op jit(solution)/shard_map/ppermute | solution.py:357
  60.0 4.7 %all-to-all-done.x_ref = bf16[32,64,128]{2,1,0:T(8,128)(2,1)S(1)} async-done(((bf16[32,64,128]{2,1,0:T(8,128)(2,1)}), bf16[32,64,128]{2,1,0:T(8,128)(2,1)S(1)}, u32[]{:S(2)}, u32[]{:S(2)}) %all-to-all-start) | async-done | bytes 524320 | tf_op jit(solution)/shard_map/all_to_all | solution.py:374
  65.5 11.4 %all-to-all-start.1 = ((bf16[8,64,128]{2,1,0:T(8,128)(2,1)}), bf16[8,64,128]{2,1,0:T(8,128)(2,1)S(1)}, u32[]{:S(2)}, u32[]{:S(2)}) async-start(bf16[8,64,128]{2,1,0:T(8,128)(2,1)} %fold_dom.1), calls=%async_computation.1 | async-start | bytes 262144 | tf_op jit(solution)/shard_map/all_to_all | solution.py:374
  76.9 1.5 %collective-permute-start.14 = (bf16[128,128]{1,0:T(8,128)(2,1)S(1)}, bf16[128,128]{1,0:T(8,128)(2,1)S(1)}, u32[]{:S(2)}, u32[]{:S(2)}) collective-permute-start(bf16[128,128]{1,0:T(8,128)(2,1)S(1)} %get-tuple-element.129), channel_id=1, source_target_pairs={{0,1},{1,0},{2,3},{3,2},{4,5},{5,4},{6,7},{7,6},{8,9},{9,8},{10,11... | collective-permute-start | bytes 98312 | tf_op jit(solution)/shard_map/ppermute | solution.py:357
  78.4 4.1 %collective-permute-done.14.t2.refs_0_ = bf16[128,128]{1,0:T(8,128)(2,1)S(1)} collective-permute-done((bf16[128,128]{1,0:T(8,128)(2,1)S(1)}, bf16[128,128]{1,0:T(8,128)(2,1)S(1)}, u32[]{:S(2)}, u32[]{:S(2)}) %collective-permute-start.14) | collective-permute-done | bytes 32800 | tf_op jit(solution)/shard_map/ppermute | solution.py:357
  82.5 3.7 %all-to-all-done.1.x_ref = bf16[8,64,128]{2,1,0:T(8,128)(2,1)S(1)} async-done(((bf16[8,64,128]{2,1,0:T(8,128)(2,1)}), bf16[8,64,128]{2,1,0:T(8,128)(2,1)S(1)}, u32[]{:S(2)}, u32[]{:S(2)}) %all-to-all-start.1) | async-done | bytes 131104 | tf_op jit(solution)/shard_map/all_to_all | solution.py:374
  87.1 4.4 %all-to-all-start.2 = ((bf16[32,64,128]{2,1,0:T(8,128)(2,1)}), bf16[32,64,128]{2,1,0:T(8,128)(2,1)S(1)}, u32[]{:S(2)}, u32[]{:S(2)}) async-start(bf16[32,64,128]{2,1,0:T(8,128)(2,1)} %fold_group.1), calls=%async_computation.2 | async-start | bytes 1048576 | tf_op jit(solution)/shard_map/all_to_all | solution.py:374
  93.1 10.1 %all-to-all-done.2 = bf16[32,64,128]{2,1,0:T(8,128)(2,1)S(1)} async-done(((bf16[32,64,128]{2,1,0:T(8,128)(2,1)}), bf16[32,64,128]{2,1,0:T(8,128)(2,1)S(1)}, u32[]{:S(2)}, u32[]{:S(2)}) %all-to-all-start.2) | async-done | bytes 524320 | tf_op jit(solution)/shard_map/all_to_all | solution.py:374
  103.2 0.9 unpack.1
  (25 shorter events, 6.1 us)
Async XLA Ops:
  1.9 8.4 %collective-permute-start.1 = (bf16[128,128]{1,0:T(8,128)(2,1)S(1)}, bf16[128,128]{1,0:T(8,128)(2,1)S(1)}, u32[]{:S(2)}, u32[]{:S(2)}) collective-permute-start(bf16[128,128]{1,0:T(8,128)(2,1)S(1)} %get-tuple-element.79), channel_id=1, source_target_pairs={{8,16},{16,8},{24,32},{32,24},{40,48},{48,40},{56,64},{64,56},{72,... | collective-permute-start | bytes 98312 | tf_op jit(solution)/shard_map/ppermute | solution.py:357
  6.5 3.8 %collective-permute-start.2 = (bf16[128,128]{1,0:T(8,128)(2,1)S(1)}, bf16[128,128]{1,0:T(8,128)(2,1)S(1)}, u32[]{:S(2)}, u32[]{:S(2)}) collective-permute-start(bf16[128,128]{1,0:T(8,128)(2,1)S(1)} %get-tuple-element.80), channel_id=1, source_target_pairs={{0,1},{1,0},{2,3},{3,2},{4,5},{5,4},{6,7},{7,6},{8,9},{9,8},{10,11... | collective-permute-start | bytes 98312 | tf_op jit(solution)/shard_map/ppermute | solution.py:357
  8.2 2.1 %collective-permute-start.3 = (bf16[128,128]{1,0:T(8,128)(2,1)S(1)}, bf16[128,128]{1,0:T(8,128)(2,1)S(1)}, u32[]{:S(2)}, u32[]{:S(2)}) collective-permute-start(bf16[128,128]{1,0:T(8,128)(2,1)S(1)} %get-tuple-element.81), channel_id=1, source_target_pairs={{1,2},{2,1},{3,4},{4,3},{5,6},{6,5},{9,10},{10,9},{11,12},{12,11},... | collective-permute-start | bytes 98312 | tf_op jit(solution)/shard_map/ppermute | solution.py:357
  8.9 1.5 %collective-permute-start = (bf16[128,128]{1,0:T(8,128)(2,1)S(1)}, bf16[128,128]{1,0:T(8,128)(2,1)S(1)}, u32[]{:S(2)}, u32[]{:S(2)}) collective-permute-start(bf16[128,128]{1,0:T(8,128)(2,1)S(1)} %get-tuple-element.74.token), channel_id=1, source_target_pairs={{0,8},{8,0},{16,24},{24,16},{32,40},{40,32},{48,56},{56,48},{64,72... | collective-permute-start | bytes 98312 | tf_op jit(solution)/shard_map/ppermute | solution.py:357
  13.9 10.4 %collective-permute-start.4 = (bf16[128,128]{1,0:T(8,128)(2,1)S(1)}, bf16[128,128]{1,0:T(8,128)(2,1)S(1)}, u32[]{:S(2)}, u32[]{:S(2)}) collective-permute-start(bf16[128,128]{1,0:T(8,128)(2,1)S(1)} %get-tuple-element.90), channel_id=1, source_target_pairs={{0,8},{8,0},{16,24},{24,16},{32,40},{40,32},{48,56},{56,48},{64,72... | collective-permute-start | bytes 98312 | tf_op jit(solution)/shard_map/ppermute | solution.py:357
  14.4 9.8 %collective-permute-start.5 = (bf16[128,128]{1,0:T(8,128)(2,1)S(1)}, bf16[128,128]{1,0:T(8,128)(2,1)S(1)}, u32[]{:S(2)}, u32[]{:S(2)}) collective-permute-start(bf16[128,128]{1,0:T(8,128)(2,1)S(1)} %get-tuple-element.91), channel_id=1, source_target_pairs={{8,16},{16,8},{24,32},{32,24},{40,48},{48,40},{56,64},{64,56},{72,... | collective-permute-start | bytes 98312 | tf_op jit(solution)/shard_map/ppermute | solution.py:357
  17.5 6.7 %collective-permute-start.6 = (bf16[128,128]{1,0:T(8,128)(2,1)S(1)}, bf16[128,128]{1,0:T(8,128)(2,1)S(1)}, u32[]{:S(2)}, u32[]{:S(2)}) collective-permute-start(bf16[128,128]{1,0:T(8,128)(2,1)S(1)} %get-tuple-element.92), channel_id=1, source_target_pairs={{0,1},{1,0},{2,3},{3,2},{4,5},{5,4},{6,7},{7,6},{8,9},{9,8},{10,11... | collective-permute-start | bytes 98312 | tf_op jit(solution)/shard_map/ppermute | solution.py:357
  22.1 2.1 %collective-permute-start.7 = (bf16[128,128]{1,0:T(8,128)(2,1)S(1)}, bf16[128,128]{1,0:T(8,128)(2,1)S(1)}, u32[]{:S(2)}, u32[]{:S(2)}) collective-permute-start(bf16[128,128]{1,0:T(8,128)(2,1)S(1)} %get-tuple-element.93), channel_id=1, source_target_pairs={{1,2},{2,1},{3,4},{4,3},{5,6},{6,5},{9,10},{10,9},{11,12},{12,11},... | collective-permute-start | bytes 98312 | tf_op jit(solution)/shard_map/ppermute | solution.py:357
  29.9 10.2 %collective-permute-start.8 = (bf16[128,128]{1,0:T(8,128)(2,1)S(1)}, bf16[128,128]{1,0:T(8,128)(2,1)S(1)}, u32[]{:S(2)}, u32[]{:S(2)}) collective-permute-start(bf16[128,128]{1,0:T(8,128)(2,1)S(1)} %get-tuple-element.115), channel_id=1, source_target_pairs={{0,8},{8,0},{16,24},{24,16},{32,40},{40,32},{48,56},{56,48},{64,72... | collective-permute-start | bytes 98312 | tf_op jit(solution)/shard_map/ppermute | solution.py:357
  29.9 10.2 %collective-permute-start.9 = (bf16[128,128]{1,0:T(8,128)(2,1)S(1)}, bf16[128,128]{1,0:T(8,128)(2,1)S(1)}, u32[]{:S(2)}, u32[]{:S(2)}) collective-permute-start(bf16[128,128]{1,0:T(8,128)(2,1)S(1)} %get-tuple-element.116), channel_id=1, source_target_pairs={{8,16},{16,8},{24,32},{32,24},{40,48},{48,40},{56,64},{64,56},{72,... | collective-permute-start | bytes 98312 | tf_op jit(solution)/shard_map/ppermute | solution.py:357
  33.2 6.9 %collective-permute-start.10 = (bf16[128,128]{1,0:T(8,128)(2,1)S(1)}, bf16[128,128]{1,0:T(8,128)(2,1)S(1)}, u32[]{:S(2)}, u32[]{:S(2)}) collective-permute-start(bf16[128,128]{1,0:T(8,128)(2,1)S(1)} %get-tuple-element.117), channel_id=1, source_target_pairs={{0,1},{1,0},{2,3},{3,2},{4,5},{5,4},{6,7},{7,6},{8,9},{9,8},{10,11... | collective-permute-start | bytes 98312 | tf_op jit(solution)/shard_map/ppermute | solution.py:357
  38.5 1.6 %collective-permute-start.11 = (bf16[128,128]{1,0:T(8,128)(2,1)S(1)}, bf16[128,128]{1,0:T(8,128)(2,1)S(1)}, u32[]{:S(2)}, u32[]{:S(2)}) collective-permute-start(bf16[128,128]{1,0:T(8,128)(2,1)S(1)} %get-tuple-element.118), channel_id=1, source_target_pairs={{1,2},{2,1},{3,4},{4,3},{5,6},{6,5},{9,10},{10,9},{11,12},{12,11},... | collective-permute-start | bytes 98312 | tf_op jit(solution)/shard_map/ppermute | solution.py:357
  44.4 20.4 %all-to-all-start = ((bf16[32,64,128]{2,1,0:T(8,128)(2,1)}), bf16[32,64,128]{2,1,0:T(8,128)(2,1)S(1)}, u32[]{:S(2)}, u32[]{:S(2)}) async-start(bf16[32,64,128]{2,1,0:T(8,128)(2,1)} %bitcast.9), calls=%async_computation | async-start | bytes 1048576 | tf_op jit(solution)/shard_map/all_to_all | solution.py:374
  53.2 3.7 %collective-permute-start.12 = (bf16[128,128]{1,0:T(8,128)(2,1)S(1)}, bf16[128,128]{1,0:T(8,128)(2,1)S(1)}, u32[]{:S(2)}, u32[]{:S(2)}) collective-permute-start(bf16[128,128]{1,0:T(8,128)(2,1)S(1)} %get-tuple-element.127), channel_id=1, source_target_pairs={{0,8},{8,0},{16,24},{24,16},{32,40},{40,32},{48,56},{56,48},{64,72... | collective-permute-start | bytes 98312 | tf_op jit(solution)/shard_map/ppermute | solution.py:357
  53.5 6.5 %collective-permute-start.13 = (bf16[128,128]{1,0:T(8,128)(2,1)S(1)}, bf16[128,128]{1,0:T(8,128)(2,1)S(1)}, u32[]{:S(2)}, u32[]{:S(2)}) collective-permute-start(bf16[128,128]{1,0:T(8,128)(2,1)S(1)} %get-tuple-element.128), channel_id=1, source_target_pairs={{8,16},{16,8},{24,32},{32,24},{40,48},{48,40},{56,64},{64,56},{72,... | collective-permute-start | bytes 98312 | tf_op jit(solution)/shard_map/ppermute | solution.py:357
  65.5 20.7 %all-to-all-start.1 = ((bf16[8,64,128]{2,1,0:T(8,128)(2,1)}), bf16[8,64,128]{2,1,0:T(8,128)(2,1)S(1)}, u32[]{:S(2)}, u32[]{:S(2)}) async-start(bf16[8,64,128]{2,1,0:T(8,128)(2,1)} %fold_dom.1), calls=%async_computation.1 | async-start | bytes 262144 | tf_op jit(solution)/shard_map/all_to_all | solution.py:374
  76.9 5.6 %collective-permute-start.14 = (bf16[128,128]{1,0:T(8,128)(2,1)S(1)}, bf16[128,128]{1,0:T(8,128)(2,1)S(1)}, u32[]{:S(2)}, u32[]{:S(2)}) collective-permute-start(bf16[128,128]{1,0:T(8,128)(2,1)S(1)} %get-tuple-element.129), channel_id=1, source_target_pairs={{0,1},{1,0},{2,3},{3,2},{4,5},{5,4},{6,7},{7,6},{8,9},{9,8},{10,11... | collective-permute-start | bytes 98312 | tf_op jit(solution)/shard_map/ppermute | solution.py:357
  87.1 16.1 %all-to-all-start.2 = ((bf16[32,64,128]{2,1,0:T(8,128)(2,1)}), bf16[32,64,128]{2,1,0:T(8,128)(2,1)S(1)}, u32[]{:S(2)}, u32[]{:S(2)}) async-start(bf16[32,64,128]{2,1,0:T(8,128)(2,1)} %fold_group.1), calls=%async_computation.2 | async-start | bytes 1048576 | tf_op jit(solution)/shard_map/all_to_all | solution.py:374
  91.5 0.7 collective-permute-start.15

commit v7 on v6

--- a/solution.py
+++ b/solution.py
@@ -472,7 +472,7 @@
     (node_grad,) = call(finish_kernel, [shape(256, H, dtype=BF16)], [], (send, own, *back), "finish")
 
     scale = (lax.axis_size("dom") * lax.axis_size("group") * x0.shape[0]) ** (-0.5)
-    grads = reduce_grads(packed, scale, back[:2], back[2:3])
+    grads = reduce_grads(packed, scale, back[2:], ())
     return (nodes_out[None], node_grad[None], edge_grad[None], *grads)
 
 

time: 105 us -> 104 us (level)
  blocking collectives: 0 us -> 20.7 us
  waiting for transfers between devices: 25.9 us -> 13.2 us
  starting transfers between devices: 55.6 us -> 47.3 us
    all_to_all x0 -> x1, blocking collectives: none -> 20.7 us  [swap_tiles(): return lax.all_to_all(x, axis, split_axis=0, concat_axis=0, tiled=True)]
    all_to_all x3 -> x2, starting transfers between devices: 24.6 us -> 12.9 us  [swap_tiles(): return lax.all_to_all(x, axis, split_axis=0, concat_axis=0, tiled=True)]
    all_to_all x3 -> x2, waiting for transfers between devices: 18.6 us -> 8.97 us  [swap_tiles(): return lax.all_to_all(x, axis, split_axis=0, concat_axis=0, tiled=True)]
    ppermute x16, starting transfers between devices: 31.1 us -> 34.5 us  [exchange(): lax.ppermute(b, axis, swaps(axis, first))]
    ppermute x16, waiting for transfers between devices: 7.24 us -> 4.19 us  [exchange(): lax.ppermute(b, axis, swaps(axis, first))]
  transfers between devices with their start and end apart: 19 -> 18, of which waited for: 5 -> 4; matrix products, arithmetic and copies ran while one was open for 0% -> 0% of each run, Pallas kernels for 4% -> 4%
where the time goes in v7:
time: 104 us; the launch traced here: 103 us
  starting transfers between devices  47.3 us (45%)
  Pallas kernels  21.1 us (20%)
  blocking collectives  20.7 us (20%)
  waiting for transfers between devices  13.2 us (13%)
    ppermute x16, starting transfers between devices, exchange(): lax.ppermute(b, axis, swaps(axis, first))  34.5 us
    pallas_call x11, Pallas kernels, call(): pl.pallas_call(kernel, out_shape=outs, in_specs=[pl.BlockSpec(memory_spac...  21.1 us
    all_to_all x1, blocking collectives, swap_tiles(): return lax.all_to_all(x, axis, split_axis=0, concat_axis=0, tiled=True)  20.7 us
    all_to_all x2, starting transfers between devices, swap_tiles(): return lax.all_to_all(x, axis, split_axis=0, concat_axis=0, tiled=True)  12.9 us
    all_to_all x2, waiting for transfers between devices, swap_tiles(): return lax.all_to_all(x, axis, split_axis=0, concat_axis=0, tiled=True)  8.97 us
    ppermute x16, waiting for transfers between devices, exchange(): lax.ppermute(b, axis, swaps(axis, first))  4.19 us
  transfers between devices with their start and end apart: 18, of which 4 were waited for; matrix products, arithmetic and copies ran while one was open for 0% of the time, Pallas kernels for 4%

profile of v7, /device:TPU:1, one launch (start us, length us, event | category | flops | bytes accessed | tf_op | source)
XLA Modules:
  0.0 103.1 jit_solution(12904748206356397880)
XLA Ops:
  0.6 1.3 %sends.1 = (bf16[128,128]{1,0:T(8,128)(2,1)S(1)}, bf16[128,128]{1,0:T(8,128)(2,1)S(1)}, bf16[128,128]{1,0:T(8,128)(2,1)S(1)}, bf16[128,128]{1,0:T(8,128)(2,1)S(1...) custom-call(s32[4,128]{1,0:T(4,128)} %bitcast.18, bf16[256,128]{1,0:T(8,128)(2,1)} %bitcast.15), custom_call_target="tpu_custom_call" | custom-call | tf_op jit(solution)/shard_map/sends/pallas_call | solution.py:339
  1.9 4.6 %collective-permute-start.1 = (bf16[128,128]{1,0:T(8,128)(2,1)S(1)}, bf16[128,128]{1,0:T(8,128)(2,1)S(1)}, u32[]{:S(2)}, u32[]{:S(2)}) collective-permute-start(bf16[128,128]{1,0:T(8,128)(2,1)S(1)} %get-tuple-element.79), channel_id=1, source_target_pairs={{8,16},{16,8},{24,32},{32,24},{40,48},{48,40},{56,64},{64,56},{72,... | collective-permute-start | bytes 98312 | tf_op jit(solution)/shard_map/ppermute | solution.py:357
  6.5 1.7 %collective-permute-start.2 = (bf16[128,128]{1,0:T(8,128)(2,1)S(1)}, bf16[128,128]{1,0:T(8,128)(2,1)S(1)}, u32[]{:S(2)}, u32[]{:S(2)}) collective-permute-start(bf16[128,128]{1,0:T(8,128)(2,1)S(1)} %get-tuple-element.80), channel_id=1, source_target_pairs={{0,1},{1,0},{2,3},{3,2},{4,5},{5,4},{6,7},{7,6},{8,9},{9,8},{10,11... | collective-permute-start | bytes 98312 | tf_op jit(solution)/shard_map/ppermute | solution.py:357
  9.0 1.3 %load.1 = (s32[2,1,768]{2,1,0:T(1,128)S(1)}, s32[2,1,768]{2,1,0:T(1,128)S(1)}, bf16[1536,128]{1,0:T(8,128)(2,1)S(1)}, bf16[256,128]{1,0:T(8,128)(2,1)S(1)}, bf16...) custom-call(s32[1,4]{1,0:T(1,128)} %cnt_hbm.1, ...), custom_call_target="tpu_custom_call" | custom-call | tf_op jit(solution)/shard_map/load/pallas_call | solution.py:339
  10.4 3.5 %layer0.1 = (bf16[1536,384]{1,0:T(8,128)(2,1)S(1)}, bf16[1536,128]{1,0:T(8,128)(2,1)S(1)}, f32[1536,128]{1,0:T(8,128)S(1)}, f32[1536,128]{1,0:T(8,128)S(1)}, f32...) custom-call(s32[2,1,768]{2,1,0:T(1,128)S(1)} %get-tuple-element.75.s, ...), custom_call_target="tpu_custom_call" | custom-call | tf_op jit(solution)/shard_map/layer0/pallas_call | solution.py:339
  14.4 3.1 %collective-permute-start.5 = (bf16[128,128]{1,0:T(8,128)(2,1)S(1)}, bf16[128,128]{1,0:T(8,128)(2,1)S(1)}, u32[]{:S(2)}, u32[]{:S(2)}) collective-permute-start(bf16[128,128]{1,0:T(8,128)(2,1)S(1)} %get-tuple-element.91), channel_id=1, source_target_pairs={{8,16},{16,8},{24,32},{32,24},{40,48},{48,40},{56,64},{64,56},{72,... | collective-permute-start | bytes 98312 | tf_op jit(solution)/shard_map/ppermute | solution.py:357
  17.5 4.6 %collective-permute-start.6 = (bf16[128,128]{1,0:T(8,128)(2,1)S(1)}, bf16[128,128]{1,0:T(8,128)(2,1)S(1)}, u32[]{:S(2)}, u32[]{:S(2)}) collective-permute-start(bf16[128,128]{1,0:T(8,128)(2,1)S(1)} %get-tuple-element.92), channel_id=1, source_target_pairs={{0,1},{1,0},{2,3},{3,2},{4,5},{5,4},{6,7},{7,6},{8,9},{9,8},{10,11... | collective-permute-start | bytes 98312 | tf_op jit(solution)/shard_map/ppermute | solution.py:357
  22.8 1.4 %own1.1 = (bf16[1536,384]{1,0:T(8,128)(2,1)S(1)}, f32[1536,128]{1,0:T(8,128)S(1)}) custom-call(s32[2,1,768]{2,1,0:T(1,128)S(1)} %get-tuple-element.75.snd_ref, s32[2,1,768]{2,1,0:T(1,128)S(1)} %get-tuple-element.76.rcv_ref, bf16[256,128]{1,0:T(8,128)(2,1)S(1)} %get-tuple-element.89.x_ref, bf16[1536,128]{1,0:T(8,128)(2,1)S(1)} %get-tuple-element.94.e_ref, ...), custom_call_target="tpu_custom_call" | custom-call | tf_op jit(solution)/shard_map/own1/pallas_call | solution.py:339
  24.2 5.7 %layer1.1 = (bf16[256,128]{1,0:T(8,128)(2,1)}, bf16[1536,128]{1,0:T(8,128)(2,1)S(1)}, f32[256,128]{1,0:T(8,128)S(1)}, bf16[128,128]{1,0:T(8,128)(2,1)S(1)}, bf16...) custom-call(s32[2,1,768]{2,1,0:T(1,128)S(1)} %get-tuple-element.75.s, ...), custom_call_target="tpu_custom_call" | custom-call | tf_op jit(solution)/shard_map/layer1/pallas_call | solution.py:339
  29.9 3.3 %collective-permute-start.9 = (bf16[128,128]{1,0:T(8,128)(2,1)S(1)}, bf16[128,128]{1,0:T(8,128)(2,1)S(1)}, u32[]{:S(2)}, u32[]{:S(2)}) collective-permute-start(bf16[128,128]{1,0:T(8,128)(2,1)S(1)} %get-tuple-element.116), channel_id=1, source_target_pairs={{8,16},{16,8},{24,32},{32,24},{40,48},{48,40},{56,64},{64,56},{72,... | collective-permute-start | bytes 98312 | tf_op jit(solution)/shard_map/ppermute | solution.py:357
  33.2 5.3 %collective-permute-start.10 = (bf16[128,128]{1,0:T(8,128)(2,1)S(1)}, bf16[128,128]{1,0:T(8,128)(2,1)S(1)}, u32[]{:S(2)}, u32[]{:S(2)}) collective-permute-start(bf16[128,128]{1,0:T(8,128)(2,1)S(1)} %get-tuple-element.117), channel_id=1, source_target_pairs={{0,1},{1,0},{2,3},{3,2},{4,5},{5,4},{6,7},{7,6},{8,9},{9,8},{10,11... | collective-permute-start | bytes 98312 | tf_op jit(solution)/shard_map/ppermute | solution.py:357
  39.1 0.9 wgrad1.1
  40.1 4.3 %back0.1 = (bf16[1536,128]{1,0:T(8,128)(2,1)}, f32[256,128]{1,0:T(8,128)S(1)}, bf16[128,128]{1,0:T(8,128)(2,1)S(1)}, bf16[128,128]{1,0:T(8,128)(2,1)S(1)}, bf16[...) custom-call(s32[2,1,768]{2,1,0:T(1,128)S(1)} %get-tuple-element.75.snd_ref, ...), custom_call_target="tpu_custom_call" | custom-call | tf_op jit(solution)/shard_map/back0/pallas_call | solution.py:339
  44.4 8.8 %all-to-all-start = ((bf16[32,64,128]{2,1,0:T(8,128)(2,1)}), bf16[32,64,128]{2,1,0:T(8,128)(2,1)S(1)}, u32[]{:S(2)}, u32[]{:S(2)}) async-start(bf16[32,64,128]{2,1,0:T(8,128)(2,1)} %bitcast.9), calls=%async_computation | async-start | bytes 1048576 | tf_op jit(solution)/shard_map/all_to_all | solution.py:374
  53.2 4.9 %collective-permute-start.14 = (bf16[128,128]{1,0:T(8,128)(2,1)S(1)}, bf16[128,128]{1,0:T(8,128)(2,1)S(1)}, u32[]{:S(2)}, u32[]{:S(2)}) collective-permute-start(bf16[128,128]{1,0:T(8,128)(2,1)S(1)} %get-tuple-element.129), channel_id=1, source_target_pairs={{0,1},{1,0},{2,3},{3,2},{4,5},{5,4},{6,7},{7,6},{8,9},{9,8},{10,11... | collective-permute-start | bytes 98312 | tf_op jit(solution)/shard_map/ppermute | solution.py:357
  58.7 0.9 collective-permute-done.14.t2.refs_0_
  59.7 5.1 %all-to-all-done.x_ref = bf16[32,64,128]{2,1,0:T(8,128)(2,1)S(1)} async-done(((bf16[32,64,128]{2,1,0:T(8,128)(2,1)}), bf16[32,64,128]{2,1,0:T(8,128)(2,1)S(1)}, u32[]{:S(2)}, u32[]{:S(2)}) %all-to-all-start) | async-done | bytes 524320 | tf_op jit(solution)/shard_map/all_to_all | solution.py:374
  64.9 20.7 %all_to_all.15.x_ref = bf16[8,64,128]{2,1,0:T(8,128)(2,1)S(1)} all-to-all(bf16[8,64,128]{2,1,0:T(8,128)(2,1)S(1)} %fold_dom.1), channel_id=1, replica_groups=mesh['dom'=32,'group'=8] {'group'}, dimensions={0} | all-to-all | bytes 262144 | tf_op jit(solution)/shard_map/all_to_all | solution.py:374
  85.5 0.9 fold_group.1
  86.4 4.1 %all-to-all-start.2 = ((bf16[32,64,128]{2,1,0:T(8,128)(2,1)}), bf16[32,64,128]{2,1,0:T(8,128)(2,1)S(1)}, u32[]{:S(2)}, u32[]{:S(2)}) async-start(bf16[32,64,128]{2,1,0:T(8,128)(2,1)} %fold_group.1), calls=%async_computation.2 | async-start | bytes 1048576 | tf_op jit(solution)/shard_map/all_to_all | solution.py:374
  90.9 3.3 %collective-permute-start.13 = (bf16[128,128]{1,0:T(8,128)(2,1)S(1)}, bf16[128,128]{1,0:T(8,128)(2,1)S(1)}, u32[]{:S(2)}, u32[]{:S(2)}) collective-permute-start(bf16[128,128]{1,0:T(8,128)(2,1)S(1)} %get-tuple-element.128), channel_id=1, source_target_pairs={{8,16},{16,8},{24,32},{32,24},{40,48},{48,40},{56,64},{64,56},{72,... | collective-permute-start | bytes 98312 | tf_op jit(solution)/shard_map/ppermute | solution.py:357
  94.3 3.2 %collective-permute-done.13.t1 = bf16[128,128]{1,0:T(8,128)(2,1)S(1)} collective-permute-done((bf16[128,128]{1,0:T(8,128)(2,1)S(1)}, bf16[128,128]{1,0:T(8,128)(2,1)S(1)}, u32[]{:S(2)}, u32[]{:S(2)}) %collective-permute-start.13) | collective-permute-done | bytes 32800 | tf_op jit(solution)/shard_map/ppermute | solution.py:357
  98.3 3.9 %all-to-all-done.2 = bf16[32,64,128]{2,1,0:T(8,128)(2,1)S(1)} async-done(((bf16[32,64,128]{2,1,0:T(8,128)(2,1)}), bf16[32,64,128]{2,1,0:T(8,128)(2,1)S(1)}, u32[]{:S(2)}, u32[]{:S(2)}) %all-to-all-start.2) | async-done | bytes 524320 | tf_op jit(solution)/shard_map/all_to_all | solution.py:374
  102.2 0.9 unpack.1
  (24 shorter events, 4.7 us)
Async XLA Ops:
  1.9 8.4 %collective-permute-start.1 = (bf16[128,128]{1,0:T(8,128)(2,1)S(1)}, bf16[128,128]{1,0:T(8,128)(2,1)S(1)}, u32[]{:S(2)}, u32[]{:S(2)}) collective-permute-start(bf16[128,128]{1,0:T(8,128)(2,1)S(1)} %get-tuple-element.79), channel_id=1, source_target_pairs={{8,16},{16,8},{24,32},{32,24},{40,48},{48,40},{56,64},{64,56},{72,... | collective-permute-start | bytes 98312 | tf_op jit(solution)/shard_map/ppermute | solution.py:357
  6.5 3.8 %collective-permute-start.2 = (bf16[128,128]{1,0:T(8,128)(2,1)S(1)}, bf16[128,128]{1,0:T(8,128)(2,1)S(1)}, u32[]{:S(2)}, u32[]{:S(2)}) collective-permute-start(bf16[128,128]{1,0:T(8,128)(2,1)S(1)} %get-tuple-element.80), channel_id=1, source_target_pairs={{0,1},{1,0},{2,3},{3,2},{4,5},{5,4},{6,7},{7,6},{8,9},{9,8},{10,11... | collective-permute-start | bytes 98312 | tf_op jit(solution)/shard_map/ppermute | solution.py:357
  8.2 2.1 %collective-permute-start.3 = (bf16[128,128]{1,0:T(8,128)(2,1)S(1)}, bf16[128,128]{1,0:T(8,128)(2,1)S(1)}, u32[]{:S(2)}, u32[]{:S(2)}) collective-permute-start(bf16[128,128]{1,0:T(8,128)(2,1)S(1)} %get-tuple-element.81), channel_id=1, source_target_pairs={{1,2},{2,1},{3,4},{4,3},{5,6},{6,5},{9,10},{10,9},{11,12},{12,11},... | collective-permute-start | bytes 98312 | tf_op jit(solution)/shard_map/ppermute | solution.py:357
  8.9 1.5 %collective-permute-start = (bf16[128,128]{1,0:T(8,128)(2,1)S(1)}, bf16[128,128]{1,0:T(8,128)(2,1)S(1)}, u32[]{:S(2)}, u32[]{:S(2)}) collective-permute-start(bf16[128,128]{1,0:T(8,128)(2,1)S(1)} %get-tuple-element.74.token), channel_id=1, source_target_pairs={{0,8},{8,0},{16,24},{24,16},{32,40},{40,32},{48,56},{56,48},{64,72... | collective-permute-start | bytes 98312 | tf_op jit(solution)/shard_map/ppermute | solution.py:357
  13.9 10.4 %collective-permute-start.4 = (bf16[128,128]{1,0:T(8,128)(2,1)S(1)}, bf16[128,128]{1,0:T(8,128)(2,1)S(1)}, u32[]{:S(2)}, u32[]{:S(2)}) collective-permute-start(bf16[128,128]{1,0:T(8,128)(2,1)S(1)} %get-tuple-element.90), channel_id=1, source_target_pairs={{0,8},{8,0},{16,24},{24,16},{32,40},{40,32},{48,56},{56,48},{64,72... | collective-permute-start | bytes 98312 | tf_op jit(solution)/shard_map/ppermute | solution.py:357
  14.4 9.8 %collective-permute-start.5 = (bf16[128,128]{1,0:T(8,128)(2,1)S(1)}, bf16[128,128]{1,0:T(8,128)(2,1)S(1)}, u32[]{:S(2)}, u32[]{:S(2)}) collective-permute-start(bf16[128,128]{1,0:T(8,128)(2,1)S(1)} %get-tuple-element.91), channel_id=1, source_target_pairs={{8,16},{16,8},{24,32},{32,24},{40,48},{48,40},{56,64},{64,56},{72,... | collective-permute-start | bytes 98312 | tf_op jit(solution)/shard_map/ppermute | solution.py:357
  17.5 6.7 %collective-permute-start.6 = (bf16[128,128]{1,0:T(8,128)(2,1)S(1)}, bf16[128,128]{1,0:T(8,128)(2,1)S(1)}, u32[]{:S(2)}, u32[]{:S(2)}) collective-permute-start(bf16[128,128]{1,0:T(8,128)(2,1)S(1)} %get-tuple-element.92), channel_id=1, source_target_pairs={{0,1},{1,0},{2,3},{3,2},{4,5},{5,4},{6,7},{7,6},{8,9},{9,8},{10,11... | collective-permute-start | bytes 98312 | tf_op jit(solution)/shard_map/ppermute | solution.py:357
  22.1 2.1 %collective-permute-start.7 = (bf16[128,128]{1,0:T(8,128)(2,1)S(1)}, bf16[128,128]{1,0:T(8,128)(2,1)S(1)}, u32[]{:S(2)}, u32[]{:S(2)}) collective-permute-start(bf16[128,128]{1,0:T(8,128)(2,1)S(1)} %get-tuple-element.93), channel_id=1, source_target_pairs={{1,2},{2,1},{3,4},{4,3},{5,6},{6,5},{9,10},{10,9},{11,12},{12,11},... | collective-permute-start | bytes 98312 | tf_op jit(solution)/shard_map/ppermute | solution.py:357
  29.9 10.2 %collective-permute-start.8 = (bf16[128,128]{1,0:T(8,128)(2,1)S(1)}, bf16[128,128]{1,0:T(8,128)(2,1)S(1)}, u32[]{:S(2)}, u32[]{:S(2)}) collective-permute-start(bf16[128,128]{1,0:T(8,128)(2,1)S(1)} %get-tuple-element.115), channel_id=1, source_target_pairs={{0,8},{8,0},{16,24},{24,16},{32,40},{40,32},{48,56},{56,48},{64,72... | collective-permute-start | bytes 98312 | tf_op jit(solution)/shard_map/ppermute | solution.py:357
  29.9 10.2 %collective-permute-start.9 = (bf16[128,128]{1,0:T(8,128)(2,1)S(1)}, bf16[128,128]{1,0:T(8,128)(2,1)S(1)}, u32[]{:S(2)}, u32[]{:S(2)}) collective-permute-start(bf16[128,128]{1,0:T(8,128)(2,1)S(1)} %get-tuple-element.116), channel_id=1, source_target_pairs={{8,16},{16,8},{24,32},{32,24},{40,48},{48,40},{56,64},{64,56},{72,... | collective-permute-start | bytes 98312 | tf_op jit(solution)/shard_map/ppermute | solution.py:357
  33.2 6.9 %collective-permute-start.10 = (bf16[128,128]{1,0:T(8,128)(2,1)S(1)}, bf16[128,128]{1,0:T(8,128)(2,1)S(1)}, u32[]{:S(2)}, u32[]{:S(2)}) collective-permute-start(bf16[128,128]{1,0:T(8,128)(2,1)S(1)} %get-tuple-element.117), channel_id=1, source_target_pairs={{0,1},{1,0},{2,3},{3,2},{4,5},{5,4},{6,7},{7,6},{8,9},{9,8},{10,11... | collective-permute-start | bytes 98312 | tf_op jit(solution)/shard_map/ppermute | solution.py:357
  38.5 1.6 %collective-permute-start.11 = (bf16[128,128]{1,0:T(8,128)(2,1)S(1)}, bf16[128,128]{1,0:T(8,128)(2,1)S(1)}, u32[]{:S(2)}, u32[]{:S(2)}) collective-permute-start(bf16[128,128]{1,0:T(8,128)(2,1)S(1)} %get-tuple-element.118), channel_id=1, source_target_pairs={{1,2},{2,1},{3,4},{4,3},{5,6},{6,5},{9,10},{10,9},{11,12},{12,11},... | collective-permute-start | bytes 98312 | tf_op jit(solution)/shard_map/ppermute | solution.py:357
  44.4 20.4 %all-to-all-start = ((bf16[32,64,128]{2,1,0:T(8,128)(2,1)}), bf16[32,64,128]{2,1,0:T(8,128)(2,1)S(1)}, u32[]{:S(2)}, u32[]{:S(2)}) async-start(bf16[32,64,128]{2,1,0:T(8,128)(2,1)} %bitcast.9), calls=%async_computation | async-start | bytes 1048576 | tf_op jit(solution)/shard_map/all_to_all | solution.py:374
  53.2 6.5 %collective-permute-start.14 = (bf16[128,128]{1,0:T(8,128)(2,1)S(1)}, bf16[128,128]{1,0:T(8,128)(2,1)S(1)}, u32[]{:S(2)}, u32[]{:S(2)}) collective-permute-start(bf16[128,128]{1,0:T(8,128)(2,1)S(1)} %get-tuple-element.129), channel_id=1, source_target_pairs={{0,1},{1,0},{2,3},{3,2},{4,5},{5,4},{6,7},{7,6},{8,9},{9,8},{10,11... | collective-permute-start | bytes 98312 | tf_op jit(solution)/shard_map/ppermute | solution.py:357
  58.1 1.6 %collective-permute-start.15 = (bf16[128,128]{1,0:T(8,128)(2,1)S(1)}, bf16[128,128]{1,0:T(8,128)(2,1)S(1)}, u32[]{:S(2)}, u32[]{:S(2)}) collective-permute-start(bf16[128,128]{1,0:T(8,128)(2,1)S(1)} %get-tuple-element.130), channel_id=1, source_target_pairs={{1,2},{2,1},{3,4},{4,3},{5,6},{6,5},{9,10},{10,9},{11,12},{12,11},... | collective-permute-start | bytes 98312 | tf_op jit(solution)/shard_map/ppermute | solution.py:357
  86.4 15.8 %all-to-all-start.2 = ((bf16[32,64,128]{2,1,0:T(8,128)(2,1)}), bf16[32,64,128]{2,1,0:T(8,128)(2,1)S(1)}, u32[]{:S(2)}, u32[]{:S(2)}) async-start(bf16[32,64,128]{2,1,0:T(8,128)(2,1)} %fold_group.1), calls=%async_computation.2 | async-start | bytes 1048576 | tf_op jit(solution)/shard_map/all_to_all | solution.py:374
  90.5 3.8 %collective-permute-start.12 = (bf16[128,128]{1,0:T(8,128)(2,1)S(1)}, bf16[128,128]{1,0:T(8,128)(2,1)S(1)}, u32[]{:S(2)}, u32[]{:S(2)}) collective-permute-start(bf16[128,128]{1,0:T(8,128)(2,1)S(1)} %get-tuple-element.127), channel_id=1, source_target_pairs={{0,8},{8,0},{16,24},{24,16},{32,40},{40,32},{48,56},{56,48},{64,72... | collective-permute-start | bytes 98312 | tf_op jit(solution)/shard_map/ppermute | solution.py:357
  90.9 6.5 %collective-permute-start.13 = (bf16[128,128]{1,0:T(8,128)(2,1)S(1)}, bf16[128,128]{1,0:T(8,128)(2,1)S(1)}, u32[]{:S(2)}, u32[]{:S(2)}) collective-permute-start(bf16[128,128]{1,0:T(8,128)(2,1)S(1)} %get-tuple-element.128), channel_id=1, source_target_pairs={{8,16},{16,8},{24,32},{32,24},{40,48},{48,40},{56,64},{64,56},{72,... | collective-permute-start | bytes 98312 | tf_op jit(solution)/shard_map/ppermute | solution.py:357
